TPU v7x, 64 devices: a 2x2x8 block of a 4x4x8 slice. The times are simulated.
64 devices in a mesh: dp: 4 (over x, y), tp: 16 (over z, core).
Axes of the slice: x: 2, y: 2, z: 8, core: 2. Of those that a mesh axis runs over, the one named last changes fastest.
The devices are a block of a 4x4x8 slice.
Arguments:
- x_in: bfloat16 [32, 256, 1408], P('dp', 'tp'), parts along dimension 0
- y_text: bfloat16 [32, 256, 1408], P('dp', 'tp'), parts along dimension 0
- t_emb: bfloat16 [32, 8448], P('dp'), parts along dimension 0
- text_len: int32 [32], P('dp'), parts along dimension 0
- mod_table: bfloat16 [6, 1408], replicated
- w_qkv: bfloat16 [1408, 16, 264], P(None, 'tp')
- b_qkv: bfloat16 [16, 264], P('tp')
- w_o: bfloat16 [16, 88, 1408], P('tp')
- b_o: bfloat16 [1408], replicated
- w_q: bfloat16 [1408, 16, 88], P(None, 'tp')
- b_q: bfloat16 [16, 88], P('tp')
- w_kv: bfloat16 [1408, 16, 176], P(None, 'tp')
- b_kv: bfloat16 [16, 176], P('tp')
- w_co: bfloat16 [16, 88, 1408], P('tp')
- b_co: bfloat16 [1408], replicated
- w_1: bfloat16 [1408, 6144], P(None, 'tp')
- b_1: bfloat16 [6144], P('tp')
- w_2: bfloat16 [6144, 1408], P('tp')
- b_2: bfloat16 [1408], replicated
- g_out: bfloat16 [32, 256, 1408], P('dp', 'tp'), parts along dimension 0
Outputs:
- output 1: bfloat16 [32, 256, 1408], P('dp', 'tp'), parts along dimension 0
- output 2: bfloat16 [32, 256, 1408], P('dp', 'tp'), parts along dimension 0
- output 3: bfloat16 [32, 256, 1408], P('dp', 'tp'), parts along dimension 0
- output 4: float32 [24, 1408], P('dp'), parts along dimension 0
- output 5: bfloat16 [5632, 16, 264], P('dp', 'tp'), parts along dimension 0
- output 6: bfloat16 [64, 264], P(('dp', 'tp')), parts along dimension 0
- output 7: bfloat16 [64, 88, 1408], P(('dp', 'tp')), parts along dimension 0
- output 8: bfloat16 [5632], P('dp'), parts along dimension 0
- output 9: bfloat16 [5632, 16, 88], P('dp', 'tp'), parts along dimension 0
- output 10: bfloat16 [64, 88], P(('dp', 'tp')), parts along dimension 0
- output 11: bfloat16 [5632, 16, 176], P('dp', 'tp'), parts along dimension 0
- output 12: bfloat16 [64, 176], P(('dp', 'tp')), parts along dimension 0
- output 13: bfloat16 [64, 88, 1408], P(('dp', 'tp')), parts along dimension 0
- output 14: bfloat16 [5632], P('dp'), parts along dimension 0
- output 15: bfloat16 [5632, 6144], P('dp', 'tp'), parts along dimension 0
- output 16: bfloat16 [24576], P(('dp', 'tp')), parts along dimension 0
- output 17: bfloat16 [24576, 1408], P(('dp', 'tp')), parts along dimension 0
- output 18: bfloat16 [5632], P('dp'), parts along dimension 0
There are 4 independent parts. A program takes and returns all parts, laid end to end along the dimension named above; an argument that names none is the same for every part.
All inputs are finite; a program needn't handle non-finite values.
Results may differ from a plain program's by a relative error of at most 0.02.
Values are sent between devices in bfloat16 or wider.
A program may use at most 768 MiB of HBM per device.

v0:
```python
import jax
import jax.numpy as jnp
from jax import lax
from jax.sharding import PartitionSpec as P

LN_EPS = 1e-6
MASK_FILL = -1e30


def product(form, lhs, rhs):
    return jnp.einsum(form, lhs, rhs, preferred_element_type=jnp.float32)


def layer_norm(tensor):
    tensor = tensor.astype(jnp.float32)
    centered = tensor - jnp.mean(tensor, axis=-1, keepdims=True)
    inv_std = lax.rsqrt(jnp.mean(centered * centered, axis=-1, keepdims=True) + LN_EPS)
    return centered * inv_std, inv_std


def layer_norm_back(normed, inv_std, g_normed):
    mean_g = jnp.mean(g_normed, axis=-1, keepdims=True)
    mean_gn = jnp.mean(g_normed * normed, axis=-1, keepdims=True)
    return inv_std * (g_normed - mean_g - normed * mean_gn)


def gelu_tanh(tensor):
    return jax.nn.gelu(tensor, approximate=True)


def attend(q_all, k_all, v_all, key_ok):
    head_dim = q_all.shape[-1]
    scores = product('bqhd,bkhd->bhqk', q_all, k_all) * head_dim ** -0.5
    if key_ok is not None:
        scores = jnp.where(key_ok[:, None, None, :], scores, MASK_FILL)
    prob_bf = jax.nn.softmax(scores, axis=-1).astype(jnp.bfloat16)
    return product('bhqk,bkhd->bqhd', prob_bf, v_all).astype(jnp.bfloat16), prob_bf


def attend_back(q_all, k_all, v_all, prob_bf, g_val):
    head_dim = q_all.shape[-1]
    g_v = product('bhqk,bqhd->bkhd', prob_bf, g_val)
    g_prob = product('bqhd,bkhd->bhqk', g_val, v_all)
    row_dot = jnp.sum(g_prob * prob_bf, axis=-1, keepdims=True)
    g_scores = (prob_bf * (g_prob - row_dot) * head_dim ** -0.5).astype(jnp.bfloat16)
    g_q = product('bhqk,bkhd->bqhd', g_scores, k_all)
    g_k = product('bhqk,bqhd->bkhd', g_scores, q_all)
    return g_q.astype(jnp.bfloat16), g_k.astype(jnp.bfloat16), g_v.astype(jnp.bfloat16)


def gather_tokens(tensor):
    return lax.all_gather(tensor, 'tp', axis=1, tiled=True)


def reduce_tokens(tensor):
    return lax.psum_scatter(tensor.astype(jnp.bfloat16), 'tp', scatter_dimension=1, tiled=True)


def token_sum(tensor):
    return jnp.sum(tensor.astype(jnp.float32), axis=(0, 1))


def device_block(x_loc, y_loc, t_loc, len_loc, mod_table, w_qkv, b_qkv, w_o, b_o, w_q, b_q, w_kv, b_kv, w_co, b_co, w_1, b_1, w_2, b_2, g_loc):
    batch, n_loc, width = x_loc.shape
    head_dim = w_q.shape[2]
    mod_rows = mod_table.astype(jnp.float32)[None] + t_loc.astype(jnp.float32).reshape(batch, 6, width)
    shift1, scale1, gate1, shift2, scale2, gate2 = [mod_rows[:, row_idx, None, :] for row_idx in range(6)]

    normed1, inv_std1 = layer_norm(x_loc)
    h1_all = gather_tokens((normed1 * (1.0 + scale1) + shift1).astype(jnp.bfloat16))
    qkv_all = (product('bnd,dhe->bnhe', h1_all, w_qkv) + b_qkv).astype(jnp.bfloat16)
    q_self = qkv_all[..., :head_dim]
    k_self = qkv_all[..., head_dim:2 * head_dim]
    v_self = qkv_all[..., 2 * head_dim:]
    attn_val, attn_prob = attend(q_self, k_self, v_self, None)
    attn_total = reduce_tokens(product('bnhe,hed->bnd', attn_val, w_o)).astype(jnp.float32) + b_o
    x1_loc = (x_loc + gate1 * attn_total).astype(jnp.bfloat16)

    x1_all = gather_tokens(x1_loc)
    y_all = gather_tokens(y_loc)
    q_cross = (product('bnd,dhe->bnhe', x1_all, w_q) + b_q).astype(jnp.bfloat16)
    kv_cross = (product('bsd,dhe->bshe', y_all, w_kv) + b_kv).astype(jnp.bfloat16)
    k_cross = kv_cross[..., :head_dim]
    v_cross = kv_cross[..., head_dim:]
    slot_ok = lax.broadcasted_iota(jnp.int32, (batch, y_all.shape[1]), 1) < len_loc[:, None]
    cross_val, cross_prob = attend(q_cross, k_cross, v_cross, slot_ok)
    cross_total = reduce_tokens(product('bnhe,hed->bnd', cross_val, w_co)).astype(jnp.float32) + b_co
    x2_loc = (x1_loc + cross_total).astype(jnp.bfloat16)

    normed2, inv_std2 = layer_norm(x2_loc)
    h2_all = gather_tokens((normed2 * (1.0 + scale2) + shift2).astype(jnp.bfloat16))
    hidden = product('bnd,df->bnf', h2_all, w_1) + b_1
    gelu_out, gelu_vjp = jax.vjp(gelu_tanh, hidden)
    gelu_out = gelu_out.astype(jnp.bfloat16)
    mlp_total = reduce_tokens(product('bnf,fd->bnd', gelu_out, w_2)).astype(jnp.float32) + b_2
    x_out = (x2_loc + gate2 * mlp_total).astype(jnp.bfloat16)

    g_x2 = g_loc.astype(jnp.float32)
    g_gate2 = jnp.sum(g_x2 * mlp_total, axis=(0, 1))
    g_mlp_all = gather_tokens((g_x2 * gate2).astype(jnp.bfloat16))
    g_b_2 = token_sum(g_mlp_all)
    g_w_2 = product('bnf,bnd->fd', gelu_out, g_mlp_all)
    g_hidden = gelu_vjp(product('bnd,fd->bnf', g_mlp_all, w_2))[0]
    g_b_1 = token_sum(g_hidden)
    g_hidden = g_hidden.astype(jnp.bfloat16)
    g_w_1 = product('bnd,bnf->df', h2_all, g_hidden)
    g_h2 = reduce_tokens(product('bnf,df->bnd', g_hidden, w_1)).astype(jnp.float32)
    g_shift2 = token_sum(g_h2)
    g_scale2 = token_sum(g_h2 * normed2)
    g_x2 = g_x2 + layer_norm_back(normed2, inv_std2, g_h2 * (1.0 + scale2))

    g_cross_all = gather_tokens(g_x2.astype(jnp.bfloat16))
    g_b_co = token_sum(g_cross_all)
    g_w_co = product('bnhe,bnd->hed', cross_val, g_cross_all)
    g_cross_val = product('bnd,hed->bnhe', g_cross_all, w_co).astype(jnp.bfloat16)
    g_q_cross, g_k_cross, g_v_cross = attend_back(q_cross, k_cross, v_cross, cross_prob, g_cross_val)
    g_kv_cross = jnp.concatenate([g_k_cross, g_v_cross], axis=-1)
    g_b_kv = token_sum(g_kv_cross)
    g_w_kv = product('bsd,bshe->dhe', y_all, g_kv_cross)
    g_y = reduce_tokens(product('bshe,dhe->bsd', g_kv_cross, w_kv))
    g_b_q = token_sum(g_q_cross)
    g_w_q = product('bnd,bnhe->dhe', x1_all, g_q_cross)
    g_x1 = g_x2 + reduce_tokens(product('bnhe,dhe->bnd', g_q_cross, w_q)).astype(jnp.float32)

    g_gate1 = jnp.sum(g_x1 * attn_total, axis=(0, 1))
    g_attn_all = gather_tokens((g_x1 * gate1).astype(jnp.bfloat16))
    g_b_o = token_sum(g_attn_all)
    g_w_o = product('bnhe,bnd->hed', attn_val, g_attn_all)
    g_attn_val = product('bnd,hed->bnhe', g_attn_all, w_o).astype(jnp.bfloat16)
    g_q_self, g_k_self, g_v_self = attend_back(q_self, k_self, v_self, attn_prob, g_attn_val)
    g_qkv = jnp.concatenate([g_q_self, g_k_self, g_v_self], axis=-1)
    g_b_qkv = token_sum(g_qkv)
    g_w_qkv = product('bnd,bnhe->dhe', h1_all, g_qkv)
    g_h1 = reduce_tokens(product('bnhe,dhe->bnd', g_qkv, w_qkv)).astype(jnp.float32)
    g_x = g_x1 + layer_norm_back(normed1, inv_std1, g_h1 * (1.0 + scale1))
    g_table = lax.psum(jnp.stack([token_sum(g_h1), token_sum(g_h1 * normed1), g_gate1, g_shift2, g_scale2, g_gate2]), 'tp')

    bf16 = jnp.bfloat16
    return (x_out, g_x.astype(bf16), g_y, g_table, g_w_qkv.astype(bf16), g_b_qkv.astype(bf16), g_w_o.astype(bf16), g_b_o.astype(bf16), g_w_q.astype(bf16), g_b_q.astype(bf16), g_w_kv.astype(bf16), g_b_kv.astype(bf16), g_w_co.astype(bf16), g_b_co.astype(bf16), g_w_1.astype(bf16), g_b_1.astype(bf16), g_w_2.astype(bf16), g_b_2.astype(bf16))


def solution(mesh):
    token_spec = P('dp', 'tp', None)
    group_rows = ('dp', 'tp')
    in_specs = (token_spec, token_spec, P('dp', None), P('dp'), P(None, None), P(None, 'tp', None), P('tp', None), P('tp', None, None), P(None), P(None, 'tp', None), P('tp', None), P(None, 'tp', None), P('tp', None), P('tp', None, None), P(None), P(None, 'tp'), P('tp'), P('tp', None), P(None), token_spec)
    out_specs = (token_spec, token_spec, token_spec, P('dp', None), P('dp', 'tp', None), P(group_rows, None), P(group_rows, None, None), P('dp'), P('dp', 'tp', None), P(group_rows, None), P('dp', 'tp', None), P(group_rows, None), P(group_rows, None, None), P('dp'), P('dp', 'tp'), P(group_rows), P(group_rows, None), P('dp'))
    return jax.shard_map(device_block, mesh=mesh, in_specs=in_specs, out_specs=out_specs, check_vma=False)
```

profile of v0, /device:TPU:21, one launch (start us, length us, event | category | flops | bytes accessed | tf_op | source)
XLA Modules:
  0.0 825.5 jit_solution(16967565254209204473)
XLA Ops:
  7.3 1.2 convert_reduce_fusion.3
  8.6 1.2 fusion.92
  12.1 2.0 fusion.87
  14.3 46.3 %all-gather.8.cloned.1.call-done = bf16[8,256,1408]{2,1,0:T(8,128)(2,1)} async-done(((bf16[8,16,1408]{2,1,0:T(8,128)(2,1)}), bf16[8,256,1408]{2,1,0:T(8,128)(2,1)}) %all-gather.8.cloned.1.call-update) | async-done | bytes 5767184 | tf_op jit(solution)/shard_map/all_gather | solution.py:52
  60.7 4.5 fusion.34
  65.2 2.1 fusion.135
  67.4 1.8 divide_convert_fusion.1
  69.2 1.3 fusion.44
  71.2 4.1 convolution_convert_fusion.6
  76.3 56.9 %reduce-scatter.8.cloned.1.call-done = bf16[8,16,1408]{2,1,0:T(8,128)(2,1)} async-done(((bf16[8,256,1408]{2,1,0:T(8,128)(2,1)}), bf16[8,16,1408]{2,1,0:T(8,128)(2,1)}) %reduce-scatter.8.cloned.1.call-update) | async-done | bytes 360464 | tf_op jit(solution)/shard_map/reduce_scatter | solution.py:56
  133.3 1.9 fusion.95
  135.4 42.9 %all-gather.10.cloned.1.call-done = bf16[8,256,1408]{2,1,0:T(8,128)(2,1)} async-done(((bf16[8,16,1408]{2,1,0:T(8,128)(2,1)}), bf16[8,256,1408]{2,1,0:T(8,128)(2,1)}) %all-gather.10.cloned.1.call-update) | async-done | bytes 5767184 | tf_op jit(solution)/shard_map/all_gather | solution.py:52
  178.3 5.7 fusion.35
  184.0 36.0 %all-gather.12.cloned.1.call-done = bf16[8,256,1408]{2,1,0:T(8,128)(2,1)} async-done(((bf16[8,16,1408]{2,1,0:T(8,128)(2,1)}), bf16[8,256,1408]{2,1,0:T(8,128)(2,1)}) %all-gather.12.cloned.1.call-update) | async-done | bytes 5767184 | tf_op jit(solution)/shard_map/all_gather | solution.py:52
  220.0 4.6 fusion.36
  224.6 3.3 fusion.136
  228.0 1.8 divide_convert_fusion
  229.8 1.0 copy-done.3
  231.1 4.1 convolution_convert_fusion.5
  236.0 57.2 %reduce-scatter.10.cloned.1.call-done = bf16[8,16,1408]{2,1,0:T(8,128)(2,1)} async-done(((bf16[8,256,1408]{2,1,0:T(8,128)(2,1)}), bf16[8,16,1408]{2,1,0:T(8,128)(2,1)}) %reduce-scatter.10.cloned.1.call-update) | async-done | bytes 360464 | tf_op jit(solution)/shard_map/reduce_scatter | solution.py:56
  293.2 1.3 convert_reduce_fusion.2
  294.7 1.1 fusion.82
  297.2 42.2 %all-gather.14.cloned.1.call-done = bf16[8,256,1408]{2,1,0:T(8,128)(2,1)} async-done(((bf16[8,16,1408]{2,1,0:T(8,128)(2,1)}), bf16[8,256,1408]{2,1,0:T(8,128)(2,1)}) %all-gather.14.cloned.1.call-update) | async-done | bytes 5767184 | tf_op jit(solution)/shard_map/all_gather | solution.py:52
  339.4 8.0 fusion.53
  347.4 33.8 %all-gather.16.cloned.1.call-done = bf16[8,256,1408]{2,1,0:T(8,128)(2,1)} async-done(((bf16[8,16,1408]{2,1,0:T(8,128)(2,1)}), bf16[8,256,1408]{2,1,0:T(8,128)(2,1)}) %all-gather.16.cloned.1.call-update) | async-done | bytes 5767184 | tf_op jit(solution)/shard_map/all_gather | solution.py:52
  381.2 9.6 %fusion.138 = (bf16[384]{0:T(512)(128)(2,1)}, bf16[8,256,384]{2,1,0:T(8,128)(2,1)S(1)}) fusion(f32[8,256,384]{2,1,0:T(8,128)} %fusion.53, f32[384]{0:T(512)S(1)} %convert_element_type.308, bf16[8,256,1408]{2,1,0:T(8,128)(2,1)} %all-gather.16.cloned.1.call-done, bf16[384,1408]{1,0:T(8,128)(2,1)S(1)} %copy-done), kind=kOutput, calls=%fused_computation.220 | convolution fusion | flops 2231893504 | bytes 11569408 | tf_op jit(solution)/shard_map/bnd,fd->bnf/dot_general | solution.py:11
  390.8 1.1 copy-done.65
  391.9 5.0 convolution_convert_fusion
  397.1 57.6 %reduce-scatter.14.cloned.1.call-done = bf16[8,16,1408]{2,1,0:T(8,128)(2,1)} async-done(((bf16[8,256,1408]{2,1,0:T(8,128)(2,1)}), bf16[8,16,1408]{2,1,0:T(8,128)(2,1)}) %reduce-scatter.14.cloned.1.call-update) | async-done | bytes 360464 | tf_op jit(solution)/shard_map/reduce_scatter | solution.py:56
  454.7 1.2 fusion.65
  455.9 2.1 fusion.134
  458.1 10.6 %reduce-scatter.12.cloned.1.call-start = ((), (), s32[]{:S(2)}) async-start(), calls=%async_computation.13 | async-start | bytes 6127616 | tf_op jit(solution)/shard_map/reduce_scatter | solution.py:56
  468.7 7.9 convolution_convert_fusion.1
  476.8 25.0 %all-gather.18.cloned.1.call-done = bf16[8,256,1408]{2,1,0:T(8,128)(2,1)} async-done(((bf16[8,16,1408]{2,1,0:T(8,128)(2,1)}), bf16[8,256,1408]{2,1,0:T(8,128)(2,1)}) %all-gather.18.cloned.1.call-update) | async-done | bytes 5767184 | tf_op jit(solution)/shard_map/all_gather | solution.py:52
  501.8 4.6 convolution_convert_fusion.10
  507.2 2.9 fusion.109
  510.1 4.4 fusion.137
  514.5 5.3 convolution_convert_fusion.4
  520.5 41.2 %reduce-scatter.12.cloned.1.call-done = bf16[8,16,1408]{2,1,0:T(8,128)(2,1)} async-done(((bf16[8,256,1408]{2,1,0:T(8,128)(2,1)}), bf16[8,16,1408]{2,1,0:T(8,128)(2,1)}) %reduce-scatter.12.cloned.1.call-update) | async-done | bytes 360464 | tf_op jit(solution)/shard_map/reduce_scatter | solution.py:56
  561.7 64.0 %reduce-scatter.16.cloned.1.call-done = bf16[8,16,1408]{2,1,0:T(8,128)(2,1)} async-done(((bf16[8,256,1408]{2,1,0:T(8,128)(2,1)}), bf16[8,16,1408]{2,1,0:T(8,128)(2,1)}) %reduce-scatter.16.cloned.1.call-update) | async-done | bytes 360464 | tf_op jit(solution)/shard_map/reduce_scatter | solution.py:56
  625.7 3.8 fusion.99
  629.6 43.5 %all-gather.20.cloned.1.call-done = bf16[8,256,1408]{2,1,0:T(8,128)(2,1)} async-done(((bf16[8,16,1408]{2,1,0:T(8,128)(2,1)}), bf16[8,256,1408]{2,1,0:T(8,128)(2,1)}) %all-gather.20.cloned.1.call-update) | async-done | bytes 5767184 | tf_op jit(solution)/shard_map/all_gather | solution.py:52
  673.1 4.6 convolution_convert_fusion.9
  677.7 1.2 fusion.46
  678.9 2.8 fusion.107
  681.7 3.8 fusion.43
  685.5 3.8 fusion.42
  689.3 7.2 convolution_convert_fusion.3
  697.5 2.9 fusion.41
  700.9 5.5 convolution_convert_fusion.2
  706.5 4.2 reduce_sum.276
  710.8 7.4 fusion.10
  718.2 3.7 fusion.11
  722.7 4.2 reduce_sum.274
  726.9 4.5 fusion.19
  731.5 1.7 fusion.20
  733.2 5.1 fusion.15
  739.3 4.1 reduce_sum.269
  743.4 4.5 fusion.21
  748.0 5.5 fusion.14
  754.2 1.4 fusion.100
  755.6 47.1 %psum.7 = f32[6,1408]{1,0:T(8,128)} all-reduce(f32[6,1408]{1,0:T(8,128)S(1)} %stack.27), channel_id=1, replica_groups=mesh['dp'=4,'tp'=16] {'tp'}, use_global_device_ids=true, to_apply=%region_27.28 | all-reduce | flops 8448 | bytes 67584 | tf_op jit(solution)/shard_map/psum | solution.py:136
  802.8 2.4 fusion.91
  805.2 13.3 %reduce-scatter.20.cloned.1.call-done = bf16[8,16,1408]{2,1,0:T(8,128)(2,1)} async-done(((bf16[8,256,1408]{2,1,0:T(8,128)(2,1)}), bf16[8,16,1408]{2,1,0:T(8,128)(2,1)}) %reduce-scatter.20.cloned.1.call-update) | async-done | bytes 360464 | tf_op jit(solution)/shard_map/reduce_scatter | solution.py:56
  (203 shorter events, 12.8 us)
Async XLA Ops:
  7.2 374.0 %copy-start = (bf16[384,1408]{1,0:T(8,128)(2,1)S(1)}, bf16[384,1408]{1,0:T(8,128)(2,1)}, u32[]{:S(2)}) copy-start(bf16[384,1408]{1,0:T(8,128)(2,1)} %param.37) | copy-start | bytes 3244036
  7.2 7.1 copy-start.58
  7.2 53.4 %copy-start.63 = (bf16[1408,1,264]{0,2,1:T(8,128)(2,1)S(1)}, bf16[1408,1,264]{0,2,1:T(8,128)(2,1)}, u32[]{:S(2)}) copy-start(bf16[1408,1,264]{0,2,1:T(8,128)(2,1)} %param.25) | copy-start | bytes 2230276
  7.2 53.4 %all-gather.8.cloned.1.call-start = ((), (), s32[]{:S(2)}) async-start(), calls=%async_computation.7 | async-start | bytes 6127616 | tf_op jit(solution)/shard_map/all_gather | solution.py:52
  14.2 119.0 %reduce-scatter.8.cloned.1.call-start = ((), (), s32[]{:S(2)}) async-start(), calls=%async_computation.8 | async-start | bytes 6127616 | tf_op jit(solution)/shard_map/reduce_scatter | solution.py:56
  75.3 57.9 %copy-start.2 = (bf16[8,16,1408]{2,1,0:T(8,128)(2,1)S(1)}, bf16[8,16,1408]{2,1,0:T(8,128)(2,1)}, u32[]{:S(2)}) copy-start(bf16[8,16,1408]{2,1,0:T(8,128)(2,1)} %param.20) | copy-start | bytes 1081348
  75.3 59.9 %copy-start.60 = (bf16[1,176]{1,0:T(2,128)(2,1)S(1)}, bf16[1,176]{1,0:T(2,128)(2,1)}, u32[]{:S(2)}) copy-start(bf16[1,176]{1,0:T(2,128)(2,1)} %param.32) | copy-start | bytes 1060
  75.4 59.9 %copy-start.64 = (bf16[1,88]{1,0:T(2,128)(2,1)S(1)}, bf16[1,88]{1,0:T(2,128)(2,1)}, u32[]{:S(2)}) copy-start(bf16[1,88]{1,0:T(2,128)(2,1)} %param.30) | copy-start | bytes 532
  75.4 59.9 %copy-start.61 = (s32[8]{0:T(128)S(1)}, s32[8]{0:T(128)}, u32[]{:S(2)}) copy-start(s32[8]{0:T(128)} %param.23) | copy-start | bytes 100
  75.4 102.9 %all-gather.10.cloned.1.call-start = ((), (), s32[]{:S(2)}) async-start(), calls=%async_computation.9 | async-start | bytes 6127616 | tf_op jit(solution)/shard_map/all_gather | solution.py:52
  76.2 143.7 %all-gather.12.cloned.1.call-start = ((), (), s32[]{:S(2)}) async-start(), calls=%async_computation.10 | async-start | bytes 6127616 | tf_op jit(solution)/shard_map/all_gather | solution.py:52
  76.3 107.7 %copy-start.41 = (f32[1408]{0:T(1024)}, f32[1408]{0:T(1024)S(1)}, u32[]{:S(2)}) copy-start(f32[1408]{0:T(1024)S(1)} %convert_element_type.292) | copy-start | bytes 16900
  135.2 158.0 %reduce-scatter.10.cloned.1.call-start = ((), (), s32[]{:S(2)}) async-start(), calls=%async_computation.11 | async-start | bytes 6127616 | tf_op jit(solution)/shard_map/reduce_scatter | solution.py:56
  178.3 41.6 %copy-start.26 = (bf16[1408,1,88]{0,2,1:T(8,128)(2,1)S(1)}, bf16[1408,1,88]{0,2,1:T(8,128)(2,1)}, u32[]{:S(2)}) copy-start(bf16[1408,1,88]{0,2,1:T(8,128)(2,1)} %param.29) | copy-start | bytes 743428
  235.3 59.4 %copy-start.36 = (f32[8,1408]{1,0:T(8,128)S(1)}, f32[8,1408]{1,0:T(8,128)}, u32[]{:S(2)}) copy-start(f32[8,1408]{1,0:T(8,128)} %get-tuple-element.33) | copy-start | bytes 135172
  235.3 60.8 %copy-start.5 = (bf16[8,16,1408]{2,1,0:T(8,128)(2,1)S(1)}, bf16[8,16,1408]{2,1,0:T(8,128)(2,1)}, u32[]{:S(2)}) copy-start(bf16[8,16,1408]{2,1,0:T(8,128)(2,1)} %param.39) | copy-start | bytes 1081348
  235.4 61.8 %copy-start.59 = (bf16[384]{0:T(512)(128)(2,1)S(1)}, bf16[384]{0:T(512)(128)(2,1)}, u32[]{:S(2)}) copy-start(bf16[384]{0:T(512)(128)(2,1)} %param.36) | copy-start | bytes 2308
  235.4 104.0 %all-gather.14.cloned.1.call-start = ((), (), s32[]{:S(2)}) async-start(), calls=%async_computation.12 | async-start | bytes 6127616 | tf_op jit(solution)/shard_map/all_gather | solution.py:52
  294.4 331.2 %copy-start.34 = (f32[8,16]{1,0:T(8,128)}, f32[8,16]{1,0:T(8,128)S(1)}, u32[]{:S(2)}) copy-start(f32[8,16]{1,0:T(8,128)S(1)} %broadcast_multiply_fusion.4) | copy-start | bytes 1540
  294.7 331.0 %copy-start.37 = (f32[8,16]{1,0:T(8,128)}, f32[8,16]{1,0:T(8,128)S(1)}, u32[]{:S(2)}) copy-start(f32[8,16]{1,0:T(8,128)S(1)} %add_rsqrt_fusion) | copy-start | bytes 1540
  295.9 85.3 %all-gather.16.cloned.1.call-start = ((), (), s32[]{:S(2)}) async-start(), calls=%async_computation.14 | async-start | bytes 6127616 | tf_op jit(solution)/shard_map/all_gather | solution.py:52
  297.1 157.6 %reduce-scatter.14.cloned.1.call-start = ((), (), s32[]{:S(2)}) async-start(), calls=%async_computation.15 | async-start | bytes 6127616 | tf_op jit(solution)/shard_map/reduce_scatter | solution.py:56
  297.2 171.6 %copy-start.56 = (f32[384]{0:T(512)}, f32[384]{0:T(512)S(1)}, u32[]{:S(2)}) copy-start(f32[384]{0:T(512)S(1)} %convert_element_type.308) | copy-start | bytes 4612
  381.2 10.7 %copy-start.62 = (bf16[1408,384]{1,0:T(8,128)(2,1)S(1)}, bf16[1408,384]{1,0:T(8,128)(2,1)}, u32[]{:S(2)}) copy-start(bf16[1408,384]{1,0:T(8,128)(2,1)} %param.35) | copy-start | bytes 3244036
  397.0 104.8 %all-gather.18.cloned.1.call-start = ((), (), s32[]{:S(2)}) async-start(), calls=%async_computation.16 | async-start | bytes 6127616 | tf_op jit(solution)/shard_map/all_gather | solution.py:52
  455.9 169.8 %copy-start.45 = (f32[8,16]{1,0:T(8,128)}, f32[8,16]{1,0:T(8,128)S(1)}, u32[]{:S(2)}) copy-start(f32[8,16]{1,0:T(8,128)S(1)} %get-tuple-element.46) | copy-start | bytes 1540
  455.9 169.8 %copy-start.47 = (f32[8,16]{1,0:T(8,128)}, f32[8,16]{1,0:T(8,128)S(1)}, u32[]{:S(2)}) copy-start(f32[8,16]{1,0:T(8,128)S(1)} %get-tuple-element.47) | copy-start | bytes 1540
  458.1 103.6 %reduce-scatter.12.cloned.1.call-start = ((), (), s32[]{:S(2)}) async-start(), calls=%async_computation.13 | async-start | bytes 6127616 | tf_op jit(solution)/shard_map/reduce_scatter | solution.py:56
  476.6 25.2 %copy-start.25 = (bf16[1,88,1408]{2,1,0:T(8,128)(2,1)S(1)}, bf16[1,88,1408]{2,1,0:T(8,128)(2,1)}, u32[]{:S(2)}) copy-start(bf16[1,88,1408]{2,1,0:T(8,128)(2,1)} %param.33) | copy-start | bytes 743428
  476.7 149.0 %reduce-scatter.16.cloned.1.call-start = ((), (), s32[]{:S(2)}) async-start(), calls=%async_computation.17 | async-start | bytes 6127616 | tf_op jit(solution)/shard_map/reduce_scatter | solution.py:56
  519.8 105.8 %copy-start.42 = (f32[1408]{0:T(1024)S(1)}, f32[1408]{0:T(1024)}, u32[]{:S(2)}) copy-start(f32[1408]{0:T(1024)} %copy-done.41) | copy-start | bytes 16900
  519.9 153.2 %all-gather.20.cloned.1.call-start = ((), (), s32[]{:S(2)}) async-start(), calls=%async_computation.18 | async-start | bytes 6127616 | tf_op jit(solution)/shard_map/all_gather | solution.py:52
  629.5 124.7 %reduce-scatter.18.cloned.1.call-start = ((), (), s32[]{:S(2)}) async-start(), calls=%async_computation.19 | async-start | bytes 6127616 | tf_op jit(solution)/shard_map/reduce_scatter | solution.py:56
  681.7 7.6 copy-start.17
  696.6 121.9 %reduce-scatter.20.cloned.1.call-start = ((), (), s32[]{:S(2)}) async-start(), calls=%async_computation.20 | async-start | bytes 6127616 | tf_op jit(solution)/shard_map/reduce_scatter | solution.py:56
  700.4 6.0 copy-start.19
  700.9 5.6 copy-start.14
  706.5 11.6 %slice-start.2 = ((s8[5767168]{0:T(1024)(128)(4,1)}), s8[1572864]{0:T(1024)(128)(4,1)S(1)}, s32[]{:S(2)}) async-start(s8[5767168]{0:T(1024)(128)(4,1)} %bitcast.244), calls=%async_computation.23 | async-start | bytes 3145728
  710.7 7.4 slice-start.3
  710.7 7.4 copy-start.57
  710.7 7.4 copy-start.66
  722.7 4.2 copy-start.11
  722.7 8.8 %slice-start = ((s8[5767168]{0:T(1024)(128)(4,1)}), s8[1572864]{0:T(1024)(128)(4,1)S(1)}, s32[]{:S(2)}) async-start(s8[5767168]{0:T(1024)(128)(4,1)} %bitcast.242), calls=%async_computation.21 | async-start | bytes 3145728
  726.9 4.5 slice-start.1
  726.9 4.5 copy-start.21
  733.2 5.1 copy-start.52
  733.2 5.1 copy-start.51
  733.2 5.2 copy-start.50
  733.2 5.2 copy-start.49
  733.2 5.2 copy-start.18
  733.2 5.2 copy-start.30
  733.2 5.2 copy-start.32
  743.4 4.5 copy-start.31
  743.4 4.5 copy-start.33
  747.9 6.3 copy-start.40
  747.9 6.3 copy-start.44
  747.9 54.9 %copy-start.6 = (bf16[8,16,1408]{2,1,0:T(8,128)(2,1)S(1)}, bf16[8,16,1408]{2,1,0:T(8,128)(2,1)}, u32[]{:S(2)}) copy-start(bf16[8,16,1408]{2,1,0:T(8,128)(2,1)} %param.39) | copy-start | bytes 1081348
  747.9 54.9 %copy-start.7 = (bf16[8,16,1408]{2,1,0:T(8,128)(2,1)S(1)}, bf16[8,16,1408]{2,1,0:T(8,128)(2,1)}, u32[]{:S(2)}) copy-start(bf16[8,16,1408]{2,1,0:T(8,128)(2,1)} %reduce-scatter.14.cloned.1.call-done) | copy-start | bytes 1081348
  747.9 54.9 %copy-start.16 = (bf16[8,16,1408]{2,1,0:T(8,128)(2,1)S(1)}, bf16[8,16,1408]{2,1,0:T(8,128)(2,1)}, u32[]{:S(2)}) copy-start(bf16[8,16,1408]{2,1,0:T(8,128)(2,1)} %reduce-scatter.16.cloned.1.call-done) | copy-start | bytes 1081348
  747.9 54.9 %copy-start.35 = (f32[8,16]{1,0:T(8,128)S(1)}, f32[8,16]{1,0:T(8,128)}, u32[]{:S(2)}) copy-start(f32[8,16]{1,0:T(8,128)} %copy-done.34) | copy-start | bytes 1540
  747.9 54.9 %copy-start.38 = (f32[8,16]{1,0:T(8,128)S(1)}, f32[8,16]{1,0:T(8,128)}, u32[]{:S(2)}) copy-start(f32[8,16]{1,0:T(8,128)} %copy-done.37) | copy-start | bytes 1540
  747.9 54.9 %copy-start.46 = (f32[8,16]{1,0:T(8,128)S(1)}, f32[8,16]{1,0:T(8,128)}, u32[]{:S(2)}) copy-start(f32[8,16]{1,0:T(8,128)} %copy-done.45) | copy-start | bytes 1540
  747.9 54.9 %copy-start.48 = (f32[8,16]{1,0:T(8,128)S(1)}, f32[8,16]{1,0:T(8,128)}, u32[]{:S(2)}) copy-start(f32[8,16]{1,0:T(8,128)} %copy-done.47) | copy-start | bytes 1540
  747.9 70.6 %copy-start.1 = (bf16[384,1408]{1,0:T(8,128)(2,1)S(1)}, bf16[384,1408]{1,0:T(8,128)(2,1)}, u32[]{:S(2)}) copy-start(bf16[384,1408]{1,0:T(8,128)(2,1)} %param.37) | copy-start | bytes 3244036
  (21 other events, 50.7 us)
Sparse Core Ops, SparseCore 0:
  14.3 46.2 all-gather.7
  75.6 57.6 reduce-scatter.7
  134.9 43.3 all-gather.9
  180.4 39.5 all-gather.11
  235.5 57.6 reduce-scatter.9
  296.0 43.3 all-gather.13
  341.6 39.5 all-gather.15
  397.1 57.4 reduce-scatter.13
  458.2 43.5 all-gather.17
  504.0 57.6 reduce-scatter.11
  564.1 61.5 reduce-scatter.15
  629.6 43.3 all-gather.19
  696.7 57.4 reduce-scatter.17
  757.0 61.4 reduce-scatter.19
where the time goes:
time: 837 us; the launch traced here: 825 us
  waiting for transfers between devices  562 us (67%)
  matrix products  143 us (17%)
  blocking collectives  47.1 us (6%)
  other arithmetic  39.7 us (5%)
  between operations  15.1 us (2%)
  starting transfers between devices  11.9 us (1%)
    reduce_scatter x7, waiting for transfers between devices, reduce_tokens(): lax.psum_scatter(tensor.astype(jnp.bfloat16), 'tp', scatter_dimension=1,...  291 us
    all_gather x7, waiting for transfers between devices, gather_tokens(): return lax.all_gather(tensor, 'tp', axis=1, tiled=True)  270 us
    dot_general x31, matrix products, product(): return jnp.einsum(form, lhs, rhs, preferred_element_type=jnp.float32)  137 us
    psum x1, blocking collectives, device_block(): lax.psum(jnp.stack([token_sum(g_h1), token_sum(g_h1 * normed1), g_gate1,...  47.1 us
    reduce_sum x7, other arithmetic, token_sum(): return jnp.sum(tensor.astype(jnp.float32), axis=(0, 1))  18.1 us
  transfers between devices with their start and end apart: 14, of which 14 were waited for; matrix products, arithmetic and copies ran while one was open for 12% of the time, Pallas kernels for 0%

commit v1 on v0

v1 whole, which is shorter than its diff:
```python
import functools

import jax
import jax.numpy as jnp
from jax import lax
from jax.experimental import pallas as pl
from jax.experimental.pallas import tpu as pltpu
from jax.sharding import PartitionSpec as P

LN_EPS = 1e-6
MASK_FILL = -1e30
LANES = 128
MESH = pl.DeviceIdType.MESH
BF16 = jnp.bfloat16
F32 = jnp.float32
VMEM_LIMIT = 66 * 1000 * 1000
NN = (((1,), (0,)), ((), ()))
NT = (((1,), (1,)), ((), ()))
TN = (((0,), (0,)), ((), ()))
UP, DOWN = 0, 1


def dot(lhs, rhs, dims=NN):
    return lax.dot_general(lhs, rhs, dims, preferred_element_type=F32)


def place(tp_size):
    me = lax.axis_index('tp')
    return tp_size // 2, me // 2, lax.rem(me, 2)


def greet(ring, chip, core):
    barrier = pltpu.get_barrier_semaphore()
    for zz, cc in ((lax.rem(chip + 1, ring), core), (lax.rem(chip + ring - 1, ring), core), (chip, 1 - core)):
        pl.semaphore_signal(barrier, inc=1, device_id={'tp': zz * 2 + cc}, device_id_type=MESH)
    pl.semaphore_wait(barrier, 3)


def gather_body(tp_size, n_src, n_in, saves, n_acc, compute, *refs):
    ring, chip, core = place(tp_size)
    half = ring // 2
    srcs, refs = refs[:n_src], refs[n_src:]
    ins, refs = refs[:n_in], refs[n_in:]
    n_save = len(saves)
    full, rsend, rrecv, ssend, srecv, save_sem = refs[-6:]
    outs = refs[:-6]
    saved, outs = outs[:n_save], outs[n_save:]
    batch, n_loc = srcs[0].shape[0], srcs[0].shape[1]
    hb = batch * n_src // 2

    for acc in outs[len(outs) - n_acc:]:
        acc[...] = jnp.zeros_like(acc)

    def wrap(zz):
        return lax.rem(zz + ring, ring)

    def part(zz, cc, ch):
        row = pl.multiple_of((zz * 2 + cc) * n_loc, n_loc)
        return full.at[pl.ds(ch * hb, hb), pl.ds(row, n_loc), :]

    def own(ch):
        return srcs[ch] if n_src == 2 else srcs[0].at[pl.ds(ch * hb, hb)]

    def ring_copy(way, k, ch, sending):
        sign = -1 if way == UP else 1
        zb = wrap(chip + sign * (k - 1 if sending else k))
        src = own(ch) if (sending and k == 1) else part(zb, core, ch)
        return pltpu.make_async_remote_copy(
            src_ref=src, dst_ref=part(zb, core, ch),
            send_sem=rsend.at[way, k - 1, ch], recv_sem=rrecv.at[way, k - 1, ch],
            device_id={'tp': wrap(chip - sign) * 2 + core}, device_id_type=MESH)

    def chip_at(slot):
        k = (slot + 1) // 2
        return wrap(chip - k) if slot % 2 else wrap(chip + k)

    def sib_copy(slot, ch, sending):
        zb = chip_at(slot)
        cc = core if sending else 1 - core
        src = own(ch) if (sending and slot == 0) else part(zb, cc, ch)
        return pltpu.make_async_remote_copy(
            src_ref=src, dst_ref=part(zb, cc, ch),
            send_sem=ssend.at[slot, ch], recv_sem=srecv.at[slot, ch],
            device_id={'tp': chip * 2 + 1 - core}, device_id_type=MESH)

    def carries(way, k, ch):
        return k < half or (k == half and ch == way)

    def slot_of(way, k):
        return 2 * half - 1 if k == half else (2 * k - 1 if way == UP else 2 * k)

    greet(ring, chip, core)
    ring_copy(UP, 1, 0, True).start()
    ring_copy(DOWN, 1, 1, True).start()
    ring_copy(UP, 1, 1, True).start()
    ring_copy(DOWN, 1, 0, True).start()
    sib_copy(0, 0, True).start()
    sib_copy(0, 1, True).start()
    for ch in (0, 1):
        row = pl.multiple_of((chip * 2 + core) * n_loc, n_loc)
        full[pl.ds(ch * hb, hb), pl.ds(row, n_loc), :] = own(ch)[...]

    def arrive(way, k, ch):
        ring_copy(way, k, ch, False).wait_recv()
        if carries(way, k + 1, ch):
            ring_copy(way, k + 1, ch, True).start()
        sib_copy(slot_of(way, k), ch, True).start()

    def group(g):
        k = g // 2 + 1
        if g % 2 == 0:
            arrive(UP, k, 0)
            arrive(DOWN, k, 1)
        else:
            arrive(UP, k, 1)
            arrive(DOWN, k, 0)

    def save_copy(stream, slot, zz):
        rows = pl.ds(pl.multiple_of(zz * 2 * n_loc, 2 * n_loc), 2 * n_loc)
        return pltpu.make_async_copy(
            full.at[pl.ds(saves[stream] * batch, batch), rows, :], saved[stream].at[:, rows, :], save_sem.at[stream, slot])

    def step(slot, carry):
        for s in range(ring):
            @pl.when(slot == s)
            def _():
                if s < ring - 2:
                    group(s)
                elif s == ring - 1:
                    group(ring - 2)
                sib_copy(s, 0, False).wait_recv()
                sib_copy(s, 1, False).wait_recv()
        k = (slot + 1) // 2
        sign = 1 - 2 * lax.rem(slot, 2)
        zz = wrap(chip + sign * k)
        rows = pl.ds(pl.multiple_of(zz * 2 * n_loc, 2 * n_loc), 2 * n_loc)
        for stream in range(n_save):
            save_copy(stream, slot, zz).start()
        compute(rows, lambda i: full[pl.ds(i * batch, batch), rows, :].reshape(batch * 2 * n_loc, full.shape[2]), ins, outs)
        return carry

    lax.fori_loop(0, ring, step, None)

    for way in (UP, DOWN):
        for k in range(1, half + 1):
            for ch in (0, 1):
                if carries(way, k, ch):
                    ring_copy(way, k, ch, True).wait_send()
    for slot in range(ring):
        for ch in (0, 1):
            sib_copy(slot, ch, True).wait_send()
        for stream in range(n_save):
            save_copy(stream, slot, chip_at(slot)).wait()


def gather_call(tp_size, cid, name, blocks, ins, saves, outs, accs, compute):
    batch, n_loc, width = blocks[0].shape
    n_tok = n_loc * tp_size
    ring, half = tp_size // 2, tp_size // 4
    vmem = pl.BlockSpec(memory_space=pltpu.VMEM)
    return pl.pallas_call(
        functools.partial(gather_body, tp_size, len(blocks), len(ins), saves, len(accs), compute),
        out_shape=[jax.ShapeDtypeStruct((batch, n_tok, width), BF16)] * len(saves)
        + [jax.ShapeDtypeStruct(s, BF16) for s in outs] + [jax.ShapeDtypeStruct(s, F32) for s in accs],
        in_specs=[vmem] * (len(blocks) + len(ins)),
        out_specs=[pl.BlockSpec(memory_space=pl.ANY)] * len(saves) + [vmem] * (len(outs) + len(accs)),
        scratch_shapes=[
            pltpu.VMEM((batch * len(blocks), n_tok, width), BF16),
            pltpu.SemaphoreType.DMA((2, half, 2)),
            pltpu.SemaphoreType.DMA((2, half, 2)),
            pltpu.SemaphoreType.DMA((ring, 2)),
            pltpu.SemaphoreType.DMA((ring, 2)),
            pltpu.SemaphoreType.DMA((max(1, len(saves)), ring)),
        ],
        compiler_params=pltpu.CompilerParams(collective_id=cid, has_side_effects=True, vmem_limit_bytes=VMEM_LIMIT),
        name=name,
    )(*blocks, *ins)


def scatter_body(tp_size, n_out, n_in, n_load, n_acc, compute, *refs):
    ring, chip, core = place(tp_size)
    half = ring // 2
    ins, refs = refs[:n_in], refs[n_in:]
    loads, refs = refs[:n_load], refs[n_load:]
    result, refs = refs[0], refs[1:]
    accs, refs = refs[:n_acc], refs[n_acc:]
    held, refs = refs[:n_load], refs[n_load:]
    pbuf, sibr, snd, rcv, rsend, rrecv, ssend, srecv, load_sem = refs
    nb, n_loc = result.shape[0], result.shape[1]
    batch, hb = nb // n_out, nb // 2

    def wrap(zz):
        return lax.rem(zz + ring, ring)

    def load_copy(i):
        return pltpu.make_async_copy(loads[i], held[i], load_sem.at[i])

    for i in range(n_load):
        load_copy(i).start()
    for acc in accs:
        acc[...] = jnp.zeros_like(acc)

    def ring_copy(way, s, ch):
        sign = 1 if way == UP else -1
        part = pl.ds(ch * hb, hb)
        return pltpu.make_async_remote_copy(
            src_ref=snd.at[way, s, part], dst_ref=rcv.at[way, s, part],
            send_sem=rsend.at[way, s, ch], recv_sem=rrecv.at[way, s, ch],
            device_id={'tp': wrap(chip + sign) * 2 + core}, device_id_type=MESH)

    def sib_copy(slot):
        rows = pl.ds(pl.multiple_of((1 - core) * n_loc, n_loc), n_loc)
        return pltpu.make_async_remote_copy(
            src_ref=pbuf.at[slot, :, rows, :], dst_ref=sibr.at[slot],
            send_sem=ssend.at[slot], recv_sem=srecv.at[slot],
            device_id={'tp': chip * 2 + 1 - core}, device_id_type=MESH)

    def own_sum(slot, part):
        rows = pl.ds(pl.multiple_of(core * n_loc, n_loc), n_loc)
        return pbuf[slot, part, rows, :].astype(F32) + sibr[slot, part].astype(F32)

    def starts_at(way, ch):
        return 0 if ch == way else 1

    def pass_on(way, s, slot, ch):
        part = pl.ds(ch * hb, hb)
        total = own_sum(slot, part)
        if s > starts_at(way, ch):
            ring_copy(way, s - 1, ch).wait_recv()
            total = total + rcv[way, s - 1, part].astype(F32)
        snd[way, s, part] = total.astype(BF16)
        ring_copy(way, s, ch).start()

    def ring_step(s):
        if s == 0:
            sib_copy(0).wait_recv()
            pass_on(UP, 0, 0, 0)
            pass_on(DOWN, 0, 0, 1)
            return
        sib_copy(2 * s - 1).wait_recv()
        pass_on(UP, s, 2 * s - 1, 1)
        sib_copy(2 * s).wait_recv()
        pass_on(DOWN, s, 2 * s, 0)
        pass_on(UP, s, 2 * s - 1, 0)
        pass_on(DOWN, s, 2 * s, 1)

    greet(ring, chip, core)
    for i in range(n_load):
        load_copy(i).wait()

    def step(slot, carry):
        away = half - (slot + 1) // 2
        sign = 2 * lax.rem(slot, 2) - 1
        zz = wrap(chip + sign * away)
        rows = pl.ds(pl.multiple_of(zz * 2 * n_loc, 2 * n_loc), 2 * n_loc)

        def put(i, value):
            pbuf[slot, pl.ds(i * batch, batch)] = value.astype(BF16).reshape(batch, 2 * n_loc, value.shape[-1])

        compute(rows, put, ins, held, accs)
        sib_copy(slot).start()
        for s in range(half):
            @pl.when(slot == 2 * s + 1)
            def _():
                ring_step(s)
        return carry

    lax.fori_loop(0, ring, step, None)

    sib_copy(ring - 1).wait_recv()
    for ch, order in ((1, (UP, DOWN)), (0, (DOWN, UP))):
        part = pl.ds(ch * hb, hb)
        total = own_sum(ring - 1, part)
        for way in order:
            ring_copy(way, half - 1, ch).wait_recv()
            total = total + rcv[way, half - 1, part].astype(F32)
        result[part] = total
    for way in (UP, DOWN):
        for s in range(half):
            for ch in (0, 1):
                if s >= starts_at(way, ch):
                    ring_copy(way, s, ch).wait_send()
    for slot in range(ring):
        sib_copy(slot).wait_send()


def scatter_call(tp_size, cid, name, n_loc, width, n_out, ins, loads, accs, compute):
    batch = ins[0].shape[0]
    nb = batch * n_out
    ring, half = tp_size // 2, tp_size // 4
    vmem = pl.BlockSpec(memory_space=pltpu.VMEM)
    return pl.pallas_call(
        functools.partial(scatter_body, tp_size, n_out, len(ins), len(loads), len(accs), compute),
        out_shape=[jax.ShapeDtypeStruct((nb, n_loc, width), F32)] + [jax.ShapeDtypeStruct(s, F32) for s in accs],
        in_specs=[vmem] * len(ins) + [pl.BlockSpec(memory_space=pl.ANY)] * len(loads),
        out_specs=[vmem] * (1 + len(accs)),
        scratch_shapes=[pltpu.VMEM(a.shape, a.dtype) for a in loads] + [
            pltpu.VMEM((ring, nb, 2 * n_loc, width), BF16),
            pltpu.VMEM((ring, nb, n_loc, width), BF16),
            pltpu.VMEM((2, half, nb, n_loc, width), BF16),
            pltpu.VMEM((2, half, nb, n_loc, width), BF16),
            pltpu.SemaphoreType.DMA((2, half, 2)),
            pltpu.SemaphoreType.DMA((2, half, 2)),
            pltpu.SemaphoreType.DMA((ring,)),
            pltpu.SemaphoreType.DMA((ring,)),
            pltpu.SemaphoreType.DMA((max(1, len(loads)),)),
        ],
        compiler_params=pltpu.CompilerParams(collective_id=cid, has_side_effects=True, vmem_limit_bytes=VMEM_LIMIT),
        name=name,
    )(*ins, *loads)


def total_body(tp_size, src, out, got, mine, send1, recv1, send2, recv2):
    me = lax.axis_index('tp')
    barrier = pltpu.get_barrier_semaphore()
    for d in range(1, tp_size):
        pl.semaphore_signal(barrier, inc=1, device_id={'tp': lax.rem(me + d, tp_size)}, device_id_type=MESH)
    pl.semaphore_wait(barrier, tp_size - 1)

    def first(d):
        peer = lax.rem(me + d, tp_size)
        return pltpu.make_async_remote_copy(
            src_ref=src.at[peer], dst_ref=got.at[d - 1], send_sem=send1.at[d - 1], recv_sem=recv1.at[d - 1],
            device_id={'tp': peer}, device_id_type=MESH)

    def second(d, sending):
        peer = lax.rem(me + d, tp_size)
        slab = me if sending else lax.rem(me + tp_size - d, tp_size)
        return pltpu.make_async_remote_copy(
            src_ref=mine, dst_ref=out.at[slab], send_sem=send2.at[d - 1], recv_sem=recv2.at[d - 1],
            device_id={'tp': peer}, device_id_type=MESH)

    for d in range(1, tp_size):
        first(d).start()
    total = src[me]
    for d in range(1, tp_size):
        first(d).wait_recv()
        total = total + got[d - 1]
    mine[...] = total
    for d in range(1, tp_size):
        second(d, True).start()
    out[me] = total
    for d in range(1, tp_size):
        second(d, False).wait_recv()
    for d in range(1, tp_size):
        first(d).wait_send()
        second(d, True).wait_send()


def total_call(tp_size, cid, rows):
    width = rows[0].shape[0]
    flat = jnp.concatenate(rows)
    per = -(-flat.shape[0] // (tp_size * 8 * LANES)) * 8
    padded = jnp.pad(flat, (0, tp_size * per * LANES - flat.shape[0])).reshape(tp_size, per, LANES)
    vmem = pl.BlockSpec(memory_space=pltpu.VMEM)
    out = pl.pallas_call(
        functools.partial(total_body, tp_size),
        out_shape=jax.ShapeDtypeStruct(padded.shape, F32),
        in_specs=[vmem],
        out_specs=vmem,
        scratch_shapes=[
            pltpu.VMEM((tp_size - 1, per, LANES), F32),
            pltpu.VMEM((per, LANES), F32),
        ] + [pltpu.SemaphoreType.DMA((tp_size - 1,))] * 4,
        compiler_params=pltpu.CompilerParams(collective_id=cid, has_side_effects=True),
        name='small_total',
    )(padded)
    flat = out.reshape(-1)
    return [flat[i * width:(i + 1) * width] for i in range(len(rows))]


def layer_norm(tensor):
    tensor = tensor.astype(F32)
    centered = tensor - jnp.mean(tensor, axis=-1, keepdims=True)
    inv_std = lax.rsqrt(jnp.mean(centered * centered, axis=-1, keepdims=True) + LN_EPS)
    return centered * inv_std, inv_std


def layer_norm_back(normed, inv_std, g_normed):
    mean_g = jnp.mean(g_normed, axis=-1, keepdims=True)
    mean_gn = jnp.mean(g_normed * normed, axis=-1, keepdims=True)
    return inv_std * (g_normed - mean_g - normed * mean_gn)


def product(form, lhs, rhs):
    return jnp.einsum(form, lhs, rhs, preferred_element_type=F32)


def attend(q_all, k_all, v_all, key_ok, scale):
    scores = product('bqe,bke->bqk', q_all, k_all) * scale
    if key_ok is not None:
        scores = jnp.where(key_ok[:, None, :], scores, MASK_FILL)
    prob_bf = jax.nn.softmax(scores, axis=-1).astype(BF16)
    return product('bqk,bke->bqe', prob_bf, v_all).astype(BF16), prob_bf


def attend_back(q_all, k_all, v_all, prob_bf, g_val, scale):
    g_v = product('bqk,bqe->bke', prob_bf, g_val)
    g_prob = product('bqe,bke->bqk', g_val, v_all)
    row_dot = jnp.sum(g_prob * prob_bf, axis=-1, keepdims=True)
    g_scores = (prob_bf * (g_prob - row_dot) * scale).astype(BF16)
    g_q = product('bqk,bke->bqe', g_scores, k_all)
    g_k = product('bqk,bqe->bke', g_scores, q_all)
    return g_q.astype(BF16), g_k.astype(BF16), g_v.astype(BF16)


def pad_heads(weight, n_part, head_dim, head_pad):
    lead = weight.shape[:-1]
    weight = weight.reshape(*lead, n_part, head_dim)
    weight = jnp.pad(weight, [(0, 0)] * (len(lead) + 1) + [(0, head_pad - head_dim)])
    return weight.reshape(*lead, n_part * head_pad)


def drop_pad(grad, n_part, head_dim, head_pad):
    tail = grad.shape[1:]
    return grad.reshape(n_part, head_pad, *tail)[:, :head_dim].reshape(n_part * head_dim, *tail)


def rows_of(ref, rows):
    block = ref[:, rows, :]
    return block.reshape(block.shape[0] * block.shape[1], block.shape[2])


def put_rows(ref, rows, value):
    ref[:, rows, :] = value.astype(ref.dtype).reshape(ref.shape[0], rows.size, ref.shape[2])


def row_sum(value):
    return jnp.sum(value, axis=0, keepdims=True)


def gelu_pair(hidden):
    c0, c1 = 0.7978845608028654, 0.044715
    square = hidden * hidden
    tanh = jnp.tanh(c0 * hidden * (1.0 + c1 * square))
    half_up = 0.5 * (1.0 + tanh)
    slope = half_up + 0.5 * hidden * (1.0 - tanh * tanh) * (c0 * (1.0 + 3.0 * c1 * square))
    return hidden * half_up, slope


def token_sum(tensor):
    return jnp.sum(tensor.astype(F32), axis=(0, 1))


def device_block(tp_size, x_loc, y_loc, t_loc, len_loc, mod_table, w_qkv, b_qkv, w_o, b_o, w_q, b_q, w_kv, b_kv, w_co, b_co, w_1, b_1, w_2, b_2, g_loc):
    batch, n_loc, width = x_loc.shape
    n_tok = n_loc * tp_size
    head_dim, ffn = w_q.shape[2], w_1.shape[1]
    head_pad = -(-head_dim // LANES) * LANES
    scale = head_dim ** -0.5
    mod_rows = mod_table.astype(F32)[None] + t_loc.astype(F32).reshape(batch, 6, width)
    shift1, scale1, gate1, shift2, scale2, gate2 = [mod_rows[:, i, None, :] for i in range(6)]

    wqkv = pad_heads(w_qkv[:, 0], 3, head_dim, head_pad)
    wkv = pad_heads(w_kv[:, 0], 2, head_dim, head_pad)
    wq = pad_heads(w_q[:, 0], 1, head_dim, head_pad)
    bqkv = pad_heads(b_qkv.astype(F32), 3, head_dim, head_pad)
    bkv = pad_heads(b_kv.astype(F32), 2, head_dim, head_pad)
    bq = pad_heads(b_q.astype(F32), 1, head_dim, head_pad)
    wo = jnp.pad(w_o[0], ((0, head_pad - head_dim), (0, 0)))
    wco = jnp.pad(w_co[0], ((0, head_pad - head_dim), (0, 0)))
    b1 = b_1.astype(F32)[None]

    normed1, inv_std1 = layer_norm(x_loc)
    h1_loc = (normed1 * (1.0 + scale1) + shift1).astype(BF16)

    def project_both(rows, get, ins, outs):
        put_rows(outs[0], rows, dot(get(0), ins[0][...]) + ins[1][...])
        put_rows(outs[1], rows, dot(get(1), ins[2][...]) + ins[3][...])

    h1_all, y_all, qkv, kv = gather_call(
        tp_size, 0, 'gather_h1_y', [h1_loc, y_loc], [wqkv, bqkv, wkv, bkv], (0, 1),
        [(batch, n_tok, 3 * head_pad), (batch, n_tok, 2 * head_pad)], [], project_both)
    q_self, k_self, v_self = [qkv[..., i * head_pad:(i + 1) * head_pad] for i in range(3)]
    k_cross, v_cross = [kv[..., i * head_pad:(i + 1) * head_pad] for i in range(2)]
    attn_val, attn_prob = attend(q_self, k_self, v_self, None, scale)

    def project_out(rows, put, ins, held, accs):
        put(0, dot(rows_of(ins[0], rows), ins[1][...]))

    attn_total, = scatter_call(tp_size, 1, 'scatter_o', n_loc, width, 1, [attn_val, wo], [], [], project_out)
    attn_total = attn_total + b_o
    x1_loc = (x_loc + gate1 * attn_total).astype(BF16)

    def project_q(rows, get, ins, outs):
        put_rows(outs[0], rows, dot(get(0), ins[0][...]) + ins[1][...])

    x1_all, q_cross = gather_call(tp_size, 2, 'gather_x1', [x1_loc], [wq, bq], (0,), [(batch, n_tok, head_pad)], [], project_q)
    slot_ok = lax.broadcasted_iota(jnp.int32, (batch, n_tok), 1) < len_loc[:, None]
    cross_val, cross_prob = attend(q_cross, k_cross, v_cross, slot_ok, scale)
    cross_total, = scatter_call(tp_size, 3, 'scatter_co', n_loc, width, 1, [cross_val, wco], [], [], project_out)
    cross_total = cross_total + b_co
    x2_loc = (x1_loc + cross_total).astype(BF16)

    normed2, inv_std2 = layer_norm(x2_loc)
    h2_loc = (normed2 * (1.0 + scale2) + shift2).astype(BF16)
    g_x2 = g_loc.astype(F32)
    g_mlp_loc = (g_x2 * gate2).astype(BF16)

    def mlp(rows, get, ins, outs):
        w1, bias1, w2 = ins
        gelu_out, g_hid, acc_w1, acc_w2, acc_b1 = outs
        h2_blk, g_blk = get(0), get(1)
        hidden = dot(h2_blk, w1[...]) + bias1[...]
        act, slope = gelu_pair(hidden)
        act = act.astype(BF16)
        put_rows(gelu_out, rows, act)
        g_hidden = dot(g_blk, w2[...], NT) * slope
        acc_b1[...] += row_sum(g_hidden)
        g_hidden = g_hidden.astype(BF16)
        put_rows(g_hid, rows, g_hidden)
        acc_w1[...] += dot(g_hidden, h2_blk, TN)
        acc_w2[...] += dot(act, g_blk, TN)

    gelu_out, g_hid, g_w_1, g_w_2, g_b_1 = gather_call(
        tp_size, 4, 'gather_h2_g', [h2_loc, g_mlp_loc], [w_1, b1, w_2], (),
        [(batch, n_tok, ffn), (batch, n_tok, ffn)], [(ffn, width), (ffn, width), (1, ffn)], mlp)

    def mlp_out(rows, put, ins, held, accs):
        g_hid, act, w1, w2 = ins
        put(0, dot(rows_of(g_hid, rows), w1[...], NT))
        put(1, dot(rows_of(act, rows), w2[...]))

    both, = scatter_call(tp_size, 5, 'scatter_h2_out', n_loc, width, 2, [g_hid, gelu_out, w_1, w_2], [], [], mlp_out)
    g_h2, mlp_total = both[:batch], both[batch:] + b_2
    x_out = (x2_loc + gate2 * mlp_total).astype(BF16)
    g_gate2 = jnp.sum(g_x2 * mlp_total, axis=(0, 1))
    g_b_2 = token_sum(g_mlp_loc)
    g_shift2 = token_sum(g_h2)
    g_scale2 = token_sum(g_h2 * normed2)
    g_x2 = g_x2 + layer_norm_back(normed2, inv_std2, g_h2 * (1.0 + scale2))

    def out_back(rows, get, ins, outs):
        val, weight = ins
        g_val, acc_w = outs
        g_blk = get(0)
        put_rows(g_val, rows, dot(g_blk, weight[...], NT))
        acc_w[...] += dot(rows_of(val, rows), g_blk, TN)

    g_cross_loc = g_x2.astype(BF16)
    g_b_co = token_sum(g_cross_loc)
    g_cross_val, g_w_co = gather_call(
        tp_size, 6, 'gather_g_cross', [g_cross_loc], [cross_val, wco], (), [(batch, n_tok, head_pad)], [(head_pad, width)], out_back)
    g_q_cross, g_k_cross, g_v_cross = attend_back(q_cross, k_cross, v_cross, cross_prob, g_cross_val, scale)
    g_kv = jnp.concatenate([g_k_cross, g_v_cross], axis=-1)

    def cross_in_back(rows, put, ins, held, accs):
        g_q, g_kv, wq, wkv = ins
        g_q_blk, g_kv_blk = rows_of(g_q, rows), rows_of(g_kv, rows)
        put(0, dot(g_q_blk, wq[...], NT))
        put(1, dot(g_kv_blk, wkv[...], NT))
        accs[0][...] += dot(g_q_blk, rows_of(held[0], rows), TN)
        accs[1][...] += dot(g_kv_blk, rows_of(held[1], rows), TN)
        accs[2][...] += row_sum(g_q_blk.astype(F32))
        accs[3][...] += row_sum(g_kv_blk.astype(F32))

    both, g_w_q, g_w_kv, g_b_q, g_b_kv = scatter_call(
        tp_size, 7, 'scatter_q_kv', n_loc, width, 2, [g_q_cross, g_kv, wq, wkv], [x1_all, y_all],
        [(head_pad, width), (2 * head_pad, width), (1, head_pad), (1, 2 * head_pad)], cross_in_back)
    g_x1 = g_x2 + both[:batch]
    g_y = both[batch:]

    g_gate1 = jnp.sum(g_x1 * attn_total, axis=(0, 1))
    g_attn_loc = (g_x1 * gate1).astype(BF16)
    g_b_o = token_sum(g_attn_loc)
    g_attn_val, g_w_o = gather_call(
        tp_size, 8, 'gather_g_attn', [g_attn_loc], [attn_val, wo], (), [(batch, n_tok, head_pad)], [(head_pad, width)], out_back)
    g_qkv = jnp.concatenate(attend_back(q_self, k_self, v_self, attn_prob, g_attn_val, scale), axis=-1)

    def self_in_back(rows, put, ins, held, accs):
        g_blk = rows_of(ins[0], rows)
        put(0, dot(g_blk, ins[1][...], NT))
        accs[0][...] += dot(g_blk, rows_of(held[0], rows), TN)
        accs[1][...] += row_sum(g_blk.astype(F32))

    g_h1, g_w_qkv, g_b_qkv = scatter_call(
        tp_size, 9, 'scatter_qkv', n_loc, width, 1, [g_qkv, wqkv], [h1_all],
        [(3 * head_pad, width), (1, 3 * head_pad)], self_in_back)
    g_x = g_x1 + layer_norm_back(normed1, inv_std1, g_h1 * (1.0 + scale1))
    sums = total_call(tp_size, 10, [token_sum(g_h1), token_sum(g_h1 * normed1), g_gate1, g_shift2, g_scale2, g_gate2, g_b_o, g_b_co, g_b_2])
    g_table = jnp.stack(sums[:6])
    g_b_o, g_b_co, g_b_2 = sums[6:]

    def head_weight(grad, n_part):
        return drop_pad(grad, n_part, head_dim, head_pad).T.astype(BF16)[:, None, :]

    def head_bias(grad, n_part):
        return drop_pad(grad[0], n_part, head_dim, head_pad)[None].astype(BF16)

    return (x_out, g_x.astype(BF16), g_y.astype(BF16), g_table,
            head_weight(g_w_qkv, 3), head_bias(g_b_qkv, 3), g_w_o[None, :head_dim].astype(BF16), g_b_o.astype(BF16),
            head_weight(g_w_q, 1), head_bias(g_b_q, 1), head_weight(g_w_kv, 2), head_bias(g_b_kv, 2),
            g_w_co[None, :head_dim].astype(BF16), g_b_co.astype(BF16),
            g_w_1.T.astype(BF16), g_b_1[0].astype(BF16), g_w_2.astype(BF16), g_b_2.astype(BF16))


def solution(mesh):
    token_spec = P('dp', 'tp', None)
    group_rows = ('dp', 'tp')
    in_specs = (token_spec, token_spec, P('dp', None), P('dp'), P(None, None), P(None, 'tp', None), P('tp', None), P('tp', None, None), P(None), P(None, 'tp', None), P('tp', None), P(None, 'tp', None), P('tp', None), P('tp', None, None), P(None), P(None, 'tp'), P('tp'), P('tp', None), P(None), token_spec)
    out_specs = (token_spec, token_spec, token_spec, P('dp', None), P('dp', 'tp', None), P(group_rows, None), P(group_rows, None, None), P('dp'), P('dp', 'tp', None), P(group_rows, None), P('dp', 'tp', None), P(group_rows, None), P(group_rows, None, None), P('dp'), P('dp', 'tp'), P(group_rows), P(group_rows, None), P('dp'))
    return jax.shard_map(functools.partial(device_block, mesh.shape['tp']), mesh=mesh, in_specs=in_specs, out_specs=out_specs, check_vma=False)
```

time: 837 us -> 602 us (0.72)
  waiting for transfers between devices: 562 us -> 0 us
  Pallas kernels: 0 us -> 500 us
  matrix products: 143 us -> 27.5 us
  blocking collectives: 47.1 us -> 0 us
  local copies, waits for them, and re-layouts: 6.79 us -> 26.1 us
  between operations: 15.1 us -> 1.65 us
  starting transfers between devices: 11.9 us -> 0 us
    pallas_call x0 -> x11, Pallas kernels: none -> 500 us  [the longest x5 249 us: gather_call(): pl.pallas_call(functools.partial(gather_body, tp_size, len(blocks), len(i...]
    reduce_scatter x7 -> x0, waiting for transfers between devices: 291 us -> none  [reduce_tokens(): lax.psum_scatter(tensor.astype(jnp.bfloat16), 'tp', scatter_dimension=1,...]
    all_gather x7 -> x0, waiting for transfers between devices: 270 us -> none  [gather_tokens(): return lax.all_gather(tensor, 'tp', axis=1, tiled=True)]
    dot_general x31 -> x10, matrix products: 137 us -> 23.5 us  [product(): return jnp.einsum(form, lhs, rhs, preferred_element_type=F32)]
    psum x1 -> x0, blocking collectives: 47.1 us -> none  [device_block(): lax.psum(jnp.stack([token_sum(g_h1), token_sum(g_h1 * normed1), g_gate1,...]
    reduce_scatter x7 -> x0, starting transfers between devices: 11.2 us -> none  [reduce_tokens(): lax.psum_scatter(tensor.astype(jnp.bfloat16), 'tp', scatter_dimension=1,...]
    reduce_sum x8 -> x6, other arithmetic: 19.4 us -> 10.5 us  [the longest x4 6.59 us: token_sum(): return jnp.sum(tensor.astype(F32), axis=(0, 1))]
  transfers between devices with their start and end apart: 14 -> 0, of which waited for: 14 -> 0; matrix products, arithmetic and copies ran while one was open for 12% -> 0% of each run, Pallas kernels for 0% -> 0%
where the time goes in v1:
time: 602 us; the launch traced here: 592 us
  Pallas kernels  500 us (83%)
  other arithmetic  37.4 us (6%)
  matrix products  27.5 us (5%)
  local copies, waits for them, and re-layouts  26.1 us (4%)
    pallas_call x5, Pallas kernels, gather_call(): pl.pallas_call(functools.partial(gather_body, tp_size, len(blocks), len(i...  249 us
    pallas_call x5, Pallas kernels, scatter_call(): pl.pallas_call(functools.partial(scatter_body, tp_size, n_out, len(ins),...  235 us
    dot_general x10, matrix products, product(): return jnp.einsum(form, lhs, rhs, preferred_element_type=F32)  23.5 us
    pallas_call x1, Pallas kernels, total_call(): pl.pallas_call(functools.partial(total_body, tp_size), out_shape=jax.Shap...  16.3 us

profile of v1, /device:TPU:21, one launch (start us, length us, event | category | flops | bytes accessed | tf_op | source)
XLA Modules:
  0.0 592.4 jit_solution(9976301500343035387)
XLA Ops:
  0.7 1.3 bitcast_convert_fusion.refs_2_
  1.9 0.7 reduce.1
  3.3 0.7 reduce
  4.7 1.2 reshape.223.refs_3_
  5.9 0.7 iota_compare_fusion
  6.6 1.1 convert_reduce_fusion.1
  7.7 1.2 fusion.55
  9.0 0.7 convert_element_type.206
  9.7 0.7 convert_element_type.211
  10.4 0.7 convert_element_type.217
  11.1 0.7 convert_element_type.202
  11.8 1.0 convert_add_fusion.3
  12.8 1.7 pad.42.refs_1_.refs_2_
  14.5 0.8 pad.45.refs_1_.refs_2_
  15.3 1.1 fusion.48.refs_0_
  16.6 0.8 pad_bitcast_fusion.refs_1_.refs_2_
  17.4 1.0 copy.60
  18.4 0.8 pad.40
  19.2 1.0 copy.105
  20.3 1.4 copy.61.refs_2_.refs_1_
  21.7 70.9 %gather_h1_y.1 = (bf16[8,256,1408]{2,1,0:T(8,128)(2,1)}, bf16[8,256,1408]{2,1,0:T(8,128)(2,1)}, bf16[8,256,384]{2,1,0:T(8,128)(2,1)}, bf16[8,256,256]{2,1,0:T(8,128)(2,1)}) custom-call(bf16[8,16,1408]{2,1,0:T(8,128)(2,1)} %fusion.48.refs_0_, bf16[8,16,1408]{2,1,0:T(8,128)(2,1)} %refs_1_.1, bf16[1408,384]{1,0:T(8,128)(2,1)} %copy.61.refs_2_.refs_1_, ...), custom_call_target="tpu_custom_call" | custom-call | tf_op jit(solution)/shard_map/gather_h1_y/pallas_call | solution.py:161
  92.6 2.0 fusion.112
  94.8 1.0 copy-done.2
  95.8 2.4 convolution_convert_fusion.3.refs_0_.refs_1_
  98.2 33.2 %scatter_o.1 = f32[8,16,1408]{2,1,0:T(8,128)} custom-call(bf16[8,256,128]{2,1,0:T(8,128)(2,1)} %convolution_convert_fusion.3.refs_0_.refs_1_, bf16[128,1408]{1,0:T(8,128)(2,1)} %pad.42.refs_1_.refs_2_), custom_call_target="tpu_custom_call" | custom-call | tf_op jit(solution)/shard_map/scatter_o/pallas_call | solution.py:292
  131.3 2.0 fusion.56.refs_0_
  133.3 36.6 %gather_x1.1 = (bf16[8,256,1408]{2,1,0:T(8,128)(2,1)}, bf16[8,256,128]{2,1,0:T(8,128)(2,1)}) custom-call(bf16[8,16,1408]{2,1,0:T(8,128)(2,1)} %fusion.56.refs_0_, bf16[1408,128]{1,0:T(8,128)(2,1)} %pad_bitcast_fusion.refs_1_.refs_2_, f32[1,128]{1,0:T(1,128)} %bitcast_convert_fusion.refs_2_), custom_call_target="tpu_custom_call" | custom-call | tf_op jit(solution)/shard_map/gather_x1/pallas_call | solution.py:161
  169.9 2.1 fusion.117
  172.2 1.0 copy-done.3
  173.5 1.3 convolution_convert_fusion.2.refs_0_.refs_1_
  174.8 34.6 %scatter_co.1 = f32[8,16,1408]{2,1,0:T(8,128)} custom-call(bf16[8,256,128]{2,1,0:T(8,128)(2,1)} %convolution_convert_fusion.2.refs_0_.refs_1_, bf16[128,1408]{1,0:T(8,128)(2,1)} %pad.45.refs_1_.refs_2_), custom_call_target="tpu_custom_call" | custom-call | tf_op jit(solution)/shard_map/scatter_co/pallas_call | solution.py:292
  209.3 1.4 convert_reduce_fusion
  211.0 2.2 convert_reduce_fusion.2
  213.2 67.7 %gather_h2_g.1 = (bf16[8,256,384]{2,1,0:T(8,128)(2,1)}, bf16[8,256,384]{2,1,0:T(8,128)(2,1)}, f32[384,1408]{1,0:T(8,128)}, f32[384,1408]{1,0:T(8,128)}, f32[1,384]{1,0:T(1,128)}) custom-call(bf16[8,16,1408]{2,1,0:T(8,128)(2,1)} %get-tuple-element.143.refs_0_, bf16[8,16,1408]{2,1,0:T(8,128)(2,1)} %get-tuple-element.113.refs_1_, bf16[1408,384]{1,0:T(8,128)(2,1)} %refs_2_.3, ...), custom_call_target="tpu_custom_call" | custom-call | tf_op jit(solution)/shard_map/gather_h2_g/pallas_call | solution.py:161
  280.9 63.2 %scatter_h2_out.1 = f32[16,16,1408]{2,1,0:T(8,128)} custom-call(bf16[8,256,384]{2,1,0:T(8,128)(2,1)} %get-tuple-element.44.refs_0_, bf16[8,256,384]{2,1,0:T(8,128)(2,1)} %get-tuple-element.45.refs_1_, bf16[1408,384]{1,0:T(8,128)(2,1)} %refs_2_.3, bf16[384,1408]{1,0:T(8,128)(2,1)} %refs_3_.1), custom_call_target="tpu_custom_call" | custom-call | tf_op jit(solution)/shard_map/scatter_h2_out/pallas_call | solution.py:292
  344.6 2.7 fusion.59
  347.4 1.1 convert_reduce_fusion.3
  348.5 36.5 %gather_g_cross.1 = (bf16[8,256,128]{2,1,0:T(8,128)(2,1)}, f32[128,1408]{1,0:T(8,128)}) custom-call(bf16[8,16,1408]{2,1,0:T(8,128)(2,1)} %get-tuple-element.115.refs_0_, bf16[8,256,128]{2,1,0:T(8,128)(2,1)} %convolution_convert_fusion.2.refs_0_.refs_1_, bf16[128,1408]{1,0:T(8,128)(2,1)} %pad.45.refs_1_.refs_2_), custom_call_target="tpu_custom_call" | custom-call | tf_op jit(solution)/shard_map/gather_g_cross/pallas_call | solution.py:161
  385.0 1.9 fusion.75
  386.9 2.6 convolution_convert_fusion.1
  389.6 1.6 copy.82
  391.3 2.8 convert_element_type.249
  394.5 3.5 fusion.18.refs_0_
  398.0 3.3 fusion.19
  401.3 2.3 pad_maximum_fusion.1.refs_1_
  403.6 66.4 %scatter_q_kv.1 = (f32[16,16,1408]{2,1,0:T(8,128)}, f32[128,1408]{1,0:T(8,128)}, f32[256,1408]{1,0:T(8,128)}, f32[1,128]{1,0:T(1,128)}, f32[1,256]{1,0:T(1,128)}) custom-call(bf16[8,256,128]{2,1,0:T(8,128)(2,1)} %fusion.18.refs_0_, bf16[8,256,256]{2,1,0:T(8,128)(2,1)} %pad_maximum_fusion.1.refs_1_, bf16[1408,128]{1,0:T(8,128)(2,1)} %pad_bitcast_fusion.refs_1_.refs_2_, ...), custom_call_target="tpu_custom_call" | custom-call | tf_op jit(solution)/shard_map/scatter_q_kv/pallas_call | solution.py:292
  470.0 2.9 convert_reduce_fusion.4
  473.0 0.7 slice_bitcast_fusion
  474.9 1.9 slice.232
  476.8 37.0 %gather_g_attn.1 = (bf16[8,256,128]{2,1,0:T(8,128)(2,1)}, f32[128,1408]{1,0:T(8,128)}) custom-call(bf16[8,16,1408]{2,1,0:T(8,128)(2,1)} %get-tuple-element.117.refs_0_, bf16[8,256,128]{2,1,0:T(8,128)(2,1)} %convolution_convert_fusion.3.refs_0_.refs_1_, bf16[128,1408]{1,0:T(8,128)(2,1)} %pad.42.refs_1_.refs_2_), custom_call_target="tpu_custom_call" | custom-call | tf_op jit(solution)/shard_map/gather_g_attn/pallas_call | solution.py:161
  513.8 1.9 fusion.74
  515.7 1.8 convolution_convert_fusion
  517.6 0.8 slice.157
  518.5 1.5 fusion.66
  520.0 3.5 fusion.16
  523.5 3.2 fusion.17
  526.7 2.6 pad_maximum_fusion.refs_0_
  529.4 37.5 %scatter_qkv.1 = (f32[8,16,1408]{2,1,0:T(8,128)}, f32[384,1408]{1,0:T(8,128)}, f32[1,384]{1,0:T(1,128)}) custom-call(bf16[8,256,384]{2,1,0:T(8,128)(2,1)} %pad_maximum_fusion.refs_0_, bf16[1408,384]{1,0:T(8,128)(2,1)} %copy.61.refs_2_.refs_1_, bf16[8,256,1408]{2,1,0:T(8,128)(2,1)} %get-tuple-element.51.refs_2_), custom_call_target="tpu_custom_call" | custom-call | tf_op jit(solution)/shard_map/scatter_qkv/pallas_call | solution.py:292
  566.9 1.8 convert.52
  568.7 0.9 slice.153
  570.7 1.2 multiply_reduce_fusion.1
  572.6 16.3 %small_total.1 = f32[16,8,128]{2,1,0:T(8,128)} custom-call(f32[16,8,128]{2,1,0:T(8,128)} %pad_bitcast_fusion.1.src), custom_call_target="tpu_custom_call" | custom-call | tf_op jit(solution)/shard_map/small_total/pallas_call | solution.py:356
  588.9 0.8 bitcast_convert_fusion.1
  590.4 0.8 fusion.110
  (93 shorter events, 8.3 us)
Async XLA Ops:
  0.7 14.6 %copy-start.1 = (bf16[8,16,1408]{2,1,0:T(8,128)(2,1)S(1)}, bf16[8,16,1408]{2,1,0:T(8,128)(2,1)}, u32[]{:S(2)}) copy-start(bf16[8,16,1408]{2,1,0:T(8,128)(2,1)} %param.20) | copy-start | bytes 1081348
  0.7 13.9 %copy-start.17 = (bf16[1,88,1408]{2,1,0:T(8,128)(2,1)S(1)}, bf16[1,88,1408]{2,1,0:T(8,128)(2,1)}, u32[]{:S(2)}) copy-start(bf16[1,88,1408]{2,1,0:T(8,128)(2,1)} %param.33) | copy-start | bytes 743428
  0.7 15.7 %copy-start.18 = (bf16[1408,1,88]{0,2,1:T(8,128)(2,1)S(1)}, bf16[1408,1,88]{0,2,1:T(8,128)(2,1)}, u32[]{:S(2)}) copy-start(bf16[1408,1,88]{0,2,1:T(8,128)(2,1)} %param.29) | copy-start | bytes 743428
  11.8 5.6 copy-start.16
  17.4 2.8 copy-start.14
  94.8 1.0 copy-start.2
  172.0 1.5 copy-start.12
  172.2 1.0 copy-start.3
  280.8 63.2 %copy-start.19 = (f32[1,384]{1,0:T(1,128)S(1)}, f32[1,384]{1,0:T(1,128)}, u32[]{:S(2)}) copy-start(f32[1,384]{1,0:T(1,128)} %get-tuple-element.62) | copy-start | bytes 4612
  344.0 3.3 copy-start
  344.0 3.3 copy-start.5
  385.0 4.5 copy-start.8
  391.2 2.8 copy-start.9
  391.2 2.8 copy-start.13
  470.0 3.0 copy-start.15
  470.0 3.7 copy-start.22
  470.0 4.2 copy-start.21
  513.8 3.7 copy-start.11
  517.5 1.1 copy-start.10
  566.9 2.8 copy-start.20
  566.9 3.4 copy-start.6
  568.7 2.0 copy-start.4
  568.7 2.0 copy-start.7

commit v2 on v1

--- a/solution.py
+++ b/solution.py
@@ -13,7 +13,7 @@
 MESH = pl.DeviceIdType.MESH
 BF16 = jnp.bfloat16
 F32 = jnp.float32
-VMEM_LIMIT = 66 * 1000 * 1000
+VMEM_LIMIT = 67 * 1000 * 1000
 NN = (((1,), (0,)), ((), ()))
 NT = (((1,), (1,)), ((), ()))
 TN = (((0,), (0,)), ((), ()))
@@ -310,63 +310,706 @@
     )(*ins, *loads)
 
 
-def total_body(tp_size, src, out, got, mine, send1, recv1, send2, recv2):
-    me = lax.axis_index('tp')
-    barrier = pltpu.get_barrier_semaphore()
-    for d in range(1, tp_size):
-        pl.semaphore_signal(barrier, inc=1, device_id={'tp': lax.rem(me + d, tp_size)}, device_id_type=MESH)
-    pl.semaphore_wait(barrier, tp_size - 1)
-
-    def first(d):
-        peer = lax.rem(me + d, tp_size)
+class Place:
+    def __init__(self, tp_size):
+        self.tp_size = tp_size
+        self.me = lax.axis_index('tp')
+        self.ring, self.chip, self.core = tp_size // 2, self.me // 2, lax.rem(self.me, 2)
+        self.half = self.ring // 2
+
+    def wrap(self, zz):
+        return lax.rem(zz + self.ring, self.ring)
+
+    def sibling(self):
+        return {'tp': self.chip * 2 + 1 - self.core}
+
+    def ahead(self, sign):
+        return {'tp': self.wrap(self.chip + sign) * 2 + self.core}
+
+    def greet_all(self):
+        barrier = pltpu.get_barrier_semaphore()
+        for d in range(1, self.tp_size):
+            pl.semaphore_signal(barrier, inc=1, device_id={'tp': lax.rem(self.me + d, self.tp_size)}, device_id_type=MESH)
+        pl.semaphore_wait(barrier, self.tp_size - 1)
+
+    def greet(self):
+        greet(self.ring, self.chip, self.core)
+
+
+class Gather:
+    def __init__(self, at, own, full, sems):
+        self.at, self.own_ref, self.full = at, own, full
+        self.rsend, self.rrecv, self.ssend, self.srecv = sems
+        self.batch, self.n_loc = own.shape[0], own.shape[1]
+        self.hb = self.batch // 2
+
+    def part(self, zz, cc, ch):
+        row = pl.multiple_of((zz * 2 + cc) * self.n_loc, self.n_loc)
+        return self.full.at[pl.ds(ch * self.hb, self.hb), pl.ds(row, self.n_loc), :]
+
+    def own(self, ch):
+        return self.own_ref.at[pl.ds(ch * self.hb, self.hb)]
+
+    def ring_copy(self, way, k, ch, sending):
+        at = self.at
+        sign = -1 if way == UP else 1
+        zb = at.wrap(at.chip + sign * (k - 1 if sending else k))
+        src = self.own(ch) if (sending and k == 1) else self.part(zb, at.core, ch)
         return pltpu.make_async_remote_copy(
-            src_ref=src.at[peer], dst_ref=got.at[d - 1], send_sem=send1.at[d - 1], recv_sem=recv1.at[d - 1],
-            device_id={'tp': peer}, device_id_type=MESH)
-
-    def second(d, sending):
-        peer = lax.rem(me + d, tp_size)
-        slab = me if sending else lax.rem(me + tp_size - d, tp_size)
+            src_ref=src, dst_ref=self.part(zb, at.core, ch),
+            send_sem=self.rsend.at[way, k - 1, ch], recv_sem=self.rrecv.at[way, k - 1, ch],
+            device_id=at.ahead(-sign), device_id_type=MESH)
+
+    def chip_at(self, slot):
+        k = (slot + 1) // 2
+        return self.at.wrap(self.at.chip - k) if slot % 2 else self.at.wrap(self.at.chip + k)
+
+    def sib_copy(self, slot, ch, sending):
+        at = self.at
+        cc = at.core if sending else 1 - at.core
+        zb = self.chip_at(slot)
+        src = self.own(ch) if (sending and slot == 0) else self.part(zb, cc, ch)
         return pltpu.make_async_remote_copy(
-            src_ref=mine, dst_ref=out.at[slab], send_sem=send2.at[d - 1], recv_sem=recv2.at[d - 1],
-            device_id={'tp': peer}, device_id_type=MESH)
-
-    for d in range(1, tp_size):
-        first(d).start()
-    total = src[me]
-    for d in range(1, tp_size):
-        first(d).wait_recv()
-        total = total + got[d - 1]
-    mine[...] = total
-    for d in range(1, tp_size):
-        second(d, True).start()
-    out[me] = total
-    for d in range(1, tp_size):
-        second(d, False).wait_recv()
-    for d in range(1, tp_size):
-        first(d).wait_send()
-        second(d, True).wait_send()
-
-
-def total_call(tp_size, cid, rows):
-    width = rows[0].shape[0]
-    flat = jnp.concatenate(rows)
-    per = -(-flat.shape[0] // (tp_size * 8 * LANES)) * 8
-    padded = jnp.pad(flat, (0, tp_size * per * LANES - flat.shape[0])).reshape(tp_size, per, LANES)
+            src_ref=src, dst_ref=self.part(zb, cc, ch),
+            send_sem=self.ssend.at[slot, ch], recv_sem=self.srecv.at[slot, ch],
+            device_id=at.sibling(), device_id_type=MESH)
+
+    def carries(self, way, k, ch):
+        return k < self.at.half or (k == self.at.half and ch == way)
+
+    def slot_of(self, way, k):
+        half = self.at.half
+        return 2 * half - 1 if k == half else (2 * k - 1 if way == UP else 2 * k)
+
+    def start(self):
+        for way, ch in ((UP, 0), (DOWN, 1), (UP, 1), (DOWN, 0)):
+            self.ring_copy(way, 1, ch, True).start()
+        for ch in (0, 1):
+            self.sib_copy(0, ch, True).start()
+        row = pl.multiple_of(self.at.me * self.n_loc, self.n_loc)
+        self.full[:, pl.ds(row, self.n_loc), :] = self.own_ref[...]
+
+    def arrive(self, way, k, ch):
+        self.ring_copy(way, k, ch, False).wait_recv()
+        if self.carries(way, k + 1, ch):
+            self.ring_copy(way, k + 1, ch, True).start()
+        self.sib_copy(self.slot_of(way, k), ch, True).start()
+
+    def group(self, g):
+        k = g // 2 + 1
+        first, second = ((UP, 0), (DOWN, 1)) if g % 2 == 0 else ((UP, 1), (DOWN, 0))
+        self.arrive(first[0], k, first[1])
+        self.arrive(second[0], k, second[1])
+
+    def groups_before(self, slot):
+        last = self.at.ring - 1
+        return () if slot == last - 1 else ((last - 1,) if slot == last else (slot,))
+
+    def ready(self, slot):
+        for ch in (0, 1):
+            self.sib_copy(slot, ch, False).wait_recv()
+
+    def rows(self, slot):
+        k = (slot + 1) // 2
+        zz = self.at.wrap(self.at.chip + (1 - 2 * lax.rem(slot, 2)) * k)
+        return pl.ds(pl.multiple_of(zz * 2 * self.n_loc, 2 * self.n_loc), 2 * self.n_loc)
+
+    def save_copy(self, dest, sem, slot):
+        rows = self.rows(slot)
+        return pltpu.make_async_copy(self.full.at[:, rows, :], dest.at[:, rows, :], sem.at[slot])
+
+    def finish(self):
+        for way in (UP, DOWN):
+            for k in range(1, self.at.half + 1):
+                for ch in (0, 1):
+                    if self.carries(way, k, ch):
+                        self.ring_copy(way, k, ch, True).wait_send()
+        for slot in range(self.at.ring):
+            for ch in (0, 1):
+                self.sib_copy(slot, ch, True).wait_send()
+
+
+class Scatter:
+    def __init__(self, at, pbuf, sibr, rcv, sems):
+        self.at, self.pbuf, self.sibr, self.rcv = at, pbuf, sibr, rcv
+        self.rsend, self.rrecv, self.ssend, self.srecv = sems
+        self.batch, self.n_loc = sibr.shape[1], sibr.shape[2]
+        self.hb = self.batch // 2
+
+    def slot_of(self, way, s):
+        return 0 if s == 0 else (2 * s - 1 if way == UP else 2 * s)
+
+    def rows(self, slot):
+        at = self.at
+        away = at.half - (slot + 1) // 2
+        zz = at.wrap(at.chip + (2 * lax.rem(slot, 2) - 1) * away)
+        return pl.ds(pl.multiple_of(zz * 2 * self.n_loc, 2 * self.n_loc), 2 * self.n_loc)
+
+    def put(self, slot, value):
+        self.pbuf[slot] = value.astype(BF16).reshape(self.batch, 2 * self.n_loc, value.shape[-1])
+        self.sib_copy(slot).start()
+
+    def ring_copy(self, way, s, ch):
+        part = pl.ds(ch * self.hb, self.hb)
+        return pltpu.make_async_remote_copy(
+            src_ref=self.sibr.at[self.slot_of(way, s), part], dst_ref=self.rcv.at[way, s, part],
+            send_sem=self.rsend.at[way, s, ch], recv_sem=self.rrecv.at[way, s, ch],
+            device_id=self.at.ahead(1 if way == UP else -1), device_id_type=MESH)
+
+    def sib_copy(self, slot):
+        rows = pl.ds(pl.multiple_of((1 - self.at.core) * self.n_loc, self.n_loc), self.n_loc)
+        return pltpu.make_async_remote_copy(
+            src_ref=self.pbuf.at[slot, :, rows, :], dst_ref=self.sibr.at[slot],
+            send_sem=self.ssend.at[slot], recv_sem=self.srecv.at[slot],
+            device_id=self.at.sibling(), device_id_type=MESH)
+
+    def own_sum(self, slot, part):
+        rows = pl.ds(pl.multiple_of(self.at.core * self.n_loc, self.n_loc), self.n_loc)
+        return self.pbuf[slot, part, rows, :].astype(F32) + self.sibr[slot, part].astype(F32)
+
+    def starts_at(self, way, ch):
+        return 0 if ch == way else 1
+
+    def pass_on(self, way, s, ch):
+        slot, part = self.slot_of(way, s), pl.ds(ch * self.hb, self.hb)
+        total = self.own_sum(slot, part)
+        if s > self.starts_at(way, ch):
+            self.ring_copy(way, s - 1, ch).wait_recv()
+            total = total + self.rcv[way, s - 1, part].astype(F32)
+        self.sibr[slot, part] = total.astype(BF16)
+        self.ring_copy(way, s, ch).start()
+
+    def step(self, s):
+        if s == 0:
+            self.sib_copy(0).wait_recv()
+            self.pass_on(UP, 0, 0)
+            self.pass_on(DOWN, 0, 1)
+            return
+        self.sib_copy(2 * s - 1).wait_recv()
+        self.pass_on(UP, s, 1)
+        self.sib_copy(2 * s).wait_recv()
+        self.pass_on(DOWN, s, 0)
+        self.pass_on(UP, s, 0)
+        self.pass_on(DOWN, s, 1)
+
+    def final(self, use):
+        last = self.at.ring - 1
+        self.sib_copy(last).wait_recv()
+        for ch, order in ((1, (UP, DOWN)), (0, (DOWN, UP))):
+            part = pl.ds(ch * self.hb, self.hb)
+            total = self.own_sum(last, part)
+            for way in order:
+                self.ring_copy(way, self.at.half - 1, ch).wait_recv()
+                total = total + self.rcv[way, self.at.half - 1, part].astype(F32)
+            use(part, total)
+
+    def finish(self):
+        for way in (UP, DOWN):
+            for s in range(self.at.half):
+                for ch in (0, 1):
+                    if s >= self.starts_at(way, ch):
+                        self.ring_copy(way, s, ch).wait_send()
+        for slot in range(self.at.ring):
+            self.sib_copy(slot).wait_send()
+
+
+def loop_slots(n, hooks, body):
+    def step(slot, carry):
+        for s in range(n):
+            @pl.when(slot == s)
+            def _():
+                hooks(s)
+        body(slot)
+        return carry
+    lax.fori_loop(0, n, step, None)
+
+
+def gather_sems(tp_size):
+    ring, half = tp_size // 2, tp_size // 4
+    return [pltpu.SemaphoreType.DMA(s) for s in ((2, half, 2), (2, half, 2), (ring, 2), (ring, 2))]
+
+
+def scatter_sems(tp_size):
+    ring, half = tp_size // 2, tp_size // 4
+    return [pltpu.SemaphoreType.DMA(s) for s in ((2, half, 2), (2, half, 2), (ring,), (ring,))]
+
+
+def pad_rows(dest, source, head_dim):
+    parts = source.shape[0] // head_dim
+    head_pad = dest.shape[0] // parts
+    width = dest.shape[1]
+    for i in range(parts):
+        dest[i * head_pad:i * head_pad + head_dim, :] = source[i * head_dim:(i + 1) * head_dim, :]
+        dest[i * head_pad + head_dim:(i + 1) * head_pad, :] = jnp.zeros((head_pad - head_dim, width), dest.dtype)
+
+
+def mod_row(t_ref, table_ref, i):
+    width = table_ref.shape[1]
+    return table_ref[i:i + 1, :].astype(F32) + t_ref[:, i * width:(i + 1) * width].astype(F32)
+
+
+def softmax_of(scores):
+    top = jnp.max(scores, axis=-1, keepdims=True)
+    powers = jnp.exp(scores - top)
+    return powers * (1.0 / jnp.sum(powers, axis=-1, keepdims=True))
+
+
+def forward_body(tp_size, head_dim, *refs):
+    at = Place(tp_size)
+    ins, refs = refs[:15], refs[15:]
+    x, y, t_emb, table, lens, wqkv_in, bqkv, wkv_in, bkv, wq_in, bq, wo_in, bo, wco_in, bco = ins
+    outs, refs = refs[:12], refs[12:]
+    h1_out, y_out, x1_out = outs[:3]
+    scratch, refs = refs[:9], refs[9:]
+    qkv, kv, q_c, val, cval, prob, cprob, atot, x2 = scratch
+    h1, x1, mod, fh, fy, fx, pbuf, sibr1, rcv1, sibr2, rcv2, wqkv, wkv, wq, wo, wco = refs[:16]
+    sems = refs[16:]
+    gather_h = Gather(at, h1, fh, sems[0:4])
+    gather_y = Gather(at, y, fy, sems[4:8])
+    gather_x = Gather(at, x1, fx, sems[8:12])
+    scat_o = Scatter(at, pbuf, sibr1, rcv1, sems[12:16])
+    scat_c = Scatter(at, pbuf, sibr2, rcv2, sems[16:20])
+    save_sem, out_sem = sems[20], sems[21]
+    batch = x.shape[0]
+    head_pad = wq.shape[0]
+    scale = head_dim ** -0.5
+
+    def out_copy(i):
+        return pltpu.make_async_copy(scratch[i], outs[3 + i], out_sem.at[i])
+
+    for i in range(3):
+        mod[i] = mod_row(t_emb, table, i)
+
+    def norm_one(b, carry):
+        rows = x[b].astype(F32)
+        centered = rows - jnp.mean(rows, axis=-1, keepdims=True)
+        normed = centered * lax.rsqrt(jnp.mean(centered * centered, axis=-1, keepdims=True) + LN_EPS)
+        h1[b] = (normed * (1.0 + mod[1, pl.ds(b, 1), :]) + mod[0, pl.ds(b, 1), :]).astype(BF16)
+        return carry
+
+    lax.fori_loop(0, batch, norm_one, None)
+    at.greet()
+    gather_h.start()
+    for dest, source in ((wqkv, wqkv_in), (wkv, wkv_in), (wq, wq_in), (wo, wo_in), (wco, wco_in)):
+        pad_rows(dest, source, head_dim)
+
+    def hooks(s):
+        for g in gather_h.groups_before(s):
+            gather_h.group(g)
+        gather_h.ready(s)
+        if s == at.ring - 4:
+            gather_y.start()
+
+    def project(slot):
+        rows = gather_h.rows(slot)
+        gather_h.save_copy(h1_out, save_sem.at[0], slot).start()
+        put_rows(qkv, rows, dot(rows_of(fh, rows), wqkv[...], NT) + bqkv[...])
+
+    loop_slots(at.ring, hooks, project)
+
+    def hooks(b):
+        if b == batch // 2:
+            gather_y.group(0)
+        if b == batch - 1:
+            gather_y.group(1)
+
+    def attend_self(b):
+        q_b, k_b, v_b = [qkv[b, :, i * head_pad:(i + 1) * head_pad] for i in range(3)]
+        p_b = softmax_of(dot(q_b, k_b, NT) * scale).astype(BF16)
+        prob[b] = p_b
+        val[b] = dot(p_b, v_b).astype(BF16)
+
+    loop_slots(batch, hooks, attend_self)
+    for i in (0, 3, 5):
+        out_copy(i).start()
+
+    ynext = {2: 2, 3: 3, 5: 4, 6: 5, 7: 6}
+
+    def hooks(s):
+        if s >= 2 and s % 2 == 0:
+            scat_o.step(s // 2 - 1)
+        if s in ynext:
+            gather_y.group(ynext[s])
+
+    def project_o(slot):
+        scat_o.put(slot, dot(rows_of(val, scat_o.rows(slot)), wo[...]))
+
+    loop_slots(at.ring, hooks, project_o)
+    scat_o.step(at.half - 1)
+
+    def take_o(part, total):
+        atot[part] = total + bo[...].astype(F32)
+
+    scat_o.final(take_o)
+    out_copy(7).start()
+
+    def x1_one(b, carry):
+        x1[b] = (x[b].astype(F32) + mod[2, pl.ds(b, 1), :] * atot[b]).astype(BF16)
+        return carry
+
+    lax.fori_loop(0, batch, x1_one, None)
+
+    gather_x.start()
+
+    def hooks(s):
+        for g in gather_x.groups_before(s):
+            gather_x.group(g)
+        gather_y.ready(s)
+        gather_x.ready(s)
+
+    def project(slot):
+        rows = gather_x.rows(slot)
+        gather_y.save_copy(y_out, save_sem.at[1], slot).start()
+        gather_x.save_copy(x1_out, save_sem.at[2], slot).start()
+        put_rows(kv, rows, dot(rows_of(fy, rows), wkv[...], NT) + bkv[...])
+        put_rows(q_c, rows, dot(rows_of(fx, rows), wq[...], NT) + bq[...])
+
+    loop_slots(at.ring, hooks, project)
+    scat_o.finish()
+
+    def attend_cross(b, carry):
+        k_b, v_b = [kv[b, :, i * head_pad:(i + 1) * head_pad] for i in range(2)]
+        scores = dot(q_c[b], k_b, NT) * scale
+        slots = lax.broadcasted_iota(jnp.int32, scores.shape, 1)
+        p_b = softmax_of(jnp.where(slots < lens[b], scores, MASK_FILL)).astype(BF16)
+        cprob[b] = p_b
+        cval[b] = dot(p_b, v_b).astype(BF16)
+        return carry
+
+    lax.fori_loop(0, batch, attend_cross, None)
+    for i in (1, 2, 4, 6):
+        out_copy(i).start()
+
+    def hooks(s):
+        if s >= 2 and s % 2 == 0:
+            scat_c.step(s // 2 - 1)
+
+    def project_c(slot):
+        scat_c.put(slot, dot(rows_of(cval, scat_c.rows(slot)), wco[...]))
+
+    loop_slots(at.ring, hooks, project_c)
+    scat_c.step(at.half - 1)
+
+    def take_c(part, total):
+        x2[part] = (x1[part].astype(F32) + total + bco[...].astype(F32)).astype(BF16)
+
+    scat_c.final(take_c)
+    out_copy(8).start()
+    for stream in (gather_h, gather_y, gather_x, scat_c):
+        stream.finish()
+    for slot in range(at.ring):
+        gather_h.save_copy(h1_out, save_sem.at[0], slot).wait()
+        gather_y.save_copy(y_out, save_sem.at[1], slot).wait()
+        gather_x.save_copy(x1_out, save_sem.at[2], slot).wait()
+    for i in range(9):
+        out_copy(i).wait()
+
+
+def forward_call(tp_size, cid, head_dim, head_pad, *ins):
+    batch, n_loc, width = ins[0].shape
+    n_tok = n_loc * tp_size
+    ring, half = tp_size // 2, tp_size // 4
+    tokens = lambda last: (batch, n_tok, last)
+    local = (batch, n_loc, width)
+    kept = [(tokens(3 * head_pad), BF16), (tokens(2 * head_pad), BF16), (tokens(head_pad), BF16), (tokens(head_pad), BF16),
+            (tokens(head_pad), BF16), (tokens(n_tok), BF16), (tokens(n_tok), BF16), (local, F32), (local, BF16)]
     vmem = pl.BlockSpec(memory_space=pltpu.VMEM)
-    out = pl.pallas_call(
-        functools.partial(total_body, tp_size),
-        out_shape=jax.ShapeDtypeStruct(padded.shape, F32),
-        in_specs=[vmem],
-        out_specs=vmem,
-        scratch_shapes=[
-            pltpu.VMEM((tp_size - 1, per, LANES), F32),
-            pltpu.VMEM((per, LANES), F32),
-        ] + [pltpu.SemaphoreType.DMA((tp_size - 1,))] * 4,
-        compiler_params=pltpu.CompilerParams(collective_id=cid, has_side_effects=True),
-        name='small_total',
-    )(padded)
-    flat = out.reshape(-1)
-    return [flat[i * width:(i + 1) * width] for i in range(len(rows))]
+    sib, rcv = (ring, *local), (2, half, *local)
+    return pl.pallas_call(
+        functools.partial(forward_body, tp_size, head_dim),
+        out_shape=[jax.ShapeDtypeStruct(tokens(width), BF16)] * 3 + [jax.ShapeDtypeStruct(*k) for k in kept],
+        in_specs=[vmem] * len(ins),
+        out_specs=[pl.BlockSpec(memory_space=pl.ANY)] * (3 + len(kept)),
+        scratch_shapes=[pltpu.VMEM(*k) for k in kept] + [
+            pltpu.VMEM(local, BF16), pltpu.VMEM(local, BF16), pltpu.VMEM((3, batch, width), F32),
+            pltpu.VMEM(tokens(width), BF16), pltpu.VMEM(tokens(width), BF16), pltpu.VMEM(tokens(width), BF16),
+            pltpu.VMEM((ring, batch, 2 * n_loc, width), BF16),
+            pltpu.VMEM(sib, BF16), pltpu.VMEM(rcv, BF16), pltpu.VMEM(sib, BF16), pltpu.VMEM(rcv, BF16)]
+        + [pltpu.VMEM((n * head_pad, width), BF16) for n in (3, 2, 1, 1, 1)]
+        + gather_sems(tp_size) * 3 + scatter_sems(tp_size) * 2
+        + [pltpu.SemaphoreType.DMA((3, ring)), pltpu.SemaphoreType.DMA((len(kept),))],
+        compiler_params=pltpu.CompilerParams(collective_id=cid, has_side_effects=True, vmem_limit_bytes=VMEM_LIMIT),
+        name='attention_forward',
+    )(*ins)
+
+
+class RowFeed:
+    def __init__(self, source, buf, sem, rows):
+        self.source, self.buf, self.sem, self.rows = source, buf, sem, rows
+
+    def copy(self, slot):
+        side = lax.rem(slot, 2)
+        return pltpu.make_async_copy(self.source.at[:, self.rows(slot), :], self.buf.at[side], self.sem.at[side])
+
+    def take(self, slot, n):
+        @pl.when(slot + 1 < n)
+        def _():
+            self.copy(slot + 1).start()
+        self.copy(slot).wait()
+        block = self.buf[lax.rem(slot, 2)]
+        return block.reshape(block.shape[0] * block.shape[1], block.shape[2])
+
+
+def small_total(at, src, got, mine, out, sems):
+    send1, recv1, send2, recv2 = sems
+    tiles = src.shape[1] // LANES
+
+    def lanes(i):
+        return pl.ds(i * LANES, LANES)
+
+    def first(tile, peer_slot):
+        return pltpu.make_async_remote_copy(
+            src_ref=src.at[:, lanes(tile)], dst_ref=got.at[peer_slot], send_sem=send1.at[tile], recv_sem=recv1.at[peer_slot],
+            device_id={'tp': tile}, device_id_type=MESH)
+
+    def second(tile, d):
+        return pltpu.make_async_remote_copy(
+            src_ref=mine, dst_ref=out.at[:, lanes(tile)], send_sem=send2.at[d - 1], recv_sem=recv2.at[tile],
+            device_id={'tp': lax.rem(at.me + d, at.tp_size)}, device_id_type=MESH)
+
+    for tile in range(tiles):
+        @pl.when(at.me != tile)
+        def _():
+            first(tile, lax.rem(at.me - tile + at.tp_size, at.tp_size) - 1).start()
+    for tile in range(tiles):
+        @pl.when(at.me == tile)
+        def _():
+            total = src[:, tile * LANES:(tile + 1) * LANES]
+            for d in range(1, at.tp_size):
+                first(tile, d - 1).wait_recv()
+                total = total + got[d - 1]
+            mine[...] = total
+            for d in range(1, at.tp_size):
+                second(tile, d).start()
+            out[:, tile * LANES:(tile + 1) * LANES] = total
+            for d in range(1, at.tp_size):
+                second(tile, d).wait_send()
+    for tile in range(tiles):
+        @pl.when(at.me != tile)
+        def _():
+            second(tile, 1).wait_recv()
+            first(tile, 0).wait_send()
+
+
+def backward_body(tp_size, head_dim, *refs):
+    at = Place(tp_size)
+    ins, refs = refs[:12], refs[12:]
+    g_cross, g_x2, x, atot, t_emb, table, wqkv_in, wkv_in, wq_in, wo_in, wco_in, sums_in = ins
+    loads, refs = refs[:7], refs[7:]
+    feeds, refs = refs[:3], refs[3:]
+    outs, refs = refs[:11], refs[11:]
+    g_x, g_y, sums_out, gw_qkv, gw_kv, gw_q, gw_o, gw_co, gb_qkv, gb_kv, gb_q = outs
+    held, refs = refs[:7], refs[7:]
+    qkv, kv, q_c, val, cval, prob, cprob = held
+    full, pbuf, sibr1, rcv1, pbufy, sibr2, rcv2, wqkv, wkv, wq, wo, wco = refs[:12]
+    g_val, g_qkv, g_kv, g_q, g_x1, g_h1, g_attn, mod, sums, got, mine, feed_a, feed_y = refs[12:25]
+    sems = refs[25:]
+    gather_c = Gather(at, g_cross, full, sems[0:4])
+    gather_a = Gather(at, g_attn, full, sems[4:8])
+    scat_q = Scatter(at, pbuf, sibr1, rcv1, sems[8:12])
+    scat_y = Scatter(at, pbufy, sibr2, rcv2, sems[12:16])
+    scat_h = Scatter(at, pbuf, sibr1, rcv1, sems[16:20])
+    load_sem, feed_sem = sems[20], sems[21]
+    feed_h = RowFeed(feeds[0], feed_a, feed_sem.at[0], scat_h.rows)
+    feed_x = RowFeed(feeds[1], feed_a, feed_sem.at[1], scat_q.rows)
+    feed_yy = RowFeed(feeds[2], feed_y, feed_sem.at[2], scat_y.rows)
+    batch, n_loc, width = x.shape
+    ring, half = at.ring, at.half
+    head_pad = wq.shape[0]
+    scale = head_dim ** -0.5
+
+    def load_copy(i):
+        return pltpu.make_async_copy(loads[i], held[i], load_sem.at[i])
+
+    for i in range(7):
+        load_copy(i).start()
+    at.greet_all()
+    gather_c.start()
+    feed_x.copy(0).start()
+    feed_yy.copy(0).start()
+    for i in range(3):
+        mod[i] = mod_row(t_emb, table, i)
+    for dest, source in ((wqkv, wqkv_in), (wkv, wkv_in), (wq, wq_in), (wo, wo_in), (wco, wco_in)):
+        pad_rows(dest, source, head_dim)
+    sums[...] = sums_in[...]
+    for acc in outs[3:]:
+        acc[...] = jnp.zeros_like(acc)
+    for i in range(7):
+        load_copy(i).wait()
+
+    def out_back(gather, value, weight, acc):
+        def body(slot):
+            rows = gather.rows(slot)
+            block = rows_of(full, rows)
+            put_rows(g_val, rows, dot(block, weight[...], NT))
+            acc[...] += dot(rows_of(value, rows), block, TN)
+        return body
+
+    def hooks(s):
+        for g in gather_c.groups_before(s):
+            gather_c.group(g)
+        gather_c.ready(s)
+
+    loop_slots(ring, hooks, out_back(gather_c, cval, wco, gw_co))
+    gather_c.finish()
+
+    def back_one(q_b, k_b, v_b, p_b, g_b):
+        g_p = dot(g_b, v_b, NT)
+        p_f = p_b.astype(F32)
+        row_dot = jnp.sum(g_p * p_f, axis=-1, keepdims=True)
+        g_s = (p_f * (g_p - row_dot) * scale).astype(BF16)
+        return dot(g_s, k_b).astype(BF16), dot(g_s, q_b, TN).astype(BF16), dot(p_b, g_b, TN).astype(BF16)
+
+    def cross_back(b, carry):
+        parts = back_one(q_c[b], kv[b, :, :head_pad], kv[b, :, head_pad:], cprob[b], g_val[b])
+        g_q[b] = parts[0]
+        g_kv[b, :, :head_pad] = parts[1]
+        g_kv[b, :, head_pad:] = parts[2]
+        return carry
+
+    lax.fori_loop(0, batch, cross_back, None)
+
+    def hooks(s):
+        if s >= 2 and s % 2 == 0:
+            scat_q.step(s // 2 - 1)
+
+    def put_q(slot):
+        block = rows_of(g_q, scat_q.rows(slot))
+        scat_q.put(slot, dot(block, wq[...]))
+        gw_q[...] += dot(block, feed_x.take(slot, ring), TN)
+        gb_q[...] += row_sum(block.astype(F32))
+
+    def put_y(first, last):
+        def body(slot, carry):
+            block = rows_of(g_kv, scat_y.rows(slot))
+            scat_y.put(slot, dot(block, wkv[...]))
+            gw_kv[...] += dot(block, feed_yy.take(slot, ring), TN)
+            gb_kv[...] += row_sum(block.astype(F32))
+            return carry
+        lax.fori_loop(first, last, body, None)
+
+    loop_slots(ring, hooks, put_q)
+    scat_q.step(half - 1)
+    put_y(0, 3)
+    scat_y.step(0)
+
+    def take_q(part, total):
+        g_x1[part] = g_x2[part] + total
+
+    scat_q.final(take_q)
+    feed_h.copy(0).start()
+
+    def x1_back(b, carry):
+        gate_sum, bias_sum = carry
+        rows = g_x1[b]
+        block = (rows * mod[2, pl.ds(b, 1), :]).astype(BF16)
+        g_attn[b] = block
+        return gate_sum + row_sum(rows * atot[b]), bias_sum + row_sum(block.astype(F32))
+
+    zero = jnp.zeros((1, width), F32)
+    gate_sum, bias_sum = lax.fori_loop(0, batch, x1_back, (zero, zero))
+    sums[2:3, :] = gate_sum
+    sums[6:7, :] = bias_sum
+
+    scat_q.finish()
+    gather_a.start()
+
+    def hooks(s):
+        for g in gather_a.groups_before(s):
+            gather_a.group(g)
+        if s == 1:
+            put_y(3, 5)
+            scat_y.step(1)
+        if s == 5:
+            put_y(5, ring)
+            scat_y.step(2)
+        gather_a.ready(s)
+
+    loop_slots(ring, hooks, out_back(gather_a, val, wo, gw_o))
+
+    def hooks(b):
+        if b == batch // 4:
+            scat_y.step(half - 1)
+
+    def self_back(b):
+        parts = back_one(*[qkv[b, :, i * head_pad:(i + 1) * head_pad] for i in range(3)], prob[b], g_val[b])
+        for i in range(3):
+            g_qkv[b, :, i * head_pad:(i + 1) * head_pad] = parts[i]
+
+    loop_slots(batch, hooks, self_back)
+
+    def take_y(part, total):
+        g_y[part] = total.astype(BF16)
+
+    def hooks(s):
+        if s >= 2 and s % 2 == 0:
+            scat_h.step(s // 2 - 1)
+        if s == 5:
+            scat_y.final(take_y)
+
+    def put_h(slot):
+        block = rows_of(g_qkv, scat_h.rows(slot))
+        scat_h.put(slot, dot(block, wqkv[...]))
+        gw_qkv[...] += dot(block, feed_h.take(slot, ring), TN)
+        gb_qkv[...] += row_sum(block.astype(F32))
+
+    loop_slots(ring, hooks, put_h)
+    scat_h.step(half - 1)
+    def take_h(part, total):
+        g_h1[part] = total
+
+    scat_h.final(take_h)
+
+    def x_back(b, carry):
+        shift_sum, scale_sum = carry
+        rows = x[b].astype(F32)
+        centered = rows - jnp.mean(rows, axis=-1, keepdims=True)
+        inv_std = lax.rsqrt(jnp.mean(centered * centered, axis=-1, keepdims=True) + LN_EPS)
+        normed = centered * inv_std
+        grad = g_h1[b]
+        g_normed = grad * (1.0 + mod[1, pl.ds(b, 1), :])
+        mean_g = jnp.mean(g_normed, axis=-1, keepdims=True)
+        mean_gn = jnp.mean(g_normed * normed, axis=-1, keepdims=True)
+        g_x[b] = (g_x1[b] + inv_std * (g_normed - mean_g - normed * mean_gn)).astype(BF16)
+        return shift_sum + row_sum(grad), scale_sum + row_sum(grad * normed)
+
+    shift_sum, scale_sum = lax.fori_loop(0, batch, x_back, (zero, zero))
+    sums[0:1, :] = shift_sum
+    sums[1:2, :] = scale_sum
+    small_total(at, sums, got, mine, sums_out, sems[22:26])
+    for stream in (gather_a, scat_y, scat_h):
+        stream.finish()
+
+
+def backward_call(tp_size, cid, head_dim, head_pad, ins, loads, feeds):
+    batch, n_loc, width = ins[0].shape
+    n_tok = n_loc * tp_size
+    ring, half = tp_size // 2, tp_size // 4
+    n_sum = ins[-1].shape[0]
+    tokens = lambda last: (batch, n_tok, last)
+    local = (batch, n_loc, width)
+    vmem, anywhere = pl.BlockSpec(memory_space=pltpu.VMEM), pl.BlockSpec(memory_space=pl.ANY)
+    sib, rcv, pbuf = (ring, *local), (2, half, *local), (ring, batch, 2 * n_loc, width)
+    outs = [(local, BF16), (local, BF16), ((n_sum, width), F32)]
+    outs += [((n * head_pad, width), F32) for n in (3, 2, 1, 1, 1)] + [((1, n * head_pad), F32) for n in (3, 2, 1)]
+    return pl.pallas_call(
+        functools.partial(backward_body, tp_size, head_dim),
+        out_shape=[jax.ShapeDtypeStruct(*o) for o in outs],
+        in_specs=[vmem] * len(ins) + [anywhere] * (len(loads) + len(feeds)),
+        out_specs=[vmem] * len(outs),
+        scratch_shapes=[pltpu.VMEM(a.shape, a.dtype) for a in loads]
+        + [pltpu.VMEM(s, BF16) for s in (tokens(width), pbuf, sib, rcv, pbuf, sib, rcv)]
+        + [pltpu.VMEM((n * head_pad, width), BF16) for n in (3, 2, 1, 1, 1)]
+        + [pltpu.VMEM(tokens(n * head_pad), BF16) for n in (1, 3, 2, 1)]
+        + [pltpu.VMEM(local, F32), pltpu.VMEM(local, F32), pltpu.VMEM(local, BF16), pltpu.VMEM((3, batch, width), F32), pltpu.VMEM((n_sum, width), F32),
+           pltpu.VMEM((tp_size - 1, n_sum, LANES), F32), pltpu.VMEM((n_sum, LANES), F32)]
+        + [pltpu.VMEM((2, batch, 2 * n_loc, width), BF16)] * 2
+        + gather_sems(tp_size) * 2 + scatter_sems(tp_size) * 3
+        + [pltpu.SemaphoreType.DMA((len(loads),)), pltpu.SemaphoreType.DMA((3, 2))]
+        + [pltpu.SemaphoreType.DMA((n,)) for n in (width // LANES, tp_size - 1, tp_size - 1, width // LANES)],
+        compiler_params=pltpu.CompilerParams(collective_id=cid, has_side_effects=True, vmem_limit_bytes=VMEM_LIMIT),
+        name='attention_backward',
+    )(*ins, *loads, *feeds)
 
 
 def layer_norm(tensor):
@@ -380,35 +1023,6 @@
     mean_g = jnp.mean(g_normed, axis=-1, keepdims=True)
     mean_gn = jnp.mean(g_normed * normed, axis=-1, keepdims=True)
     return inv_std * (g_normed - mean_g - normed * mean_gn)
-
-
-def product(form, lhs, rhs):
-    return jnp.einsum(form, lhs, rhs, preferred_element_type=F32)
-
-
-def attend(q_all, k_all, v_all, key_ok, scale):
-    scores = product('bqe,bke->bqk', q_all, k_all) * scale
-    if key_ok is not None:
-        scores = jnp.where(key_ok[:, None, :], scores, MASK_FILL)
-    prob_bf = jax.nn.softmax(scores, axis=-1).astype(BF16)
-    return product('bqk,bke->bqe', prob_bf, v_all).astype(BF16), prob_bf
-
-
-def attend_back(q_all, k_all, v_all, prob_bf, g_val, scale):
-    g_v = product('bqk,bqe->bke', prob_bf, g_val)
-    g_prob = product('bqe,bke->bqk', g_val, v_all)
-    row_dot = jnp.sum(g_prob * prob_bf, axis=-1, keepdims=True)
-    g_scores = (prob_bf * (g_prob - row_dot) * scale).astype(BF16)
-    g_q = product('bqk,bke->bqe', g_scores, k_all)
-    g_k = product('bqk,bqe->bke', g_scores, q_all)
-    return g_q.astype(BF16), g_k.astype(BF16), g_v.astype(BF16)
-
-
-def pad_heads(weight, n_part, head_dim, head_pad):
-    lead = weight.shape[:-1]
-    weight = weight.reshape(*lead, n_part, head_dim)
-    weight = jnp.pad(weight, [(0, 0)] * (len(lead) + 1) + [(0, head_pad - head_dim)])
-    return weight.reshape(*lead, n_part * head_pad)
 
 
 def drop_pad(grad, n_part, head_dim, head_pad):
@@ -447,50 +1061,21 @@
     n_tok = n_loc * tp_size
     head_dim, ffn = w_q.shape[2], w_1.shape[1]
     head_pad = -(-head_dim // LANES) * LANES
-    scale = head_dim ** -0.5
-    mod_rows = mod_table.astype(F32)[None] + t_loc.astype(F32).reshape(batch, 6, width)
-    shift1, scale1, gate1, shift2, scale2, gate2 = [mod_rows[:, i, None, :] for i in range(6)]
-
-    wqkv = pad_heads(w_qkv[:, 0], 3, head_dim, head_pad)
-    wkv = pad_heads(w_kv[:, 0], 2, head_dim, head_pad)
-    wq = pad_heads(w_q[:, 0], 1, head_dim, head_pad)
-    bqkv = pad_heads(b_qkv.astype(F32), 3, head_dim, head_pad)
-    bkv = pad_heads(b_kv.astype(F32), 2, head_dim, head_pad)
-    bq = pad_heads(b_q.astype(F32), 1, head_dim, head_pad)
-    wo = jnp.pad(w_o[0], ((0, head_pad - head_dim), (0, 0)))
-    wco = jnp.pad(w_co[0], ((0, head_pad - head_dim), (0, 0)))
+    mod_rows = mod_table[3:].astype(F32)[None] + t_loc[:, 3 * width:].astype(F32).reshape(batch, 3, width)
+    shift2, scale2, gate2 = [mod_rows[:, i, None, :] for i in range(3)]
+
+    wqkv, wq, wkv = [w.transpose(1, 2, 0)[0] for w in (w_qkv, w_q, w_kv)]
+    wo, wco = w_o[0], w_co[0]
+
+    def pad_bias(bias):
+        bias = bias.astype(F32).reshape(-1, head_dim)
+        return jnp.pad(bias, ((0, 0), (0, head_pad - head_dim))).reshape(1, -1)
+
     b1 = b_1.astype(F32)[None]
-
-    normed1, inv_std1 = layer_norm(x_loc)
-    h1_loc = (normed1 * (1.0 + scale1) + shift1).astype(BF16)
-
-    def project_both(rows, get, ins, outs):
-        put_rows(outs[0], rows, dot(get(0), ins[0][...]) + ins[1][...])
-        put_rows(outs[1], rows, dot(get(1), ins[2][...]) + ins[3][...])
-
-    h1_all, y_all, qkv, kv = gather_call(
-        tp_size, 0, 'gather_h1_y', [h1_loc, y_loc], [wqkv, bqkv, wkv, bkv], (0, 1),
-        [(batch, n_tok, 3 * head_pad), (batch, n_tok, 2 * head_pad)], [], project_both)
-    q_self, k_self, v_self = [qkv[..., i * head_pad:(i + 1) * head_pad] for i in range(3)]
-    k_cross, v_cross = [kv[..., i * head_pad:(i + 1) * head_pad] for i in range(2)]
-    attn_val, attn_prob = attend(q_self, k_self, v_self, None, scale)
-
-    def project_out(rows, put, ins, held, accs):
-        put(0, dot(rows_of(ins[0], rows), ins[1][...]))
-
-    attn_total, = scatter_call(tp_size, 1, 'scatter_o', n_loc, width, 1, [attn_val, wo], [], [], project_out)
-    attn_total = attn_total + b_o
-    x1_loc = (x_loc + gate1 * attn_total).astype(BF16)
-
-    def project_q(rows, get, ins, outs):
-        put_rows(outs[0], rows, dot(get(0), ins[0][...]) + ins[1][...])
-
-    x1_all, q_cross = gather_call(tp_size, 2, 'gather_x1', [x1_loc], [wq, bq], (0,), [(batch, n_tok, head_pad)], [], project_q)
-    slot_ok = lax.broadcasted_iota(jnp.int32, (batch, n_tok), 1) < len_loc[:, None]
-    cross_val, cross_prob = attend(q_cross, k_cross, v_cross, slot_ok, scale)
-    cross_total, = scatter_call(tp_size, 3, 'scatter_co', n_loc, width, 1, [cross_val, wco], [], [], project_out)
-    cross_total = cross_total + b_co
-    x2_loc = (x1_loc + cross_total).astype(BF16)
+    lens = jnp.broadcast_to(len_loc[:, None, None], (batch, 1, n_tok))
+    h1_all, y_all, x1_all, qkv, kv, q_cross, attn_val, cross_val, attn_prob, cross_prob, attn_total, x2_loc = forward_call(
+        tp_size, 0, head_dim, head_pad, x_loc, y_loc, t_loc, mod_table, lens, wqkv, pad_bias(b_qkv), wkv, pad_bias(b_kv),
+        wq, pad_bias(b_q), wo, b_o[None], wco, b_co[None])
 
     normed2, inv_std2 = layer_norm(x2_loc)
     h2_loc = (normed2 * (1.0 + scale2) + shift2).astype(BF16)
@@ -513,7 +1098,7 @@
         acc_w2[...] += dot(act, g_blk, TN)
 
     gelu_out, g_hid, g_w_1, g_w_2, g_b_1 = gather_call(
-        tp_size, 4, 'gather_h2_g', [h2_loc, g_mlp_loc], [w_1, b1, w_2], (),
+        tp_size, 1, 'gather_h2_g', [h2_loc, g_mlp_loc], [w_1, b1, w_2], (),
         [(batch, n_tok, ffn), (batch, n_tok, ffn)], [(ffn, width), (ffn, width), (1, ffn)], mlp)
 
     def mlp_out(rows, put, ins, held, accs):
@@ -521,7 +1106,7 @@
         put(0, dot(rows_of(g_hid, rows), w1[...], NT))
         put(1, dot(rows_of(act, rows), w2[...]))
 
-    both, = scatter_call(tp_size, 5, 'scatter_h2_out', n_loc, width, 2, [g_hid, gelu_out, w_1, w_2], [], [], mlp_out)
+    both, = scatter_call(tp_size, 2, 'scatter_h2_out', n_loc, width, 2, [g_hid, gelu_out, w_1, w_2], [], [], mlp_out)
     g_h2, mlp_total = both[:batch], both[batch:] + b_2
     x_out = (x2_loc + gate2 * mlp_total).astype(BF16)
     g_gate2 = jnp.sum(g_x2 * mlp_total, axis=(0, 1))
@@ -529,69 +1114,27 @@
     g_shift2 = token_sum(g_h2)
     g_scale2 = token_sum(g_h2 * normed2)
     g_x2 = g_x2 + layer_norm_back(normed2, inv_std2, g_h2 * (1.0 + scale2))
-
-    def out_back(rows, get, ins, outs):
-        val, weight = ins
-        g_val, acc_w = outs
-        g_blk = get(0)
-        put_rows(g_val, rows, dot(g_blk, weight[...], NT))
-        acc_w[...] += dot(rows_of(val, rows), g_blk, TN)
-
     g_cross_loc = g_x2.astype(BF16)
     g_b_co = token_sum(g_cross_loc)
-    g_cross_val, g_w_co = gather_call(
-        tp_size, 6, 'gather_g_cross', [g_cross_loc], [cross_val, wco], (), [(batch, n_tok, head_pad)], [(head_pad, width)], out_back)
-    g_q_cross, g_k_cross, g_v_cross = attend_back(q_cross, k_cross, v_cross, cross_prob, g_cross_val, scale)
-    g_kv = jnp.concatenate([g_k_cross, g_v_cross], axis=-1)
-
-    def cross_in_back(rows, put, ins, held, accs):
-        g_q, g_kv, wq, wkv = ins
-        g_q_blk, g_kv_blk = rows_of(g_q, rows), rows_of(g_kv, rows)
-        put(0, dot(g_q_blk, wq[...], NT))
-        put(1, dot(g_kv_blk, wkv[...], NT))
-        accs[0][...] += dot(g_q_blk, rows_of(held[0], rows), TN)
-        accs[1][...] += dot(g_kv_blk, rows_of(held[1], rows), TN)
-        accs[2][...] += row_sum(g_q_blk.astype(F32))
-        accs[3][...] += row_sum(g_kv_blk.astype(F32))
-
-    both, g_w_q, g_w_kv, g_b_q, g_b_kv = scatter_call(
-        tp_size, 7, 'scatter_q_kv', n_loc, width, 2, [g_q_cross, g_kv, wq, wkv], [x1_all, y_all],
-        [(head_pad, width), (2 * head_pad, width), (1, head_pad), (1, 2 * head_pad)], cross_in_back)
-    g_x1 = g_x2 + both[:batch]
-    g_y = both[batch:]
-
-    g_gate1 = jnp.sum(g_x1 * attn_total, axis=(0, 1))
-    g_attn_loc = (g_x1 * gate1).astype(BF16)
-    g_b_o = token_sum(g_attn_loc)
-    g_attn_val, g_w_o = gather_call(
-        tp_size, 8, 'gather_g_attn', [g_attn_loc], [attn_val, wo], (), [(batch, n_tok, head_pad)], [(head_pad, width)], out_back)
-    g_qkv = jnp.concatenate(attend_back(q_self, k_self, v_self, attn_prob, g_attn_val, scale), axis=-1)
-
-    def self_in_back(rows, put, ins, held, accs):
-        g_blk = rows_of(ins[0], rows)
-        put(0, dot(g_blk, ins[1][...], NT))
-        accs[0][...] += dot(g_blk, rows_of(held[0], rows), TN)
-        accs[1][...] += row_sum(g_blk.astype(F32))
-
-    g_h1, g_w_qkv, g_b_qkv = scatter_call(
-        tp_size, 9, 'scatter_qkv', n_loc, width, 1, [g_qkv, wqkv], [h1_all],
-        [(3 * head_pad, width), (1, 3 * head_pad)], self_in_back)
-    g_x = g_x1 + layer_norm_back(normed1, inv_std1, g_h1 * (1.0 + scale1))
-    sums = total_call(tp_size, 10, [token_sum(g_h1), token_sum(g_h1 * normed1), g_gate1, g_shift2, g_scale2, g_gate2, g_b_o, g_b_co, g_b_2])
-    g_table = jnp.stack(sums[:6])
-    g_b_o, g_b_co, g_b_2 = sums[6:]
+
+    zero = jnp.zeros_like(g_b_2)
+    sums_in = jnp.stack([zero, zero, zero, g_shift2, g_scale2, g_gate2, zero, g_b_co, g_b_2] + [zero] * 7)
+    g_x, g_y, sums, g_w_qkv, g_w_kv, g_w_q, g_w_o, g_w_co, g_b_qkv, g_b_kv, g_b_q = backward_call(
+        tp_size, 3, head_dim, head_pad,
+        [g_cross_loc, g_x2, x_loc, attn_total, t_loc, mod_table, wqkv, wkv, wq, wo, wco, sums_in],
+        [qkv, kv, q_cross, attn_val, cross_val, attn_prob, cross_prob], [h1_all, x1_all, y_all])
 
     def head_weight(grad, n_part):
-        return drop_pad(grad, n_part, head_dim, head_pad).T.astype(BF16)[:, None, :]
+        return drop_pad(grad, n_part, head_dim, head_pad).astype(BF16)[None].transpose(2, 0, 1)
 
     def head_bias(grad, n_part):
         return drop_pad(grad[0], n_part, head_dim, head_pad)[None].astype(BF16)
 
-    return (x_out, g_x.astype(BF16), g_y.astype(BF16), g_table,
-            head_weight(g_w_qkv, 3), head_bias(g_b_qkv, 3), g_w_o[None, :head_dim].astype(BF16), g_b_o.astype(BF16),
+    return (x_out, g_x, g_y, sums[:6],
+            head_weight(g_w_qkv, 3), head_bias(g_b_qkv, 3), g_w_o[None, :head_dim].astype(BF16), sums[6].astype(BF16),
             head_weight(g_w_q, 1), head_bias(g_b_q, 1), head_weight(g_w_kv, 2), head_bias(g_b_kv, 2),
-            g_w_co[None, :head_dim].astype(BF16), g_b_co.astype(BF16),
-            g_w_1.T.astype(BF16), g_b_1[0].astype(BF16), g_w_2.astype(BF16), g_b_2.astype(BF16))
+            g_w_co[None, :head_dim].astype(BF16), sums[7].astype(BF16),
+            g_w_1.T.astype(BF16), g_b_1[0].astype(BF16), g_w_2.astype(BF16), sums[8].astype(BF16))
 
 
 def solution(mesh):

time: 602 us -> 529 us (0.88)
  matrix products: 27.5 us -> 0 us
  Pallas kernels: 500 us -> 475 us
  other arithmetic: 37.4 us -> 20.8 us
    pallas_call x1 -> x2, Pallas kernels: 16.3 us -> 340 us  [the longest x1 177 us: backward_call(): pl.pallas_call(functools.partial(backward_body, tp_size, head_dim), out_s...]
    pallas_call x5 -> x1, Pallas kernels: 249 us -> 69.5 us  [gather_call(): pl.pallas_call(functools.partial(gather_body, tp_size, len(blocks), len(i...]
    pallas_call x5 -> x1, Pallas kernels: 235 us -> 64.7 us  [scatter_call(): pl.pallas_call(functools.partial(scatter_body, tp_size, n_out, len(ins),...]
    dot_general x10 -> x0, matrix products: 23.5 us -> none  [product(): return jnp.einsum(form, lhs, rhs, preferred_element_type=F32)]
where the time goes in v2:
time: 529 us; the launch traced here: 519 us
  Pallas kernels  475 us (90%)
  local copies, waits for them, and re-layouts  22.7 us (4%)
  other arithmetic  20.8 us (4%)
    pallas_call x1, Pallas kernels, backward_call(): pl.pallas_call(functools.partial(backward_body, tp_size, head_dim), out_s...  177 us
    pallas_call x1, Pallas kernels, forward_call(): pl.pallas_call(functools.partial(forward_body, tp_size, head_dim), out_sh...  163 us
    pallas_call x1, Pallas kernels, gather_call(): pl.pallas_call(functools.partial(gather_body, tp_size, len(blocks), len(i...  69.5 us
    pallas_call x1, Pallas kernels, scatter_call(): pl.pallas_call(functools.partial(scatter_body, tp_size, n_out, len(ins),...  64.7 us

profile of v2, /device:TPU:21, one launch (start us, length us, event | category | flops | bytes accessed | tf_op | source)
XLA Modules:
  0.0 519.1 jit_solution(5045935248067862677)
XLA Ops:
  0.7 1.2 pad_convert_fusion.refs_10_
  1.8 0.7 reduce.1
  2.5 0.1 reshape.157
  2.6 0.6 pad_convert_fusion.1
  3.2 0.7 reduce
  3.9 0.1 reshape.154
  4.0 0.6 copy.41
  4.5 1.2 reshape.171.refs_3_
  5.8 1.3 broadcast_in_dim.11.refs_12_
  7.1 1.3 broadcast_in_dim.12.refs_14_
  8.4 1.3 broadcast_in_dim.10.refs_4_
  9.7 0.7 convert_element_type.131
  10.4 0.7 slice_convert_fusion.2
  11.1 0.9 slice.69
  12.0 0.7 slice_bitcast_fusion.2
  12.7 163.0 %attention_forward.1 = (bf16[8,256,1408]{2,1,0:T(8,128)(2,1)}, bf16[8,256,1408]{2,1,0:T(8,128)(2,1)}, bf16[8,256,1408]{2,1,0:T(8,128)(2,1)}, bf16[8,256,384]{2,1...) custom-call(bf16[8,16,1408]{2,1,0:T(8,128)(2,1)} %refs_2_.7, ...), custom_call_target="tpu_custom_call" | custom-call | tf_op jit(solution)/shard_map/attention_forward/pallas_call | solution.py:718
  175.7 1.1 convert_reduce_fusion
  176.8 1.2 fusion.12
  178.0 2.3 convert_reduce_fusion.1
  180.4 69.5 %gather_h2_g.1 = (bf16[8,256,384]{2,1,0:T(8,128)(2,1)}, bf16[8,256,384]{2,1,0:T(8,128)(2,1)}, f32[384,1408]{1,0:T(8,128)}, f32[384,1408]{1,0:T(8,128)}, f32[1,384]{1,0:T(1,128)}) custom-call(bf16[8,16,1408]{2,1,0:T(8,128)(2,1)} %get-tuple-element.112.refs_0_, bf16[8,16,1408]{2,1,0:T(8,128)(2,1)} %get-tuple-element.104.refs_1_, bf16[1408,384]{1,0:T(8,128)(2,1)} %refs_2_.6, ...), custom_call_target="tpu_custom_call" | custom-call | tf_op jit(solution)/shard_map/gather_h2_g/pallas_call | solution.py:161
  249.8 0.0 copy-start.10
  249.9 64.7 %scatter_h2_out.1 = f32[16,16,1408]{2,1,0:T(8,128)} custom-call(bf16[8,256,384]{2,1,0:T(8,128)(2,1)} %get-tuple-element.47.refs_0_, bf16[8,256,384]{2,1,0:T(8,128)(2,1)} %get-tuple-element.48.refs_1_, bf16[1408,384]{1,0:T(8,128)(2,1)} %refs_2_.6, bf16[384,1408]{1,0:T(8,128)(2,1)} %refs_3_.3), custom_call_target="tpu_custom_call" | custom-call | tf_op jit(solution)/shard_map/scatter_h2_out/pallas_call | solution.py:292
  314.5 0.0 copy-done.10
  314.5 0.0 copy-start
  314.6 0.0 copy-start.1
  314.6 0.0 copy-start.2
  314.6 0.0 copy-start.7
  314.6 0.6 convert_reduce_fusion.3
  315.2 2.8 fusion.15
  318.0 0.0 copy-done
  318.0 0.0 copy-done.1
  318.0 0.0 copy-done.2
  318.0 0.0 copy-done.7
  318.0 1.3 convert_reduce_fusion.2
  319.4 1.3 stack.27.refs_11_
  320.8 177.5 %attention_backward.1 = (bf16[8,16,1408]{2,1,0:T(8,128)(2,1)}, bf16[8,16,1408]{2,1,0:T(8,128)(2,1)}, f32[16,1408]{1,0:T(8,128)}, f32[384,1408]{1,0:T(8,128)}, f3...) custom-call(bf16[8,16,1408]{2,1,0:T(8,128)(2,1)} %get-tuple-element., ...), custom_call_target="tpu_custom_call" | custom-call | tf_op jit(solution)/shard_map/attention_backward/pallas_call | solution.py:995
  498.2 0.0 copy-start.6
  498.2 1.3 convert.51
  499.6 0.7 convert_reduce_fusion.5
  500.2 0.6 convert_element_type.141
  500.9 0.7 convert_reduce_fusion.4
  501.6 0.6 convert_element_type.137
  502.2 0.9 convert.49
  503.1 1.4 slice.75
  504.5 0.7 slice_reduce_fusion.1
  505.2 1.8 fusion.16
  506.9 1.8 fusion.17
  508.7 1.1 convert_bitcast_fusion.1
  509.8 0.7 slice_bitcast_fusion
  510.5 0.0 copy-done.6
  510.6 0.1 convert.52
  510.6 0.8 slice.94
  511.5 0.9 copy-done.5
  512.3 0.1 convert.46
  512.5 0.9 slice.90
  513.4 0.8 copy-done.4
  514.2 0.1 convert_bitcast_fusion
  514.3 0.0 copy-start.3
  514.3 1.4 copy.38
  515.8 0.6 copy-done.3
  516.3 1.1 convert_element_type.148
  517.4 0.0 copy-done.9
  517.4 0.7 copy.44
  518.2 0.7 copy.45
  (19 shorter events, 0.1 us)
Async XLA Ops:
  249.8 64.7 %copy-start.10 = (f32[1,384]{1,0:T(1,128)S(1)}, f32[1,384]{1,0:T(1,128)}, u32[]{:S(2)}) copy-start(f32[1,384]{1,0:T(1,128)} %get-tuple-element.72) | copy-start | bytes 4612
  314.5 3.4 copy-start
  314.6 3.4 copy-start.1
  314.6 3.4 copy-start.2
  314.6 3.4 copy-start.7
  498.2 12.3 %copy-start.6 = (f32[256,1408]{1,0:T(8,128)S(1)}, f32[256,1408]{1,0:T(8,128)}, u32[]{:S(2)}) copy-start(f32[256,1408]{1,0:T(8,128)} %get-tuple-element.68) | copy-start | bytes 4325380
  510.6 1.8 copy-start.5
  512.3 1.9 copy-start.4
  514.3 2.0 copy-start.3
  516.3 1.1 copy-start.9
  516.3 1.8 copy-start.8

commit v3 on v2

v3 whole, which is shorter than its diff:
```python
import functools
import itertools

import jax
import jax.numpy as jnp
from jax import lax
from jax.experimental import pallas as pl
from jax.experimental.pallas import tpu as pltpu
from jax.sharding import PartitionSpec as P

LN_EPS = 1e-6
MASK_FILL = -1e30
LANES = 128
MESH = pl.DeviceIdType.MESH
BF16 = jnp.bfloat16
F32 = jnp.float32
NN = (((1,), (0,)), ((), ()))
NT = (((1,), (1,)), ((), ()))
TN = (((0,), (0,)), ((), ()))
SHIFT1, SCALE1, GATE1, SHIFT2, SCALE2, GATE2, B_O, B_CO, B_2 = range(9)
SUM_ROWS = 16
FORWARD_BIASES = 'qkv', 'kv', 'q', 'o', 'co'
UP, DOWN = HALVES = WAYS = 0, 1
SEND, TAKE = True, False
KERNEL = functools.partial(pltpu.CompilerParams, has_side_effects=True, vmem_limit_bytes=67 * 1000 * 1000)
VMEM, ANY = pl.BlockSpec(memory_space=pltpu.VMEM), pl.BlockSpec(memory_space=pl.ANY)


def dot(lhs, rhs, dims=NN):
    return lax.dot_general(lhs, rhs, dims, preferred_element_type=F32)


def cutter(refs):
    left = iter(refs)
    return lambda n: list(itertools.islice(left, n))


def biases_of(packed, names, width, head_dim):
    return [packed[:, at:at + size] for at, size in (bias_place(name, width, head_dim, packed.shape[1]) for name in names)]


def bias_place(name, width, head_dim, total):
    head_pad = -(-head_dim // LANES) * LANES
    sizes = {'qkv': 3 * head_pad, 'kv': 2 * head_pad, 'q': head_pad, 'o': width, 'co': width, '2': width}
    sizes['1'] = total - sum(sizes.values())
    names = list(sizes)
    return sum(sizes[n] for n in names[:names.index(name)]), sizes[name]


class Place:
    def __init__(self, tp_size):
        self.tp_size = tp_size
        self.me = lax.axis_index('tp')
        self.ring, self.chip, self.core = tp_size // 2, self.me // 2, lax.rem(self.me, 2)
        self.half = self.ring // 2

    def wrap(self, zz):
        return lax.rem(zz + self.ring, self.ring)

    def sibling(self):
        return {'tp': self.chip * 2 + 1 - self.core}

    def ahead(self, sign):
        return {'tp': self.wrap(self.chip + sign) * 2 + self.core}

    def other(self, d):
        return {'tp': lax.rem(self.me + d, self.tp_size)}

    def greet(self, peers):
        barrier = pltpu.get_barrier_semaphore()
        for peer in peers:
            pl.semaphore_signal(barrier, device_id=peer, device_id_type=MESH)
        pl.semaphore_wait(barrier, len(peers))

    def greet_all(self):
        self.greet([self.other(d) for d in range(1, self.tp_size)])

    def greet_near(self):
        self.greet([self.ahead(1), self.ahead(-1), self.sibling()])


class Gather:
    def __init__(self, at, own, full, sems):
        self.at, self.own_ref, self.full = at, own, full
        self.rsend, self.rrecv, self.ssend, self.srecv = sems
        self.batch, self.n_loc = own.shape[0], own.shape[1]
        self.hb = self.batch // 2

    def part(self, zz, cc, ch):
        row = pl.multiple_of((zz * 2 + cc) * self.n_loc, self.n_loc)
        return self.full.at[pl.ds(ch * self.hb, self.hb), pl.ds(row, self.n_loc), :]

    def own(self, ch):
        return self.own_ref.at[pl.ds(ch * self.hb, self.hb)]

    def ring_copy(self, way, k, ch, sending):
        at = self.at
        sign = -1 if way == UP else 1
        zb = at.wrap(at.chip + sign * (k - 1 if sending else k))
        src = self.own(ch) if (sending and k == 1) else self.part(zb, at.core, ch)
        return pltpu.make_async_remote_copy(
            src_ref=src, dst_ref=self.part(zb, at.core, ch),
            send_sem=self.rsend.at[way, k - 1, ch], recv_sem=self.rrecv.at[way, k - 1, ch],
            device_id=at.ahead(-sign), device_id_type=MESH)

    def chip_at(self, slot):
        k = (slot + 1) // 2
        return self.at.wrap(self.at.chip - k) if slot % 2 else self.at.wrap(self.at.chip + k)

    def sib_copy(self, slot, ch, sending):
        at = self.at
        cc = at.core if sending else 1 - at.core
        zb = self.chip_at(slot)
        src = self.own(ch) if (sending and slot == 0) else self.part(zb, cc, ch)
        return pltpu.make_async_remote_copy(
            src_ref=src, dst_ref=self.part(zb, cc, ch),
            send_sem=self.ssend.at[slot, ch], recv_sem=self.srecv.at[slot, ch],
            device_id=at.sibling(), device_id_type=MESH)

    def carries(self, way, k, ch):
        return k < self.at.half or (k == self.at.half and ch == way)

    def slot_of(self, way, k):
        half = self.at.half
        return 2 * half - 1 if k == half else (2 * k - 1 if way == UP else 2 * k)

    def start(self):
        for way, ch in ((UP, 0), (DOWN, 1), (UP, 1), (DOWN, 0)):
            self.ring_copy(way, 1, ch, SEND).start()
        for ch in HALVES:
            self.sib_copy(0, ch, SEND).start()
        row = pl.multiple_of(self.at.me * self.n_loc, self.n_loc)
        self.full[:, pl.ds(row, self.n_loc), :] = self.own_ref[...]

    def arrive(self, way, k, ch):
        self.ring_copy(way, k, ch, TAKE).wait_recv()
        if self.carries(way, k + 1, ch):
            self.ring_copy(way, k + 1, ch, SEND).start()
        self.sib_copy(self.slot_of(way, k), ch, SEND).start()

    def group(self, g):
        k = g // 2 + 1
        first, second = ((UP, 0), (DOWN, 1)) if g % 2 == 0 else ((UP, 1), (DOWN, 0))
        self.arrive(first[0], k, first[1])
        self.arrive(second[0], k, second[1])

    def groups_before(self, slot):
        last = self.at.ring - 1
        return () if slot == last - 1 else ((last - 1,) if slot == last else (slot,))

    def ready(self, slot):
        for ch in HALVES:
            self.sib_copy(slot, ch, TAKE).wait_recv()

    def rows(self, slot):
        k = (slot + 1) // 2
        zz = self.at.wrap(self.at.chip + (1 - 2 * lax.rem(slot, 2)) * k)
        return pl.ds(pl.multiple_of(zz * 2 * self.n_loc, 2 * self.n_loc), 2 * self.n_loc)

    def save_copy(self, dest, sem, slot):
        rows = self.rows(slot)
        return pltpu.make_async_copy(self.full.at[:, rows, :], dest.at[:, rows, :], sem.at[slot])

    def finish(self):
        for way in WAYS:
            for k in range(1, self.at.half + 1):
                for ch in HALVES:
                    if self.carries(way, k, ch):
                        self.ring_copy(way, k, ch, SEND).wait_send()
        for slot in range(self.at.ring):
            for ch in HALVES:
                self.sib_copy(slot, ch, SEND).wait_send()


class Scatter:
    def __init__(self, at, pbuf, sibr, rcv, sems):
        self.at, self.pbuf, self.sibr, self.rcv = at, pbuf, sibr, rcv
        self.rsend, self.rrecv, self.ssend, self.srecv = sems
        self.batch, self.n_loc = sibr.shape[1], sibr.shape[2]
        self.hb = self.batch // 2

    def slot_of(self, way, s):
        return 0 if s == 0 else (2 * s - 1 if way == UP else 2 * s)

    def rows(self, slot):
        at = self.at
        away = at.half - (slot + 1) // 2
        zz = at.wrap(at.chip + (2 * lax.rem(slot, 2) - 1) * away)
        return pl.ds(pl.multiple_of(zz * 2 * self.n_loc, 2 * self.n_loc), 2 * self.n_loc)

    def put(self, slot, value):
        self.pbuf[slot] = value.astype(BF16).reshape(self.batch, 2 * self.n_loc, value.shape[-1])
        self.sib_copy(slot).start()

    def ring_copy(self, way, s, ch):
        part = pl.ds(ch * self.hb, self.hb)
        return pltpu.make_async_remote_copy(
            src_ref=self.sibr.at[self.slot_of(way, s), part], dst_ref=self.rcv.at[way, s, part],
            send_sem=self.rsend.at[way, s, ch], recv_sem=self.rrecv.at[way, s, ch],
            device_id=self.at.ahead(1 if way == UP else -1), device_id_type=MESH)

    def sib_copy(self, slot):
        rows = pl.ds(pl.multiple_of((1 - self.at.core) * self.n_loc, self.n_loc), self.n_loc)
        return pltpu.make_async_remote_copy(
            src_ref=self.pbuf.at[slot, :, rows, :], dst_ref=self.sibr.at[slot],
            send_sem=self.ssend.at[slot], recv_sem=self.srecv.at[slot],
            device_id=self.at.sibling(), device_id_type=MESH)

    def own_sum(self, slot, part):
        rows = pl.ds(pl.multiple_of(self.at.core * self.n_loc, self.n_loc), self.n_loc)
        return self.pbuf[slot, part, rows, :].astype(F32) + self.sibr[slot, part].astype(F32)

    def starts_at(self, way, ch):
        return 0 if ch == way else 1

    def pass_on(self, way, s, ch):
        slot, part = self.slot_of(way, s), pl.ds(ch * self.hb, self.hb)
        total = self.own_sum(slot, part)
        if s > self.starts_at(way, ch):
            self.ring_copy(way, s - 1, ch).wait_recv()
            total = total + self.rcv[way, s - 1, part].astype(F32)
        self.sibr[slot, part] = total.astype(BF16)
        self.ring_copy(way, s, ch).start()

    def step(self, s):
        if s == 0:
            self.sib_copy(0).wait_recv()
            self.pass_on(UP, 0, 0)
            self.pass_on(DOWN, 0, 1)
            return
        self.sib_copy(2 * s - 1).wait_recv()
        self.pass_on(UP, s, 1)
        self.sib_copy(2 * s).wait_recv()
        self.pass_on(DOWN, s, 0)
        self.pass_on(UP, s, 0)
        self.pass_on(DOWN, s, 1)

    def final(self, use):
        last = self.at.ring - 1
        self.sib_copy(last).wait_recv()
        for ch, order in ((1, (UP, DOWN)), (0, (DOWN, UP))):
            part = pl.ds(ch * self.hb, self.hb)
            total = self.own_sum(last, part)
            for way in order:
                self.ring_copy(way, self.at.half - 1, ch).wait_recv()
                total = total + self.rcv[way, self.at.half - 1, part].astype(F32)
            use(part, total)

    def finish(self):
        for way in WAYS:
            for s in range(self.at.half):
                for ch in HALVES:
                    if s >= self.starts_at(way, ch):
                        self.ring_copy(way, s, ch).wait_send()
        for slot in range(self.at.ring):
            self.sib_copy(slot).wait_send()


def loop_slots(n, hooks, body):
    def step(slot, carry):
        for s in range(n):
            @pl.when(slot == s)
            def _():
                hooks(s)
        body(slot)
        return carry
    lax.fori_loop(0, n, step, None)


def gather_sems(tp_size):
    ring, half = tp_size // 2, tp_size // 4
    return [pltpu.SemaphoreType.DMA(s) for s in ((2, half, 2), (2, half, 2), (ring, 2), (ring, 2))]


def scatter_sems(tp_size):
    ring, half = tp_size // 2, tp_size // 4
    return [pltpu.SemaphoreType.DMA(s) for s in ((2, half, 2), (2, half, 2), (ring,), (ring,))]


def pad_rows(dest, source, head_dim):
    parts = source.shape[0] // head_dim
    head_pad = dest.shape[0] // parts
    width = dest.shape[1]
    for i in range(parts):
        dest[i * head_pad:i * head_pad + head_dim, :] = source[i * head_dim:(i + 1) * head_dim, :]
        dest[i * head_pad + head_dim:(i + 1) * head_pad, :] = jnp.zeros((head_pad - head_dim, width), dest.dtype)


def mod_row(t_ref, table_ref, i):
    width = table_ref.shape[1]
    return table_ref[i:i + 1, :].astype(F32) + t_ref[:, i * width:(i + 1) * width].astype(F32)


def rows_of(ref, rows):
    block = ref[:, rows, :]
    return block.reshape(block.shape[0] * block.shape[1], block.shape[2])


def put_rows(ref, rows, value):
    ref[:, rows, :] = value.astype(ref.dtype).reshape(ref.shape[0], rows.size, ref.shape[2])


def row_sum(value):
    return jnp.sum(value, axis=0, keepdims=True)


def gelu_pair(hidden):
    c0, c1 = 0.7978845608028654, 0.044715
    square = hidden * hidden
    tanh = jnp.tanh(c0 * hidden * (1.0 + c1 * square))
    half_up = 0.5 * (1.0 + tanh)
    slope = half_up + 0.5 * hidden * (1.0 - tanh * tanh) * (c0 * (1.0 + 3.0 * c1 * square))
    return hidden * half_up, slope


def normalize(rows):
    rows = rows.astype(F32)
    centered = rows - jnp.mean(rows, axis=-1, keepdims=True)
    inv_std = lax.rsqrt(jnp.mean(centered * centered, axis=-1, keepdims=True) + LN_EPS)
    return centered * inv_std, inv_std


def normalize_back(normed, inv_std, g_normed):
    mean_g = jnp.mean(g_normed, axis=-1, keepdims=True)
    mean_gn = jnp.mean(g_normed * normed, axis=-1, keepdims=True)
    return inv_std * (g_normed - mean_g - normed * mean_gn)


def softmax_of(scores):
    top = jnp.max(scores, axis=-1, keepdims=True)
    powers = jnp.exp(scores - top)
    return powers * (1.0 / jnp.sum(powers, axis=-1, keepdims=True))


def forward_body(tp_size, head_dim, *refs):
    at = Place(tp_size)
    take = cutter(refs)
    x, y, t_emb, table, lens, biases, wqkv_in, wkv_in, wq_in, wo_in, wco_in = take(11)
    bqkv, bkv, bq, bo, bco = biases_of(biases, FORWARD_BIASES, wqkv_in.shape[1], head_dim)
    h1_out, y_out, x1_out = take(3)
    outs, scratch = take(9), take(9)
    qkv, kv, q_c, val, cval, prob, cprob, atot, x2 = scratch
    h1, x1, mod, fh, fy, fx, pbuf, sibr1, rcv1, sibr2, rcv2, wqkv, wkv, wq, wo, wco = take(16)
    gather_h, gather_y, gather_x = [Gather(at, own, full, take(4)) for own, full in ((h1, fh), (y, fy), (x1, fx))]
    scat_o, scat_c = [Scatter(at, pbuf, sibr, rcv, take(4)) for sibr, rcv in ((sibr1, rcv1), (sibr2, rcv2))]
    saves, out_sem = take(3), refs[-1]
    batch = x.shape[0]
    head_pad = wq.shape[0]
    scale = head_dim ** -0.5

    def out_copy(i):
        return pltpu.make_async_copy(scratch[i], outs[i], out_sem.at[i])

    for i in range(3):
        mod[i] = mod_row(t_emb, table, i)

    def norm_one(b, carry):
        normed, _ = normalize(x[b])
        h1[b] = (normed * (1.0 + mod[1, pl.ds(b, 1), :]) + mod[0, pl.ds(b, 1), :]).astype(BF16)
        return carry

    lax.fori_loop(0, batch, norm_one, None)
    at.greet_near()
    gather_h.start()
    for dest, source in ((wqkv, wqkv_in), (wkv, wkv_in), (wq, wq_in), (wo, wo_in), (wco, wco_in)):
        pad_rows(dest, source, head_dim)

    def hooks(s):
        for g in gather_h.groups_before(s):
            gather_h.group(g)
        gather_h.ready(s)
        if s == at.ring - 4:
            gather_y.start()

    def project(slot):
        rows = gather_h.rows(slot)
        gather_h.save_copy(h1_out, saves[0], slot).start()
        put_rows(qkv, rows, dot(rows_of(fh, rows), wqkv[...], NT) + bqkv)

    loop_slots(at.ring, hooks, project)

    def hooks(b):
        if b == batch // 2:
            gather_y.group(0)
        if b == batch - 1:
            gather_y.group(1)

    def attend_self(b):
        q_b, k_b, v_b = [qkv[b, :, i * head_pad:(i + 1) * head_pad] for i in range(3)]
        p_b = softmax_of(dot(q_b, k_b, NT) * scale).astype(BF16)
        prob[b] = p_b
        val[b] = dot(p_b, v_b).astype(BF16)

    loop_slots(batch, hooks, attend_self)
    for i in (0, 3, 5):
        out_copy(i).start()

    ynext = {2: 2, 3: 3, 5: 4, 6: 5, 7: 6}

    def hooks(s):
        if s >= 2 and s % 2 == 0:
            scat_o.step(s // 2 - 1)
        if s in ynext:
            gather_y.group(ynext[s])

    def project_o(slot):
        scat_o.put(slot, dot(rows_of(val, scat_o.rows(slot)), wo[...]))

    loop_slots(at.ring, hooks, project_o)
    scat_o.step(at.half - 1)

    def take_o(part, total):
        atot[part] = total + bo

    scat_o.final(take_o)
    out_copy(7).start()

    def x1_one(b, carry):
        x1[b] = (x[b].astype(F32) + mod[2, pl.ds(b, 1), :] * atot[b]).astype(BF16)
        return carry

    lax.fori_loop(0, batch, x1_one, None)

    gather_x.start()

    def hooks(s):
        for g in gather_x.groups_before(s):
            gather_x.group(g)
        gather_y.ready(s)
        gather_x.ready(s)

    def project(slot):
        rows = gather_x.rows(slot)
        gather_y.save_copy(y_out, saves[1], slot).start()
        gather_x.save_copy(x1_out, saves[2], slot).start()
        put_rows(kv, rows, dot(rows_of(fy, rows), wkv[...], NT) + bkv)
        put_rows(q_c, rows, dot(rows_of(fx, rows), wq[...], NT) + bq)

    loop_slots(at.ring, hooks, project)
    scat_o.finish()

    def attend_cross(b, carry):
        k_b, v_b = [kv[b, :, i * head_pad:(i + 1) * head_pad] for i in range(2)]
        scores = dot(q_c[b], k_b, NT) * scale
        slots = lax.broadcasted_iota(jnp.int32, scores.shape, 1)
        p_b = softmax_of(jnp.where(slots < lens[b], scores, MASK_FILL)).astype(BF16)
        cprob[b] = p_b
        cval[b] = dot(p_b, v_b).astype(BF16)
        return carry

    lax.fori_loop(0, batch, attend_cross, None)
    for i in (1, 2, 4, 6):
        out_copy(i).start()

    def hooks(s):
        if s >= 2 and s % 2 == 0:
            scat_c.step(s // 2 - 1)

    def project_c(slot):
        scat_c.put(slot, dot(rows_of(cval, scat_c.rows(slot)), wco[...]))

    loop_slots(at.ring, hooks, project_c)
    scat_c.step(at.half - 1)

    def take_c(part, total):
        x2[part] = (x1[part].astype(F32) + total + bco).astype(BF16)

    scat_c.final(take_c)
    out_copy(8).start()
    for stream in (gather_h, gather_y, gather_x, scat_c):
        stream.finish()
    for slot in range(at.ring):
        gather_h.save_copy(h1_out, saves[0], slot).wait()
        gather_y.save_copy(y_out, saves[1], slot).wait()
        gather_x.save_copy(x1_out, saves[2], slot).wait()
    for i in range(9):
        out_copy(i).wait()


def forward_call(tp_size, cid, head_dim, head_pad, *ins):
    batch, n_loc, width = ins[0].shape
    n_tok = n_loc * tp_size
    ring, half = tp_size // 2, tp_size // 4
    tokens = lambda last: (batch, n_tok, last)
    local = (batch, n_loc, width)
    kept = [(tokens(3 * head_pad), BF16), (tokens(2 * head_pad), BF16), (tokens(head_pad), BF16), (tokens(head_pad), BF16),
            (tokens(head_pad), BF16), (tokens(n_tok), BF16), (tokens(n_tok), BF16), (local, F32), (local, BF16)]
    sib, rcv = (ring, *local), (2, half, *local)
    return pl.pallas_call(
        functools.partial(forward_body, tp_size, head_dim),
        out_shape=[jax.ShapeDtypeStruct(tokens(width), BF16)] * 3 + [jax.ShapeDtypeStruct(*k) for k in kept],
        in_specs=[VMEM] * 4 + [pl.BlockSpec(memory_space=pltpu.SMEM)] + [VMEM] * (len(ins) - 5),
        out_specs=[ANY] * (3 + len(kept)),
        scratch_shapes=[pltpu.VMEM(*k) for k in kept] + [
            pltpu.VMEM(local, BF16), pltpu.VMEM(local, BF16), pltpu.VMEM((3, batch, width), F32),
            pltpu.VMEM(tokens(width), BF16), pltpu.VMEM(tokens(width), BF16), pltpu.VMEM(tokens(width), BF16),
            pltpu.VMEM((ring, batch, 2 * n_loc, width), BF16),
            pltpu.VMEM(sib, BF16), pltpu.VMEM(rcv, BF16), pltpu.VMEM(sib, BF16), pltpu.VMEM(rcv, BF16)]
        + [pltpu.VMEM((n * head_pad, width), BF16) for n in (3, 2, 1, 1, 1)]
        + gather_sems(tp_size) * 3 + scatter_sems(tp_size) * 2
        + [pltpu.SemaphoreType.DMA((ring,))] * 3 + [pltpu.SemaphoreType.DMA((len(kept),))],
        compiler_params=KERNEL(collective_id=cid),
        name='attention_forward',
    )(*ins)


class RowFeed:
    def __init__(self, source, buf, sem, rows):
        self.source, self.buf, self.sem, self.rows = source, buf, sem, rows

    def copy(self, slot):
        side = lax.rem(slot, 2)
        return pltpu.make_async_copy(self.source.at[:, self.rows(slot), :], self.buf.at[side], self.sem.at[side])

    def take(self, slot, n):
        @pl.when(slot + 1 < n)
        def _():
            self.copy(slot + 1).start()
        self.copy(slot).wait()
        block = self.buf[lax.rem(slot, 2)]
        return block.reshape(block.shape[0] * block.shape[1], block.shape[2])


def small_total(at, src, got, mine, out, sems):
    send1, recv1, send2, recv2 = sems
    tiles = src.shape[1] // LANES

    def lanes(i):
        return pl.ds(i * LANES, LANES)

    def first(tile, peer_slot):
        return pltpu.make_async_remote_copy(
            src_ref=src.at[:, lanes(tile)], dst_ref=got.at[peer_slot], send_sem=send1.at[tile], recv_sem=recv1.at[peer_slot],
            device_id={'tp': tile}, device_id_type=MESH)

    def second(tile, d):
        return pltpu.make_async_remote_copy(
            src_ref=mine, dst_ref=out.at[:, lanes(tile)], send_sem=send2.at[d - 1], recv_sem=recv2.at[tile],
            device_id=at.other(d), device_id_type=MESH)

    for tile in range(tiles):
        @pl.when(at.me != tile)
        def _():
            first(tile, lax.rem(at.me - tile + at.tp_size, at.tp_size) - 1).start()
    for tile in range(tiles):
        @pl.when(at.me == tile)
        def _():
            total = src[:, tile * LANES:(tile + 1) * LANES]
            for d in range(1, at.tp_size):
                first(tile, d - 1).wait_recv()
                total = total + got[d - 1]
            mine[...] = total
            for d in range(1, at.tp_size):
                second(tile, d).start()
            out[:, tile * LANES:(tile + 1) * LANES] = total
            for d in range(1, at.tp_size):
                second(tile, d).wait_send()
    for tile in range(tiles):
        @pl.when(at.me != tile)
        def _():
            second(tile, 1).wait_recv()
            first(tile, 0).wait_send()


def backward_body(tp_size, head_dim, *refs):
    at = Place(tp_size)
    take = cutter(refs)
    g_cross, g_x2, x, atot, t_emb, table, wqkv_in, wkv_in, wq_in, wo_in, wco_in, sums_in = take(12)
    loads, feeds = take(7), take(3)
    g_x, g_y, sums_out = take(3)
    accs = take(8)
    gw_qkv, gw_kv, gw_q, gw_o, gw_co, gb_qkv, gb_kv, gb_q = accs
    held = take(7)
    qkv, kv, q_c, val, cval, prob, cprob = held
    full, pbuf, sibr1, rcv1, pbufy, sibr2, rcv2, wqkv, wkv, wq, wo, wco = take(12)
    g_val, g_qkv, g_kv, g_q, g_x1, g_h1, g_attn, mod, sums, got, mine, feed_a, feed_y = take(13)
    gather_c, gather_a = [Gather(at, own, full, take(4)) for own in (g_cross, g_attn)]
    near, far = (pbuf, sibr1, rcv1), (pbufy, sibr2, rcv2)
    scat_q, scat_y, scat_h = [Scatter(at, *bufs, take(4)) for bufs in (near, far, near)]
    load_sem, *feed_sems = take(4)
    feed_h, feed_x, feed_yy = [
        RowFeed(source, buf, sem, scat.rows)
        for source, buf, sem, scat in zip(feeds, (feed_a, feed_a, feed_y), feed_sems, (scat_h, scat_q, scat_y))]
    batch, n_loc, width = x.shape
    ring, half = at.ring, at.half
    head_pad = wq.shape[0]
    scale = head_dim ** -0.5

    def load_copy(i):
        return pltpu.make_async_copy(loads[i], held[i], load_sem.at[i])

    for i in range(len(held)):
        load_copy(i).start()
    at.greet_all()
    gather_c.start()
    feed_x.copy(0).start()
    feed_yy.copy(0).start()
    for i in range(3):
        mod[i] = mod_row(t_emb, table, i)
    for dest, source in ((wqkv, wqkv_in), (wkv, wkv_in), (wq, wq_in), (wo, wo_in), (wco, wco_in)):
        pad_rows(dest, source, head_dim)
    sums[...] = sums_in[...]
    for acc in accs:
        acc[...] = jnp.zeros_like(acc)
    for i in range(len(held)):
        load_copy(i).wait()

    def out_back(gather, value, weight, acc):
        def body(slot):
            rows = gather.rows(slot)
            block = rows_of(full, rows)
            put_rows(g_val, rows, dot(block, weight[...], NT))
            acc[...] += dot(rows_of(value, rows), block, TN)
        return body

    def hooks(s):
        for g in gather_c.groups_before(s):
            gather_c.group(g)
        gather_c.ready(s)

    loop_slots(ring, hooks, out_back(gather_c, cval, wco, gw_co))
    gather_c.finish()

    def back_one(q_b, k_b, v_b, p_b, g_b):
        g_p = dot(g_b, v_b, NT)
        p_f = p_b.astype(F32)
        row_dot = jnp.sum(g_p * p_f, axis=-1, keepdims=True)
        g_s = (p_f * (g_p - row_dot) * scale).astype(BF16)
        return dot(g_s, k_b).astype(BF16), dot(g_s, q_b, TN).astype(BF16), dot(p_b, g_b, TN).astype(BF16)

    def cross_back(b, carry):
        parts = back_one(q_c[b], kv[b, :, :head_pad], kv[b, :, head_pad:], cprob[b], g_val[b])
        g_q[b] = parts[0]
        g_kv[b, :, :head_pad] = parts[1]
        g_kv[b, :, head_pad:] = parts[2]
        return carry

    lax.fori_loop(0, batch, cross_back, None)

    def hooks(s):
        if s >= 2 and s % 2 == 0:
            scat_q.step(s // 2 - 1)

    def put_q(slot):
        block = rows_of(g_q, scat_q.rows(slot))
        scat_q.put(slot, dot(block, wq[...]))
        gw_q[...] += dot(block, feed_x.take(slot, ring), TN)
        gb_q[...] += row_sum(block.astype(F32))

    def put_y(first, last):
        def body(slot, carry):
            block = rows_of(g_kv, scat_y.rows(slot))
            scat_y.put(slot, dot(block, wkv[...]))
            gw_kv[...] += dot(block, feed_yy.take(slot, ring), TN)
            gb_kv[...] += row_sum(block.astype(F32))
            return carry
        lax.fori_loop(first, last, body, None)

    loop_slots(ring, hooks, put_q)
    scat_q.step(half - 1)
    put_y(0, 3)
    scat_y.step(0)

    def take_q(part, total):
        g_x1[part] = g_x2[part] + total

    scat_q.final(take_q)
    feed_h.copy(0).start()

    def x1_back(b, carry):
        gate_sum, bias_sum = carry
        rows = g_x1[b]
        block = (rows * mod[2, pl.ds(b, 1), :]).astype(BF16)
        g_attn[b] = block
        return gate_sum + row_sum(rows * atot[b]), bias_sum + row_sum(block.astype(F32))

    zero = jnp.zeros((1, width), F32)
    gate_sum, bias_sum = lax.fori_loop(0, batch, x1_back, (zero, zero))
    for row, value in ((GATE1, gate_sum), (B_O, bias_sum)):
        sums[row:row + 1, :] = value

    scat_q.finish()
    gather_a.start()

    def hooks(s):
        for g in gather_a.groups_before(s):
            gather_a.group(g)
        if s == 1:
            put_y(3, 5)
            scat_y.step(1)
        if s == 5:
            put_y(5, ring)
            scat_y.step(2)
        gather_a.ready(s)

    loop_slots(ring, hooks, out_back(gather_a, val, wo, gw_o))

    def hooks(b):
        if b == batch // 4:
            scat_y.step(half - 1)

    def self_back(b):
        parts = back_one(*[qkv[b, :, i * head_pad:(i + 1) * head_pad] for i in range(3)], prob[b], g_val[b])
        for i in range(3):
            g_qkv[b, :, i * head_pad:(i + 1) * head_pad] = parts[i]

    loop_slots(batch, hooks, self_back)

    def take_y(part, total):
        g_y[part] = total.astype(BF16)

    def hooks(s):
        if s >= 2 and s % 2 == 0:
            scat_h.step(s // 2 - 1)
        if s == 5:
            scat_y.final(take_y)

    def put_h(slot):
        block = rows_of(g_qkv, scat_h.rows(slot))
        scat_h.put(slot, dot(block, wqkv[...]))
        gw_qkv[...] += dot(block, feed_h.take(slot, ring), TN)
        gb_qkv[...] += row_sum(block.astype(F32))

    loop_slots(ring, hooks, put_h)
    scat_h.step(half - 1)
    def take_h(part, total):
        g_h1[part] = total

    scat_h.final(take_h)

    def x_back(b, carry):
        shift_sum, scale_sum = carry
        normed, inv_std = normalize(x[b])
        grad = g_h1[b]
        back = normalize_back(normed, inv_std, grad * (1.0 + mod[1, pl.ds(b, 1), :]))
        g_x[b] = (g_x1[b] + back).astype(BF16)
        return shift_sum + row_sum(grad), scale_sum + row_sum(grad * normed)

    shift_sum, scale_sum = lax.fori_loop(0, batch, x_back, (zero, zero))
    for row, value in ((SHIFT1, shift_sum), (SCALE1, scale_sum)):
        sums[row:row + 1, :] = value
    small_total(at, sums, got, mine, sums_out, take(4))
    for stream in (gather_a, scat_y, scat_h):
        stream.finish()


def backward_call(tp_size, cid, head_dim, head_pad, ins, loads, feeds):
    batch, n_loc, width = ins[0].shape
    n_tok = n_loc * tp_size
    ring, half = tp_size // 2, tp_size // 4
    n_sum = ins[-1].shape[0]
    tokens = lambda last: (batch, n_tok, last)
    local = (batch, n_loc, width)
    sib, rcv, pbuf = (ring, *local), (2, half, *local), (ring, batch, 2 * n_loc, width)
    outs = [(local, BF16), (local, BF16), ((n_sum, width), F32)]
    outs += [((n * head_pad, width), F32) for n in (3, 2, 1, 1, 1)] + [((1, n * head_pad), F32) for n in (3, 2, 1)]
    return pl.pallas_call(
        functools.partial(backward_body, tp_size, head_dim),
        out_shape=[jax.ShapeDtypeStruct(*o) for o in outs],
        in_specs=[VMEM] * len(ins) + [ANY] * (len(loads) + len(feeds)),
        out_specs=[VMEM] * len(outs),
        scratch_shapes=[pltpu.VMEM(a.shape, a.dtype) for a in loads]
        + [pltpu.VMEM(s, BF16) for s in (tokens(width), pbuf, sib, rcv, pbuf, sib, rcv)]
        + [pltpu.VMEM((n * head_pad, width), BF16) for n in (3, 2, 1, 1, 1)]
        + [pltpu.VMEM(tokens(n * head_pad), BF16) for n in (1, 3, 2, 1)]
        + [pltpu.VMEM(local, F32), pltpu.VMEM(local, F32), pltpu.VMEM(local, BF16), pltpu.VMEM((3, batch, width), F32), pltpu.VMEM((n_sum, width), F32),
           pltpu.VMEM((tp_size - 1, n_sum, LANES), F32), pltpu.VMEM((n_sum, LANES), F32)]
        + [pltpu.VMEM((2, batch, 2 * n_loc, width), BF16)] * 2
        + gather_sems(tp_size) * 2 + scatter_sems(tp_size) * 3
        + [pltpu.SemaphoreType.DMA((len(loads),))] + [pltpu.SemaphoreType.DMA((2,))] * 3
        + [pltpu.SemaphoreType.DMA((n,)) for n in (width // LANES, tp_size - 1, tp_size - 1, width // LANES)],
        compiler_params=KERNEL(collective_id=cid),
        name='attention_backward',
    )(*ins, *loads, *feeds)


def mlp_body(tp_size, head_dim, *refs):
    at = Place(tp_size)
    take = cutter(refs)
    x2, g, t_emb, table, biases, w1, w2 = take(7)
    b1, b2 = biases_of(biases, ('1', '2'), x2.shape[-1], head_dim)
    x_out, g_x2, g_cross, sums, gw_1, gw_2, gb_1 = take(7)
    h2, gm, mod, fh, fg, act_all, hid_all, g_h2, total = take(9)
    ring_bufs = take(3), take(3)
    gather_h, gather_g = [Gather(at, own, full, take(4)) for own, full in ((h2, fh), (gm, fg))]
    scat_h, scat_m = [Scatter(at, *bufs, take(4)) for bufs in ring_bufs]
    batch = x2.shape[0]

    for i in range(3):
        mod[i] = mod_row(t_emb, table, 3 + i)

    def shift_scale_gate(b):
        return [mod[i, pl.ds(b, 1), :] for i in range(3)]

    def norm_one(b, carry):
        shift, scale, gate = shift_scale_gate(b)
        normed, _ = normalize(x2[b])
        h2[b] = (normed * (1.0 + scale) + shift).astype(BF16)
        gm[b] = (g[b].astype(F32) * gate).astype(BF16)
        return carry

    lax.fori_loop(0, batch, norm_one, None)
    at.greet_near()
    gather_h.start()
    gather_g.start()
    for acc in (gw_1, gw_2, gb_1):
        acc[...] = jnp.zeros_like(acc)

    def hooks(s):
        for stream in (gather_h, gather_g):
            for group in stream.groups_before(s):
                stream.group(group)
        gather_h.ready(s)
        gather_g.ready(s)

    def mlp(slot):
        rows = gather_h.rows(slot)
        h2_blk, g_blk = rows_of(fh, rows), rows_of(fg, rows)
        act, slope = gelu_pair(dot(h2_blk, w1[...]) + b1)
        act = act.astype(BF16)
        put_rows(act_all, rows, act)
        g_hidden = dot(g_blk, w2[...], NT) * slope
        gb_1[...] += row_sum(g_hidden)
        g_hidden = g_hidden.astype(BF16)
        put_rows(hid_all, rows, g_hidden)
        gw_1[...] += dot(g_hidden, h2_blk, TN)
        gw_2[...] += dot(act, g_blk, TN)

    loop_slots(at.ring, hooks, mlp)

    def hooks(s):
        if s >= 2 and s % 2 == 0:
            scat_h.step(s // 2 - 1)
            scat_m.step(s // 2 - 1)

    def put_both(slot):
        rows = scat_h.rows(slot)
        scat_h.put(slot, dot(rows_of(hid_all, rows), w1[...], NT))
        scat_m.put(slot, dot(rows_of(act_all, rows), w2[...]))

    loop_slots(at.ring, hooks, put_both)
    scat_h.step(at.half - 1)
    scat_m.step(at.half - 1)

    def take_h(part, value):
        g_h2[part] = value

    def take_m(part, value):
        total[part] = value + b2

    scat_h.final(take_h)
    scat_m.final(take_m)

    def back_one(b, carry):
        _, scale, gate = shift_scale_gate(b)
        g_out, mlp_total, grad = g[b].astype(F32), total[b], g_h2[b]
        x_out[b] = (x2[b].astype(F32) + gate * mlp_total).astype(BF16)
        normed, inv_std = normalize(x2[b])
        back = g_out + normalize_back(normed, inv_std, grad * (1.0 + scale))
        g_x2[b] = back
        g_cross[b] = back.astype(BF16)
        terms = grad, grad * normed, g_out * mlp_total, back.astype(BF16).astype(F32), gm[b].astype(F32)
        return tuple(c + row_sum(t) for c, t in zip(carry, terms))

    zero = jnp.zeros((1, x2.shape[-1]), F32)
    sums[...] = jnp.zeros_like(sums)
    found = lax.fori_loop(0, batch, back_one, (zero,) * 5)
    for row, value in zip((SHIFT2, SCALE2, GATE2, B_CO, B_2), found):
        sums[row:row + 1, :] = value
    for stream in (gather_h, gather_g, scat_h, scat_m):
        stream.finish()


def mlp_call(tp_size, cid, head_dim, *ins):
    batch, n_loc, width = ins[0].shape
    ffn = ins[-1].shape[0]
    n_tok = n_loc * tp_size
    ring, half = tp_size // 2, tp_size // 4
    local, tokens, hidden = (batch, n_loc, width), (batch, n_tok, width), (batch, n_tok, ffn)
    bufs = (ring, batch, 2 * n_loc, width), (ring, *local), (2, half, *local)
    outs = [(local, BF16), (local, F32), (local, BF16), ((SUM_ROWS, width), F32), ((ffn, width), F32), ((ffn, width), F32), ((1, ffn), F32)]
    scratch = [(local, BF16), (local, BF16), ((3, batch, width), F32), (tokens, BF16), (tokens, BF16), (hidden, BF16), (hidden, BF16),
               (local, F32), (local, F32)]
    return pl.pallas_call(
        functools.partial(mlp_body, tp_size, head_dim),
        out_shape=[jax.ShapeDtypeStruct(*o) for o in outs],
        in_specs=[VMEM] * len(ins),
        out_specs=[VMEM] * len(outs),
        scratch_shapes=[pltpu.VMEM(*k) for k in scratch] + [pltpu.VMEM(k, BF16) for k in bufs * 2]
        + gather_sems(tp_size) * 2 + scatter_sems(tp_size) * 2,
        compiler_params=KERNEL(collective_id=cid),
        name='mlp_both_ways',
    )(*ins)


def finish_body(head_dim, n_head, *refs):
    sources, results = refs[:len(refs) // 2], refs[len(refs) // 2:]
    for i, (source, result) in enumerate(zip(sources, results)):
        if i >= n_head:
            result[...] = source[...].astype(result.dtype)
            continue
        parts = result.shape[0] // head_dim
        head_pad = source.shape[0] // parts
        for p in range(parts):
            result[p * head_dim:(p + 1) * head_dim, :] = source[p * head_pad:p * head_pad + head_dim, :].astype(result.dtype)


def finish_call(head_dim, head_pad, padded, plain):
    shapes = [(a.shape[0] // head_pad * head_dim, a.shape[1]) for a in padded] + [a.shape for a in plain]
    return pl.pallas_call(
        functools.partial(finish_body, head_dim, len(padded)),
        out_shape=[jax.ShapeDtypeStruct(shape, BF16) for shape in shapes],
        in_specs=[VMEM] * len(shapes),
        out_specs=[VMEM] * len(shapes),
        compiler_params=pltpu.CompilerParams(vmem_limit_bytes=67 * 1000 * 1000),
        name='results',
    )(*padded, *plain)


def device_block(tp_size, x_loc, y_loc, t_loc, len_loc, mod_table, w_qkv, b_qkv, w_o, b_o, w_q, b_q, w_kv, b_kv, w_co, b_co, w_1, b_1, w_2, b_2, g_loc):
    head_dim = w_q.shape[2]
    head_pad = -(-head_dim // LANES) * LANES
    wqkv, wq, wkv = [w.transpose(1, 2, 0)[0] for w in (w_qkv, w_q, w_kv)]
    wo, wco = w_o[0], w_co[0]

    gap = jnp.zeros((1, head_pad - head_dim), BF16)
    pieces = []
    for bias in (b_qkv, b_kv, b_q):
        for at in range(0, bias.shape[1], head_dim):
            pieces += [bias[:, at:at + head_dim], gap]
    biases = jnp.concatenate(pieces + [b[None] for b in (b_o, b_co, b_2, b_1)], axis=1).astype(F32)

    h1_all, y_all, x1_all, qkv, kv, q_cross, attn_val, cross_val, attn_prob, cross_prob, attn_total, x2_loc = forward_call(
        tp_size, 0, head_dim, head_pad, x_loc, y_loc, t_loc, mod_table, len_loc, biases, wqkv, wkv, wq, wo, wco)
    x_out, g_x2, g_cross, sums, g_w_1, g_w_2, g_b_1 = mlp_call(tp_size, 1, head_dim, x2_loc, g_loc, t_loc, mod_table, biases, w_1, w_2)
    g_x, g_y, sums, g_w_qkv, g_w_kv, g_w_q, g_w_o, g_w_co, g_b_qkv, g_b_kv, g_b_q = backward_call(
        tp_size, 2, head_dim, head_pad,
        [g_cross, g_x2, x_loc, attn_total, t_loc, mod_table, wqkv, wkv, wq, wo, wco, sums],
        [qkv, kv, q_cross, attn_val, cross_val, attn_prob, cross_prob], [h1_all, x1_all, y_all])

    g_w_qkv, g_w_kv, g_w_q, g_w_o, g_w_co, g_w_2, x_out, g_x, g_y = finish_call(
        head_dim, head_pad, [g_w_qkv, g_w_kv, g_w_q, g_w_o, g_w_co], [g_w_2, x_out, g_x, g_y])

    def head_weight(grad):
        return grad[None].transpose(2, 0, 1)

    def head_bias(grad):
        return grad.reshape(-1, head_pad)[:, :head_dim].reshape(1, -1).astype(BF16)

    vectors = sums.astype(BF16)
    return (x_out, g_x, g_y, sums[:6],
            head_weight(g_w_qkv), head_bias(g_b_qkv), g_w_o[None], vectors[B_O],
            head_weight(g_w_q), head_bias(g_b_q), head_weight(g_w_kv), head_bias(g_b_kv),
            g_w_co[None], vectors[B_CO],
            g_w_1.T.astype(BF16), g_b_1[0].astype(BF16), g_w_2, vectors[B_2])


def solution(mesh):
    token, heads, rows, whole = P('dp', 'tp'), P(None, 'tp'), P('tp'), P()
    group, group_rows, group_heads = P('dp'), P(('dp', 'tp')), P('dp', 'tp')
    in_specs = (token, token, group, group, whole, heads, rows, rows, whole, heads, rows, heads, rows, rows, whole, heads, rows, rows, whole, token)
    out_specs = (token, token, token, group, group_heads, group_rows, group_rows, group, group_heads, group_rows, group_heads, group_rows,
                 group_rows, group, group_heads, group_rows, group_rows, group)
    return jax.shard_map(functools.partial(device_block, mesh.shape['tp']), mesh=mesh, in_specs=in_specs, out_specs=out_specs, check_vma=False)
```

time: 529 us -> 493 us (0.932); the launches traced: 519 us -> 492 us
  other arithmetic: 20.8 us -> 4.38 us
  local copies, waits for them, and re-layouts: 22.7 us -> 9.16 us
    reduce_sum x5 -> x0, other arithmetic: 8.79 us -> none  [the longest x2 3.68 us: token_sum(): return jnp.sum(tensor.astype(F32), axis=(0, 1))]
where the time goes in v3:
time: 493 us; the launch traced here: 492 us
  Pallas kernels  478 us (97%)
  local copies, waits for them, and re-layouts  9.16 us (2%)
    pallas_call x1, Pallas kernels, backward_call(): pl.pallas_call(functools.partial(backward_body, tp_size, head_dim), out_s...  176 us
    pallas_call x1, Pallas kernels, forward_call(): pl.pallas_call(functools.partial(forward_body, tp_size, head_dim), out_sh...  163 us
    pallas_call x1, Pallas kernels, mlp_call(): pl.pallas_call(functools.partial(mlp_body, tp_size, head_dim), out_shape=...  133 us

profile of v3, /device:TPU:21, one launch (start us, length us, event | category | flops | bytes accessed | tf_op | source)
XLA Modules:
  0.0 492.3 jit_solution(2835446983943181585)
XLA Ops:
  0.7 0.7 concatenate.22
  1.3 0.8 fusion
  2.2 0.7 concatenate.19
  2.9 0.7 concatenate.20
  3.6 0.7 concatenate.21
  4.3 0.8 concatenate.23
  5.0 0.6 convert_element_type.43.refs_5_.refs_4_
  5.6 163.1 %attention_forward.1 = (bf16[8,256,1408]{2,1,0:T(8,128)(2,1)}, bf16[8,256,1408]{2,1,0:T(8,128)(2,1)}, bf16[8,256,1408]{2,1,0:T(8,128)(2,1)}, bf16[8,256,384]{2,1...) custom-call(bf16[8,16,1408]{2,1,0:T(8,128)(2,1)} %refs_2_.5, ...), custom_call_target="tpu_custom_call" | custom-call | tf_op jit(solution)/shard_map/attention_forward/pallas_call | solution.py:489
  168.8 133.1 %mlp_both_ways.1 = (bf16[8,16,1408]{2,1,0:T(8,128)(2,1)}, f32[8,16,1408]{2,1,0:T(8,128)}, bf16[8,16,1408]{2,1,0:T(8,128)(2,1)}, f32[16,1408]{1,0:T(8,128)}, f32[...) custom-call(bf16[8,16,1408]{2,1,0:T(8,128)(2,1)} %get-tuple-element.57.refs_0_, ...), custom_call_target="tpu_custom_call" | custom-call | tf_op jit(solution)/shard_map/mlp_both_ways/pallas_call | solution.py:884
  301.9 176.0 %attention_backward.1 = (bf16[8,16,1408]{2,1,0:T(8,128)(2,1)}, bf16[8,16,1408]{2,1,0:T(8,128)(2,1)}, f32[16,1408]{1,0:T(8,128)}, f32[384,1408]{1,0:T(8,128)}, f3...) custom-call(bf16[8,16,1408]{2,1,0:T(8,128)(2,1)} %get-tuple-element., ...), custom_call_target="tpu_custom_call" | custom-call | tf_op jit(solution)/shard_map/attention_backward/pallas_call | solution.py:757
  477.9 0.0 copy-start.3
  477.9 0.0 copy-start.2
  477.9 0.0 copy-start.1
  478.0 0.0 copy-start
  478.0 5.7 %results.1 = (bf16[264,1408]{1,0:T(8,128)(2,1)}, bf16[176,1408]{1,0:T(8,128)(2,1)}, bf16[88,1408]{1,0:T(8,128)(2,1)}, bf16[88,1408]{1,0:T(8,128)(2,1)}, bf16[88,...) custom-call(f32[384,1408]{1,0:T(8,128)} %get-tuple-element.72.refs_0, ...), custom_call_target="tpu_custom_call" | custom-call | tf_op jit(solution)/shard_map/results/pallas_call | solution.py:910
  483.7 0.0 copy-done.3
  483.7 0.5 convert.12
  484.2 0.0 copy-done.2
  484.2 0.6 convert_element_type.46
  484.9 0.0 copy-done.1
  484.9 0.7 convert_element_type.44
  485.5 0.0 copy-done
  485.5 0.6 convert_reduce_fusion
  486.1 0.9 convert_element_type.45
  487.0 1.4 slice.44
  488.4 0.7 slice_reduce_fusion
  489.1 1.7 convert_bitcast_fusion
  490.8 1.4 copy.38
  (3 shorter events, 0.0 us)
Async XLA Ops:
  477.9 5.8 %copy-start.3 = (f32[1,128]{1,0:T(1,128)S(1)}, f32[1,128]{1,0:T(1,128)}, u32[]{:S(2)}) copy-start(f32[1,128]{1,0:T(1,128)} %get-tuple-element.89) | copy-start | bytes 1540
  477.9 6.3 %copy-start.2 = (f32[1,256]{1,0:T(1,128)S(1)}, f32[1,256]{1,0:T(1,128)}, u32[]{:S(2)}) copy-start(f32[1,256]{1,0:T(1,128)} %get-tuple-element.91) | copy-start | bytes 3076
  477.9 6.9 %copy-start.1 = (f32[1,384]{1,0:T(1,128)S(1)}, f32[1,384]{1,0:T(1,128)}, u32[]{:S(2)}) copy-start(f32[1,384]{1,0:T(1,128)} %get-tuple-element.86) | copy-start | bytes 4612
  478.0 7.6 %copy-start = (f32[1,384]{1,0:T(1,128)S(1)}, f32[1,384]{1,0:T(1,128)}, u32[]{:S(2)}) copy-start(f32[1,384]{1,0:T(1,128)} %get-tuple-element.94) | copy-start | bytes 4612

commit v4 on v3

--- a/solution.py
+++ b/solution.py
@@ -27,7 +27,23 @@
 
 
 def dot(lhs, rhs, dims=NN):
-    return lax.dot_general(lhs, rhs, dims, preferred_element_type=F32)
+    return lax.dot_general(lhs, rhs[...], dims, preferred_element_type=F32)
+
+
+def add_to(acc, value):
+    acc[...] += value
+
+
+def clear(refs):
+    for ref in refs:
+        ref[...] = jnp.zeros_like(ref)
+
+
+def each(n, body):
+    def step(i, carry):
+        body(i)
+        return carry
+    lax.fori_loop(0, n, step, None)
 
 
 def cutter(refs):
@@ -257,14 +273,13 @@
 
 
 def loop_slots(n, hooks, body):
-    def step(slot, carry):
+    def step(slot):
         for s in range(n):
             @pl.when(slot == s)
             def _():
                 hooks(s)
         body(slot)
-        return carry
-    lax.fori_loop(0, n, step, None)
+    each(n, step)
 
 
 def gather_sems(tp_size):
@@ -286,6 +301,15 @@
         dest[i * head_pad + head_dim:(i + 1) * head_pad, :] = jnp.zeros((head_pad - head_dim, width), dest.dtype)
 
 
+def at_sample(mod, b):
+    return [mod[i, pl.ds(b, 1), :] for i in range(mod.shape[0])]
+
+
+def fill_mod(mod, t_ref, table_ref, rows):
+    for i, row in enumerate(rows):
+        mod[i] = mod_row(t_ref, table_ref, row)
+
+
 def mod_row(t_ref, table_ref, i):
     width = table_ref.shape[1]
     return table_ref[i:i + 1, :].astype(F32) + t_ref[:, i * width:(i + 1) * width].astype(F32)
@@ -335,15 +359,15 @@
 def forward_body(tp_size, head_dim, *refs):
     at = Place(tp_size)
     take = cutter(refs)
-    x, y, t_emb, table, lens, biases, wqkv_in, wkv_in, wq_in, wo_in, wco_in = take(11)
+    x, y, g, t_emb, table, lens, biases, wqkv_in, wkv_in, wq_in, wo_in, wco_in = take(12)
     bqkv, bkv, bq, bo, bco = biases_of(biases, FORWARD_BIASES, wqkv_in.shape[1], head_dim)
-    h1_out, y_out, x1_out = take(3)
+    h1_out, y_out, x1_out, g_out = take(4)
     outs, scratch = take(9), take(9)
     qkv, kv, q_c, val, cval, prob, cprob, atot, x2 = scratch
-    h1, x1, mod, fh, fy, fx, pbuf, sibr1, rcv1, sibr2, rcv2, wqkv, wkv, wq, wo, wco = take(16)
-    gather_h, gather_y, gather_x = [Gather(at, own, full, take(4)) for own, full in ((h1, fh), (y, fy), (x1, fx))]
+    h1, x1, gm, mod, fh, fy, fx, fg, pbuf, sibr1, rcv1, sibr2, rcv2, wqkv, wkv, wq, wo, wco = take(18)
+    gather_h, gather_y, gather_x, gather_g = [Gather(at, own, full, take(4)) for own, full in ((h1, fh), (y, fy), (x1, fx), (gm, fg))]
     scat_o, scat_c = [Scatter(at, pbuf, sibr, rcv, take(4)) for sibr, rcv in ((sibr1, rcv1), (sibr2, rcv2))]
-    saves, out_sem = take(3), refs[-1]
+    saves, out_sem = take(4), refs[-1]
     batch = x.shape[0]
     head_pad = wq.shape[0]
     scale = head_dim ** -0.5
@@ -351,16 +375,17 @@
     def out_copy(i):
         return pltpu.make_async_copy(scratch[i], outs[i], out_sem.at[i])
 
-    for i in range(3):
-        mod[i] = mod_row(t_emb, table, i)
-
-    def norm_one(b, carry):
+    at.greet_near()
+    gather_y.start()
+    fill_mod(mod, t_emb, table, (SHIFT1, SCALE1, GATE1, GATE2))
+
+    def norm_one(b):
+        shift, scale, _, gate = at_sample(mod, b)
         normed, _ = normalize(x[b])
-        h1[b] = (normed * (1.0 + mod[1, pl.ds(b, 1), :]) + mod[0, pl.ds(b, 1), :]).astype(BF16)
-        return carry
-
-    lax.fori_loop(0, batch, norm_one, None)
-    at.greet_near()
+        h1[b] = (normed * (1.0 + scale) + shift).astype(BF16)
+        gm[b] = (g[b].astype(F32) * gate).astype(BF16)
+
+    each(batch, norm_one)
     gather_h.start()
     for dest, source in ((wqkv, wqkv_in), (wkv, wkv_in), (wq, wq_in), (wo, wo_in), (wco, wco_in)):
         pad_rows(dest, source, head_dim)
@@ -369,21 +394,21 @@
         for g in gather_h.groups_before(s):
             gather_h.group(g)
         gather_h.ready(s)
-        if s == at.ring - 4:
-            gather_y.start()
+        if s in (3, 5):
+            gather_y.group(s // 2 - 1)
 
     def project(slot):
         rows = gather_h.rows(slot)
         gather_h.save_copy(h1_out, saves[0], slot).start()
-        put_rows(qkv, rows, dot(rows_of(fh, rows), wqkv[...], NT) + bqkv)
+        put_rows(qkv, rows, dot(rows_of(fh, rows), wqkv, NT) + bqkv)
 
     loop_slots(at.ring, hooks, project)
 
     def hooks(b):
         if b == batch // 2:
-            gather_y.group(0)
+            gather_y.group(2)
         if b == batch - 1:
-            gather_y.group(1)
+            gather_y.group(3)
 
     def attend_self(b):
         q_b, k_b, v_b = [qkv[b, :, i * head_pad:(i + 1) * head_pad] for i in range(3)]
@@ -395,16 +420,15 @@
     for i in (0, 3, 5):
         out_copy(i).start()
 
-    ynext = {2: 2, 3: 3, 5: 4, 6: 5, 7: 6}
-
     def hooks(s):
         if s >= 2 and s % 2 == 0:
             scat_o.step(s // 2 - 1)
-        if s in ynext:
-            gather_y.group(ynext[s])
+            gather_y.group(s // 2 + 3)
+        if s == at.ring - 1:
+            gather_g.start()
 
     def project_o(slot):
-        scat_o.put(slot, dot(rows_of(val, scat_o.rows(slot)), wo[...]))
+        scat_o.put(slot, dot(rows_of(val, scat_o.rows(slot)), wo))
 
     loop_slots(at.ring, hooks, project_o)
     scat_o.step(at.half - 1)
@@ -415,11 +439,11 @@
     scat_o.final(take_o)
     out_copy(7).start()
 
-    def x1_one(b, carry):
-        x1[b] = (x[b].astype(F32) + mod[2, pl.ds(b, 1), :] * atot[b]).astype(BF16)
-        return carry
-
-    lax.fori_loop(0, batch, x1_one, None)
+    def x1_one(b):
+        _, _, gate, _ = at_sample(mod, b)
+        x1[b] = (x[b].astype(F32) + gate * atot[b]).astype(BF16)
+
+    each(batch, x1_one)
 
     gather_x.start()
 
@@ -428,51 +452,71 @@
             gather_x.group(g)
         gather_y.ready(s)
         gather_x.ready(s)
+        if s >= 2 and s % 2 == 0:
+            gather_g.group(s // 2 - 1)
 
     def project(slot):
         rows = gather_x.rows(slot)
         gather_y.save_copy(y_out, saves[1], slot).start()
         gather_x.save_copy(x1_out, saves[2], slot).start()
-        put_rows(kv, rows, dot(rows_of(fy, rows), wkv[...], NT) + bkv)
-        put_rows(q_c, rows, dot(rows_of(fx, rows), wq[...], NT) + bq)
+        put_rows(kv, rows, dot(rows_of(fy, rows), wkv, NT) + bkv)
+        put_rows(q_c, rows, dot(rows_of(fx, rows), wq, NT) + bq)
 
     loop_slots(at.ring, hooks, project)
     scat_o.finish()
 
-    def attend_cross(b, carry):
+    def hooks(b):
+        if b == batch // 2:
+            gather_g.group(3)
+        if b == batch - 1:
+            gather_g.group(4)
+
+    def attend_cross(b):
         k_b, v_b = [kv[b, :, i * head_pad:(i + 1) * head_pad] for i in range(2)]
         scores = dot(q_c[b], k_b, NT) * scale
         slots = lax.broadcasted_iota(jnp.int32, scores.shape, 1)
         p_b = softmax_of(jnp.where(slots < lens[b], scores, MASK_FILL)).astype(BF16)
         cprob[b] = p_b
         cval[b] = dot(p_b, v_b).astype(BF16)
-        return carry
-
-    lax.fori_loop(0, batch, attend_cross, None)
+
+    loop_slots(batch, hooks, attend_cross)
     for i in (1, 2, 4, 6):
         out_copy(i).start()
+
+    def save_g(slots):
+        for slot in slots:
+            gather_g.ready(slot)
+            gather_g.save_copy(g_out, saves[3], slot).start()
 
     def hooks(s):
         if s >= 2 and s % 2 == 0:
             scat_c.step(s // 2 - 1)
+        if s == 3:
+            gather_g.group(5)
+            save_g(range(3))
+        if s == 5:
+            gather_g.group(6)
+            save_g((3, 4))
 
     def project_c(slot):
-        scat_c.put(slot, dot(rows_of(cval, scat_c.rows(slot)), wco[...]))
+        scat_c.put(slot, dot(rows_of(cval, scat_c.rows(slot)), wco))
 
     loop_slots(at.ring, hooks, project_c)
     scat_c.step(at.half - 1)
+    save_g(range(5, at.ring))
 
     def take_c(part, total):
         x2[part] = (x1[part].astype(F32) + total + bco).astype(BF16)
 
     scat_c.final(take_c)
     out_copy(8).start()
-    for stream in (gather_h, gather_y, gather_x, scat_c):
+    for stream in (gather_h, gather_y, gather_x, gather_g, scat_c):
         stream.finish()
     for slot in range(at.ring):
         gather_h.save_copy(h1_out, saves[0], slot).wait()
         gather_y.save_copy(y_out, saves[1], slot).wait()
         gather_x.save_copy(x1_out, saves[2], slot).wait()
+        gather_g.save_copy(g_out, saves[3], slot).wait()
     for i in range(9):
         out_copy(i).wait()
 
@@ -488,17 +532,16 @@
     sib, rcv = (ring, *local), (2, half, *local)
     return pl.pallas_call(
         functools.partial(forward_body, tp_size, head_dim),
-        out_shape=[jax.ShapeDtypeStruct(tokens(width), BF16)] * 3 + [jax.ShapeDtypeStruct(*k) for k in kept],
-        in_specs=[VMEM] * 4 + [pl.BlockSpec(memory_space=pltpu.SMEM)] + [VMEM] * (len(ins) - 5),
-        out_specs=[ANY] * (3 + len(kept)),
+        out_shape=[jax.ShapeDtypeStruct(tokens(width), BF16)] * 4 + [jax.ShapeDtypeStruct(*k) for k in kept],
+        in_specs=[VMEM] * 5 + [pl.BlockSpec(memory_space=pltpu.SMEM)] + [VMEM] * (len(ins) - 6),
+        out_specs=[ANY] * (4 + len(kept)),
         scratch_shapes=[pltpu.VMEM(*k) for k in kept] + [
-            pltpu.VMEM(local, BF16), pltpu.VMEM(local, BF16), pltpu.VMEM((3, batch, width), F32),
-            pltpu.VMEM(tokens(width), BF16), pltpu.VMEM(tokens(width), BF16), pltpu.VMEM(tokens(width), BF16),
+            *[pltpu.VMEM(local, BF16)] * 3, pltpu.VMEM((4, batch, width), F32), *[pltpu.VMEM(tokens(width), BF16)] * 4,
             pltpu.VMEM((ring, batch, 2 * n_loc, width), BF16),
             pltpu.VMEM(sib, BF16), pltpu.VMEM(rcv, BF16), pltpu.VMEM(sib, BF16), pltpu.VMEM(rcv, BF16)]
         + [pltpu.VMEM((n * head_pad, width), BF16) for n in (3, 2, 1, 1, 1)]
-        + gather_sems(tp_size) * 3 + scatter_sems(tp_size) * 2
-        + [pltpu.SemaphoreType.DMA((ring,))] * 3 + [pltpu.SemaphoreType.DMA((len(kept),))],
+        + gather_sems(tp_size) * 4 + scatter_sems(tp_size) * 2
+        + [pltpu.SemaphoreType.DMA((ring,))] * 4 + [pltpu.SemaphoreType.DMA((len(kept),))],
         compiler_params=KERNEL(collective_id=cid),
         name='attention_forward',
     )(*ins)
@@ -565,18 +608,19 @@
 def backward_body(tp_size, head_dim, *refs):
     at = Place(tp_size)
     take = cutter(refs)
-    g_cross, g_x2, x, atot, t_emb, table, wqkv_in, wkv_in, wq_in, wo_in, wco_in, sums_in = take(12)
-    loads, feeds = take(7), take(3)
-    g_x, g_y, sums_out = take(3)
+    g_cross, g_x2, x, x2, g, atot, t_emb, table, biases, w2, wqkv_in, wkv_in, wq_in, wo_in, wco_in, sums_in = take(16)
+    b2, = biases_of(biases, ('2',), x.shape[-1], head_dim)
+    loads, feeds = take(8), take(3)
+    x_out, g_x, g_y, sums_out = take(4)
     accs = take(8)
     gw_qkv, gw_kv, gw_q, gw_o, gw_co, gb_qkv, gb_kv, gb_q = accs
-    held = take(7)
-    qkv, kv, q_c, val, cval, prob, cprob = held
+    held = take(8)
+    qkv, kv, q_c, val, cval, prob, cprob, act_all = held
     full, pbuf, sibr1, rcv1, pbufy, sibr2, rcv2, wqkv, wkv, wq, wo, wco = take(12)
     g_val, g_qkv, g_kv, g_q, g_x1, g_h1, g_attn, mod, sums, got, mine, feed_a, feed_y = take(13)
     gather_c, gather_a = [Gather(at, own, full, take(4)) for own in (g_cross, g_attn)]
     near, far = (pbuf, sibr1, rcv1), (pbufy, sibr2, rcv2)
-    scat_q, scat_y, scat_h = [Scatter(at, *bufs, take(4)) for bufs in (near, far, near)]
+    scat_m, scat_q, scat_y, scat_h = [Scatter(at, *bufs, take(4)) for bufs in (far, near, far, near)]
     load_sem, *feed_sems = take(4)
     feed_h, feed_x, feed_yy = [
         RowFeed(source, buf, sem, scat.rows)
@@ -595,27 +639,40 @@
     gather_c.start()
     feed_x.copy(0).start()
     feed_yy.copy(0).start()
-    for i in range(3):
-        mod[i] = mod_row(t_emb, table, i)
+    fill_mod(mod, t_emb, table, (SHIFT1, SCALE1, GATE1, GATE2))
     for dest, source in ((wqkv, wqkv_in), (wkv, wkv_in), (wq, wq_in), (wo, wo_in), (wco, wco_in)):
         pad_rows(dest, source, head_dim)
     sums[...] = sums_in[...]
-    for acc in accs:
-        acc[...] = jnp.zeros_like(acc)
+    clear(accs)
     for i in range(len(held)):
         load_copy(i).wait()
+
+    def put_m(first, last):
+        def body(slot, carry):
+            scat_m.put(slot, dot(rows_of(act_all, scat_m.rows(slot)), w2))
+            return carry
+        lax.fori_loop(first, last, body, None)
 
     def out_back(gather, value, weight, acc):
         def body(slot):
             rows = gather.rows(slot)
             block = rows_of(full, rows)
-            put_rows(g_val, rows, dot(block, weight[...], NT))
-            acc[...] += dot(rows_of(value, rows), block, TN)
+            put_rows(g_val, rows, dot(block, weight, NT))
+            add_to(acc, dot(rows_of(value, rows), block, TN))
         return body
 
     def hooks(s):
         for g in gather_c.groups_before(s):
             gather_c.group(g)
+        if s == 1:
+            put_m(0, 3)
+            scat_m.step(0)
+        if s == 3:
+            put_m(3, 5)
+            scat_m.step(1)
+        if s == 5:
+            put_m(5, ring)
+            scat_m.step(2)
         gather_c.ready(s)
 
     loop_slots(ring, hooks, out_back(gather_c, cval, wco, gw_co))
@@ -628,38 +685,53 @@
         g_s = (p_f * (g_p - row_dot) * scale).astype(BF16)
         return dot(g_s, k_b).astype(BF16), dot(g_s, q_b, TN).astype(BF16), dot(p_b, g_b, TN).astype(BF16)
 
-    def cross_back(b, carry):
+    def hooks(b):
+        if b == batch // 2:
+            scat_m.step(half - 1)
+
+    def cross_back(b):
         parts = back_one(q_c[b], kv[b, :, :head_pad], kv[b, :, head_pad:], cprob[b], g_val[b])
         g_q[b] = parts[0]
         g_kv[b, :, :head_pad] = parts[1]
         g_kv[b, :, head_pad:] = parts[2]
-        return carry
-
-    lax.fori_loop(0, batch, cross_back, None)
+
+    loop_slots(batch, hooks, cross_back)
 
     def hooks(s):
         if s >= 2 and s % 2 == 0:
             scat_q.step(s // 2 - 1)
+        if s == 3:
+            scat_m.final(take_m)
+            scat_m.finish()
+
+    def take_m(part, total):
+        g_h1[part] = total + b2
 
     def put_q(slot):
         block = rows_of(g_q, scat_q.rows(slot))
-        scat_q.put(slot, dot(block, wq[...]))
-        gw_q[...] += dot(block, feed_x.take(slot, ring), TN)
-        gb_q[...] += row_sum(block.astype(F32))
+        scat_q.put(slot, dot(block, wq))
+        add_to(gw_q, dot(block, feed_x.take(slot, ring), TN))
+        add_to(gb_q, row_sum(block.astype(F32)))
 
     def put_y(first, last):
         def body(slot, carry):
             block = rows_of(g_kv, scat_y.rows(slot))
-            scat_y.put(slot, dot(block, wkv[...]))
-            gw_kv[...] += dot(block, feed_yy.take(slot, ring), TN)
-            gb_kv[...] += row_sum(block.astype(F32))
+            scat_y.put(slot, dot(block, wkv))
+            add_to(gw_kv, dot(block, feed_yy.take(slot, ring), TN))
+            add_to(gb_kv, row_sum(block.astype(F32)))
             return carry
         lax.fori_loop(first, last, body, None)
 
     loop_slots(ring, hooks, put_q)
     scat_q.step(half - 1)
-    put_y(0, 3)
-    scat_y.step(0)
+
+    def out_one(b, gate_sum):
+        gate, g_out, total = at_sample(mod, b)[-1], g[b].astype(F32), g_h1[b]
+        x_out[b] = (x2[b].astype(F32) + gate * total).astype(BF16)
+        return gate_sum + row_sum(g_out * total)
+
+    zero = jnp.zeros((1, width), F32)
+    sums[GATE2:GATE2 + 1, :] = lax.fori_loop(0, batch, out_one, zero)
 
     def take_q(part, total):
         g_x1[part] = g_x2[part] + total
@@ -674,13 +746,14 @@
         g_attn[b] = block
         return gate_sum + row_sum(rows * atot[b]), bias_sum + row_sum(block.astype(F32))
 
-    zero = jnp.zeros((1, width), F32)
     gate_sum, bias_sum = lax.fori_loop(0, batch, x1_back, (zero, zero))
     for row, value in ((GATE1, gate_sum), (B_O, bias_sum)):
         sums[row:row + 1, :] = value
 
     scat_q.finish()
     gather_a.start()
+    put_y(0, 3)
+    scat_y.step(0)
 
     def hooks(s):
         for g in gather_a.groups_before(s):
@@ -717,9 +790,9 @@
 
     def put_h(slot):
         block = rows_of(g_qkv, scat_h.rows(slot))
-        scat_h.put(slot, dot(block, wqkv[...]))
-        gw_qkv[...] += dot(block, feed_h.take(slot, ring), TN)
-        gb_qkv[...] += row_sum(block.astype(F32))
+        scat_h.put(slot, dot(block, wqkv))
+        add_to(gw_qkv, dot(block, feed_h.take(slot, ring), TN))
+        add_to(gb_qkv, row_sum(block.astype(F32)))
 
     loop_slots(ring, hooks, put_h)
     scat_h.step(half - 1)
@@ -752,7 +825,7 @@
     tokens = lambda last: (batch, n_tok, last)
     local = (batch, n_loc, width)
     sib, rcv, pbuf = (ring, *local), (2, half, *local), (ring, batch, 2 * n_loc, width)
-    outs = [(local, BF16), (local, BF16), ((n_sum, width), F32)]
+    outs = [(local, BF16)] * 3 + [((n_sum, width), F32)]
     outs += [((n * head_pad, width), F32) for n in (3, 2, 1, 1, 1)] + [((1, n * head_pad), F32) for n in (3, 2, 1)]
     return pl.pallas_call(
         functools.partial(backward_body, tp_size, head_dim),
@@ -763,10 +836,10 @@
         + [pltpu.VMEM(s, BF16) for s in (tokens(width), pbuf, sib, rcv, pbuf, sib, rcv)]
         + [pltpu.VMEM((n * head_pad, width), BF16) for n in (3, 2, 1, 1, 1)]
         + [pltpu.VMEM(tokens(n * head_pad), BF16) for n in (1, 3, 2, 1)]
-        + [pltpu.VMEM(local, F32), pltpu.VMEM(local, F32), pltpu.VMEM(local, BF16), pltpu.VMEM((3, batch, width), F32), pltpu.VMEM((n_sum, width), F32),
+        + [pltpu.VMEM(local, F32), pltpu.VMEM(local, F32), pltpu.VMEM(local, BF16), pltpu.VMEM((4, batch, width), F32), pltpu.VMEM((n_sum, width), F32),
            pltpu.VMEM((tp_size - 1, n_sum, LANES), F32), pltpu.VMEM((n_sum, LANES), F32)]
         + [pltpu.VMEM((2, batch, 2 * n_loc, width), BF16)] * 2
-        + gather_sems(tp_size) * 2 + scatter_sems(tp_size) * 3
+        + gather_sems(tp_size) * 2 + scatter_sems(tp_size) * 4
         + [pltpu.SemaphoreType.DMA((len(loads),))] + [pltpu.SemaphoreType.DMA((2,))] * 3
         + [pltpu.SemaphoreType.DMA((n,)) for n in (width // LANES, tp_size - 1, tp_size - 1, width // LANES)],
         compiler_params=KERNEL(collective_id=cid),
@@ -777,117 +850,96 @@
 def mlp_body(tp_size, head_dim, *refs):
     at = Place(tp_size)
     take = cutter(refs)
-    x2, g, t_emb, table, biases, w1, w2 = take(7)
-    b1, b2 = biases_of(biases, ('1', '2'), x2.shape[-1], head_dim)
-    x_out, g_x2, g_cross, sums, gw_1, gw_2, gb_1 = take(7)
-    h2, gm, mod, fh, fg, act_all, hid_all, g_h2, total = take(9)
-    ring_bufs = take(3), take(3)
-    gather_h, gather_g = [Gather(at, own, full, take(4)) for own, full in ((h2, fh), (gm, fg))]
-    scat_h, scat_m = [Scatter(at, *bufs, take(4)) for bufs in ring_bufs]
+    x2, g, t_emb, table, biases, w1, w2, g_all = take(8)
+    b1, = biases_of(biases, ('1',), x2.shape[-1], head_dim)
+    act_all, g_x2, g_cross, sums, gw_1, gw_2, gb_1 = take(7)
+    h2, mod, fh, hid_all, g_h2, feed, *bufs = take(9)
+    gather_h, scat_h = Gather(at, h2, fh, take(4)), Scatter(at, *bufs, take(4))
+    feed_g = RowFeed(g_all, feed, refs[-1], gather_h.rows)
     batch = x2.shape[0]
 
-    for i in range(3):
-        mod[i] = mod_row(t_emb, table, 3 + i)
-
-    def shift_scale_gate(b):
-        return [mod[i, pl.ds(b, 1), :] for i in range(3)]
-
-    def norm_one(b, carry):
-        shift, scale, gate = shift_scale_gate(b)
+    feed_g.copy(0).start()
+    at.greet_near()
+    fill_mod(mod, t_emb, table, (SHIFT2, SCALE2, GATE2))
+
+    def norm_one(b):
+        shift, scale, _ = at_sample(mod, b)
         normed, _ = normalize(x2[b])
         h2[b] = (normed * (1.0 + scale) + shift).astype(BF16)
-        gm[b] = (g[b].astype(F32) * gate).astype(BF16)
-        return carry
-
-    lax.fori_loop(0, batch, norm_one, None)
-    at.greet_near()
+
+    each(batch, norm_one)
     gather_h.start()
-    gather_g.start()
-    for acc in (gw_1, gw_2, gb_1):
-        acc[...] = jnp.zeros_like(acc)
+    clear((gw_1, gw_2, gb_1, sums))
 
     def hooks(s):
-        for stream in (gather_h, gather_g):
-            for group in stream.groups_before(s):
-                stream.group(group)
+        for group in gather_h.groups_before(s):
+            gather_h.group(group)
         gather_h.ready(s)
-        gather_g.ready(s)
 
     def mlp(slot):
         rows = gather_h.rows(slot)
-        h2_blk, g_blk = rows_of(fh, rows), rows_of(fg, rows)
-        act, slope = gelu_pair(dot(h2_blk, w1[...]) + b1)
+        h2_blk, g_blk = rows_of(fh, rows), feed_g.take(slot, at.ring)
+        act, slope = gelu_pair(dot(h2_blk, w1) + b1)
         act = act.astype(BF16)
         put_rows(act_all, rows, act)
-        g_hidden = dot(g_blk, w2[...], NT) * slope
-        gb_1[...] += row_sum(g_hidden)
+        g_hidden = dot(g_blk, w2, NT) * slope
+        add_to(gb_1, row_sum(g_hidden))
         g_hidden = g_hidden.astype(BF16)
         put_rows(hid_all, rows, g_hidden)
-        gw_1[...] += dot(g_hidden, h2_blk, TN)
-        gw_2[...] += dot(act, g_blk, TN)
+        add_to(gw_1, dot(g_hidden, h2_blk, TN))
+        add_to(gw_2, dot(act, g_blk, TN))
 
     loop_slots(at.ring, hooks, mlp)
 
     def hooks(s):
         if s >= 2 and s % 2 == 0:
             scat_h.step(s // 2 - 1)
-            scat_m.step(s // 2 - 1)
-
-    def put_both(slot):
-        rows = scat_h.rows(slot)
-        scat_h.put(slot, dot(rows_of(hid_all, rows), w1[...], NT))
-        scat_m.put(slot, dot(rows_of(act_all, rows), w2[...]))
-
-    loop_slots(at.ring, hooks, put_both)
+
+    def put_h(slot):
+        scat_h.put(slot, dot(rows_of(hid_all, scat_h.rows(slot)), w1, NT))
+
+    loop_slots(at.ring, hooks, put_h)
     scat_h.step(at.half - 1)
-    scat_m.step(at.half - 1)
 
     def take_h(part, value):
         g_h2[part] = value
 
-    def take_m(part, value):
-        total[part] = value + b2
-
     scat_h.final(take_h)
-    scat_m.final(take_m)
 
     def back_one(b, carry):
-        _, scale, gate = shift_scale_gate(b)
-        g_out, mlp_total, grad = g[b].astype(F32), total[b], g_h2[b]
-        x_out[b] = (x2[b].astype(F32) + gate * mlp_total).astype(BF16)
+        _, scale, gate = at_sample(mod, b)
+        g_out, grad = g[b].astype(F32), g_h2[b]
         normed, inv_std = normalize(x2[b])
         back = g_out + normalize_back(normed, inv_std, grad * (1.0 + scale))
         g_x2[b] = back
         g_cross[b] = back.astype(BF16)
-        terms = grad, grad * normed, g_out * mlp_total, back.astype(BF16).astype(F32), gm[b].astype(F32)
+        terms = grad, grad * normed, back.astype(BF16).astype(F32), (g_out * gate).astype(BF16).astype(F32)
         return tuple(c + row_sum(t) for c, t in zip(carry, terms))
 
     zero = jnp.zeros((1, x2.shape[-1]), F32)
-    sums[...] = jnp.zeros_like(sums)
-    found = lax.fori_loop(0, batch, back_one, (zero,) * 5)
-    for row, value in zip((SHIFT2, SCALE2, GATE2, B_CO, B_2), found):
+    found = lax.fori_loop(0, batch, back_one, (zero,) * 4)
+    for row, value in zip((SHIFT2, SCALE2, B_CO, B_2), found):
         sums[row:row + 1, :] = value
-    for stream in (gather_h, gather_g, scat_h, scat_m):
-        stream.finish()
+    gather_h.finish()
+    scat_h.finish()
 
 
 def mlp_call(tp_size, cid, head_dim, *ins):
     batch, n_loc, width = ins[0].shape
-    ffn = ins[-1].shape[0]
+    ffn = ins[-2].shape[0]
     n_tok = n_loc * tp_size
     ring, half = tp_size // 2, tp_size // 4
     local, tokens, hidden = (batch, n_loc, width), (batch, n_tok, width), (batch, n_tok, ffn)
-    bufs = (ring, batch, 2 * n_loc, width), (ring, *local), (2, half, *local)
-    outs = [(local, BF16), (local, F32), (local, BF16), ((SUM_ROWS, width), F32), ((ffn, width), F32), ((ffn, width), F32), ((1, ffn), F32)]
-    scratch = [(local, BF16), (local, BF16), ((3, batch, width), F32), (tokens, BF16), (tokens, BF16), (hidden, BF16), (hidden, BF16),
-               (local, F32), (local, F32)]
+    chip = batch, 2 * n_loc, width
+    outs = [(hidden, BF16), (local, F32), (local, BF16), ((SUM_ROWS, width), F32), ((ffn, width), F32), ((ffn, width), F32), ((1, ffn), F32)]
+    scratch = [(local, BF16), ((3, batch, width), F32), (tokens, BF16), (hidden, BF16), (local, F32), ((2, *chip), BF16),
+               ((ring, *chip), BF16), ((ring, *local), BF16), ((2, half, *local), BF16)]
     return pl.pallas_call(
         functools.partial(mlp_body, tp_size, head_dim),
         out_shape=[jax.ShapeDtypeStruct(*o) for o in outs],
-        in_specs=[VMEM] * len(ins),
+        in_specs=[VMEM] * (len(ins) - 1) + [ANY],
         out_specs=[VMEM] * len(outs),
-        scratch_shapes=[pltpu.VMEM(*k) for k in scratch] + [pltpu.VMEM(k, BF16) for k in bufs * 2]
-        + gather_sems(tp_size) * 2 + scatter_sems(tp_size) * 2,
+        scratch_shapes=[pltpu.VMEM(*k) for k in scratch] + gather_sems(tp_size) + scatter_sems(tp_size) + [pltpu.SemaphoreType.DMA((2,))],
         compiler_params=KERNEL(collective_id=cid),
         name='mlp_both_ways',
     )(*ins)
@@ -930,13 +982,14 @@
             pieces += [bias[:, at:at + head_dim], gap]
     biases = jnp.concatenate(pieces + [b[None] for b in (b_o, b_co, b_2, b_1)], axis=1).astype(F32)
 
-    h1_all, y_all, x1_all, qkv, kv, q_cross, attn_val, cross_val, attn_prob, cross_prob, attn_total, x2_loc = forward_call(
-        tp_size, 0, head_dim, head_pad, x_loc, y_loc, t_loc, mod_table, len_loc, biases, wqkv, wkv, wq, wo, wco)
-    x_out, g_x2, g_cross, sums, g_w_1, g_w_2, g_b_1 = mlp_call(tp_size, 1, head_dim, x2_loc, g_loc, t_loc, mod_table, biases, w_1, w_2)
-    g_x, g_y, sums, g_w_qkv, g_w_kv, g_w_q, g_w_o, g_w_co, g_b_qkv, g_b_kv, g_b_q = backward_call(
+    h1_all, y_all, x1_all, g_all, qkv, kv, q_cross, attn_val, cross_val, attn_prob, cross_prob, attn_total, x2_loc = forward_call(
+        tp_size, 0, head_dim, head_pad, x_loc, y_loc, g_loc, t_loc, mod_table, len_loc, biases, wqkv, wkv, wq, wo, wco)
+    gelu_out, g_x2, g_cross, sums, g_w_1, g_w_2, g_b_1 = mlp_call(
+        tp_size, 1, head_dim, x2_loc, g_loc, t_loc, mod_table, biases, w_1, w_2, g_all)
+    x_out, g_x, g_y, sums, g_w_qkv, g_w_kv, g_w_q, g_w_o, g_w_co, g_b_qkv, g_b_kv, g_b_q = backward_call(
         tp_size, 2, head_dim, head_pad,
-        [g_cross, g_x2, x_loc, attn_total, t_loc, mod_table, wqkv, wkv, wq, wo, wco, sums],
-        [qkv, kv, q_cross, attn_val, cross_val, attn_prob, cross_prob], [h1_all, x1_all, y_all])
+        [g_cross, g_x2, x_loc, x2_loc, g_loc, attn_total, t_loc, mod_table, biases, w_2, wqkv, wkv, wq, wo, wco, sums],
+        [qkv, kv, q_cross, attn_val, cross_val, attn_prob, cross_prob, gelu_out], [h1_all, x1_all, y_all])
 
     g_w_qkv, g_w_kv, g_w_q, g_w_o, g_w_co, g_w_2, x_out, g_x, g_y = finish_call(
         head_dim, head_pad, [g_w_qkv, g_w_kv, g_w_q, g_w_o, g_w_co], [g_w_2, x_out, g_x, g_y])

time: 493 us -> 488 us (0.990); the launches traced: 492 us -> 478 us
  Pallas kernels: 478 us -> 464 us
    pallas_call x1, Pallas kernels: 133 us -> 78.1 us  [mlp_call(): pl.pallas_call(functools.partial(mlp_body, tp_size, head_dim), out_shape=...]
    pallas_call x1, Pallas kernels: 163 us -> 184 us  [forward_call(): pl.pallas_call(functools.partial(forward_body, tp_size, head_dim), out_sh...]
    pallas_call x1, Pallas kernels: 176 us -> 196 us  [backward_call(): pl.pallas_call(functools.partial(backward_body, tp_size, head_dim), out_s...]
where the time goes in v4:
time: 488 us; the launch traced here: 478 us
  Pallas kernels  464 us (95%)
  local copies, waits for them, and re-layouts  9.16 us (2%)
    pallas_call x1, Pallas kernels, backward_call(): pl.pallas_call(functools.partial(backward_body, tp_size, head_dim), out_s...  196 us
    pallas_call x1, Pallas kernels, forward_call(): pl.pallas_call(functools.partial(forward_body, tp_size, head_dim), out_sh...  184 us
    pallas_call x1, Pallas kernels, mlp_call(): pl.pallas_call(functools.partial(mlp_body, tp_size, head_dim), out_shape=...  78.1 us

profile of v4, /device:TPU:21, one launch (start us, length us, event | category | flops | bytes accessed | tf_op | source)
XLA Modules:
  0.0 478.1 jit_solution(11444100124164484010)
XLA Ops:
  0.7 0.7 concatenate.22
  1.3 0.8 fusion
  2.2 0.7 concatenate.19
  2.9 0.7 concatenate.20
  3.6 0.7 concatenate.21
  4.3 0.8 concatenate.23
  5.0 0.6 convert_element_type.43.refs_6_.refs_4_.refs_8_
  5.6 183.6 %attention_forward.1 = (bf16[8,256,1408]{2,1,0:T(8,128)(2,1)}, bf16[8,256,1408]{2,1,0:T(8,128)(2,1)}, bf16[8,256,1408]{2,1,0:T(8,128)(2,1)}, bf16[8,256,1408]{2,...) custom-call(bf16[8,16,1408]{2,1,0:T(8,128)(2,1)} %refs_2_.5, ...), custom_call_target="tpu_custom_call" | custom-call | tf_op jit(solution)/shard_map/attention_forward/pallas_call | solution.py:533
  189.3 78.1 %mlp_both_ways.1 = (bf16[8,256,384]{2,1,0:T(8,128)(2,1)}, f32[8,16,1408]{2,1,0:T(8,128)}, bf16[8,16,1408]{2,1,0:T(8,128)(2,1)}, f32[16,1408]{1,0:T(8,128)}, f32[...) custom-call(bf16[8,16,1408]{2,1,0:T(8,128)(2,1)} %get-tuple-element.59.refs_0_.refs_3_, ...), custom_call_target="tpu_custom_call" | custom-call | tf_op jit(solution)/shard_map/mlp_both_ways/pallas_call | solution.py:937
  267.3 196.4 %attention_backward.1 = (bf16[8,16,1408]{2,1,0:T(8,128)(2,1)}, bf16[8,16,1408]{2,1,0:T(8,128)(2,1)}, bf16[8,16,1408]{2,1,0:T(8,128)(2,1)}, f32[16,1408]{1,0:T(8,...) custom-call(bf16[8,16,1408]{2,1,0:T(8,128)(2,1)} %get-tuple-element., ...), custom_call_target="tpu_custom_call" | custom-call | tf_op jit(solution)/shard_map/attention_backward/pallas_call | solution.py:830
  463.7 0.0 copy-start.3
  463.8 0.0 copy-start.2
  463.8 0.0 copy-start.1
  463.8 0.0 copy-start
  463.8 5.6 %results.1 = (bf16[264,1408]{1,0:T(8,128)(2,1)}, bf16[176,1408]{1,0:T(8,128)(2,1)}, bf16[88,1408]{1,0:T(8,128)(2,1)}, bf16[88,1408]{1,0:T(8,128)(2,1)}, bf16[88,...) custom-call(f32[384,1408]{1,0:T(8,128)} %get-tuple-element.76.refs_0, ...), custom_call_target="tpu_custom_call" | custom-call | tf_op jit(solution)/shard_map/results/pallas_call | solution.py:962
  469.4 0.0 copy-done.3
  469.4 0.5 convert.12
  469.9 0.0 copy-done.2
  469.9 0.6 convert_element_type.46
  470.6 0.0 copy-done.1
  470.6 0.7 convert_element_type.44
  471.2 0.0 copy-done
  471.2 0.6 convert_reduce_fusion
  471.8 0.9 convert_element_type.45
  472.7 1.4 slice.44
  474.1 0.7 slice_reduce_fusion
  474.8 1.7 convert_bitcast_fusion
  476.5 1.4 copy.38
  (3 shorter events, 0.0 us)
Async XLA Ops:
  463.7 5.6 %copy-start.3 = (f32[1,128]{1,0:T(1,128)S(1)}, f32[1,128]{1,0:T(1,128)}, u32[]{:S(2)}) copy-start(f32[1,128]{1,0:T(1,128)} %get-tuple-element.93) | copy-start | bytes 1540
  463.8 6.1 %copy-start.2 = (f32[1,256]{1,0:T(1,128)S(1)}, f32[1,256]{1,0:T(1,128)}, u32[]{:S(2)}) copy-start(f32[1,256]{1,0:T(1,128)} %get-tuple-element.95) | copy-start | bytes 3076
  463.8 6.8 %copy-start.1 = (f32[1,384]{1,0:T(1,128)S(1)}, f32[1,384]{1,0:T(1,128)}, u32[]{:S(2)}) copy-start(f32[1,384]{1,0:T(1,128)} %get-tuple-element.90) | copy-start | bytes 4612
  463.8 7.5 %copy-start = (f32[1,384]{1,0:T(1,128)S(1)}, f32[1,384]{1,0:T(1,128)}, u32[]{:S(2)}) copy-start(f32[1,384]{1,0:T(1,128)} %get-tuple-element.98) | copy-start | bytes 4612

commit v5 on v4

--- a/solution.py
+++ b/solution.py
@@ -19,7 +19,6 @@
 TN = (((0,), (0,)), ((), ()))
 SHIFT1, SCALE1, GATE1, SHIFT2, SCALE2, GATE2, B_O, B_CO, B_2 = range(9)
 SUM_ROWS = 16
-FORWARD_BIASES = 'qkv', 'kv', 'q', 'o', 'co'
 UP, DOWN = HALVES = WAYS = 0, 1
 SEND, TAKE = True, False
 KERNEL = functools.partial(pltpu.CompilerParams, has_side_effects=True, vmem_limit_bytes=67 * 1000 * 1000)
@@ -51,16 +50,14 @@
     return lambda n: list(itertools.islice(left, n))
 
 
-def biases_of(packed, names, width, head_dim):
-    return [packed[:, at:at + size] for at, size in (bias_place(name, width, head_dim, packed.shape[1]) for name in names)]
-
-
-def bias_place(name, width, head_dim, total):
-    head_pad = -(-head_dim // LANES) * LANES
-    sizes = {'qkv': 3 * head_pad, 'kv': 2 * head_pad, 'q': head_pad, 'o': width, 'co': width, '2': width}
-    sizes['1'] = total - sum(sizes.values())
-    names = list(sizes)
-    return sum(sizes[n] for n in names[:names.index(name)]), sizes[name]
+def padded_bias(ref, head_dim, head_pad):
+    gap = jnp.zeros((1, head_pad - head_dim), F32)
+    parts = [ref[:, p:p + head_dim].astype(F32) for p in range(0, ref.shape[1], head_dim)]
+    return jnp.concatenate([piece for part in parts for piece in (part, gap)], axis=1)
+
+
+def row_of(ref):
+    return ref[...].astype(F32).reshape(1, -1)
 
 
 class Place:
@@ -359,8 +356,8 @@
 def forward_body(tp_size, head_dim, *refs):
     at = Place(tp_size)
     take = cutter(refs)
-    x, y, g, t_emb, table, lens, biases, wqkv_in, wkv_in, wq_in, wo_in, wco_in = take(12)
-    bqkv, bkv, bq, bo, bco = biases_of(biases, FORWARD_BIASES, wqkv_in.shape[1], head_dim)
+    x, y, g, t_emb, table, lens, *bias_in = take(11)
+    wqkv_in, wkv_in, wq_in, wo_in, wco_in = take(5)
     h1_out, y_out, x1_out, g_out = take(4)
     outs, scratch = take(9), take(9)
     qkv, kv, q_c, val, cval, prob, cprob, atot, x2 = scratch
@@ -370,6 +367,8 @@
     saves, out_sem = take(4), refs[-1]
     batch = x.shape[0]
     head_pad = wq.shape[0]
+    bqkv, bkv, bq = [padded_bias(ref, head_dim, head_pad) for ref in bias_in[:3]]
+    bo, bco = [row_of(ref) for ref in bias_in[3:]]
     scale = head_dim ** -0.5
 
     def out_copy(i):
@@ -608,8 +607,8 @@
 def backward_body(tp_size, head_dim, *refs):
     at = Place(tp_size)
     take = cutter(refs)
-    g_cross, g_x2, x, x2, g, atot, t_emb, table, biases, w2, wqkv_in, wkv_in, wq_in, wo_in, wco_in, sums_in = take(16)
-    b2, = biases_of(biases, ('2',), x.shape[-1], head_dim)
+    g_cross, g_x2, x, x2, g, atot, t_emb, table, b2_in, w2, wqkv_in, wkv_in, wq_in, wo_in, wco_in, sums_in = take(16)
+    b2 = row_of(b2_in)
     loads, feeds = take(8), take(3)
     x_out, g_x, g_y, sums_out = take(4)
     accs = take(8)
@@ -647,35 +646,26 @@
     for i in range(len(held)):
         load_copy(i).wait()
 
-    def put_m(first, last):
-        def body(slot, carry):
-            scat_m.put(slot, dot(rows_of(act_all, scat_m.rows(slot)), w2))
-            return carry
-        lax.fori_loop(first, last, body, None)
-
-    def out_back(gather, value, weight, acc):
+    def put_m(slot):
+        scat_m.put(slot, dot(rows_of(act_all, scat_m.rows(slot)), w2))
+
+    def out_back(gather, value, weight, acc, beside):
         def body(slot):
             rows = gather.rows(slot)
             block = rows_of(full, rows)
             put_rows(g_val, rows, dot(block, weight, NT))
             add_to(acc, dot(rows_of(value, rows), block, TN))
+            beside(slot)
         return body
 
     def hooks(s):
         for g in gather_c.groups_before(s):
             gather_c.group(g)
-        if s == 1:
-            put_m(0, 3)
-            scat_m.step(0)
-        if s == 3:
-            put_m(3, 5)
-            scat_m.step(1)
-        if s == 5:
-            put_m(5, ring)
-            scat_m.step(2)
+        if s >= 2 and s % 2 == 0:
+            scat_m.step(s // 2 - 1)
         gather_c.ready(s)
 
-    loop_slots(ring, hooks, out_back(gather_c, cval, wco, gw_co))
+    loop_slots(ring, hooks, out_back(gather_c, cval, wco, gw_co, put_m))
     gather_c.finish()
 
     def back_one(q_b, k_b, v_b, p_b, g_b):
@@ -713,14 +703,11 @@
         add_to(gw_q, dot(block, feed_x.take(slot, ring), TN))
         add_to(gb_q, row_sum(block.astype(F32)))
 
-    def put_y(first, last):
-        def body(slot, carry):
-            block = rows_of(g_kv, scat_y.rows(slot))
-            scat_y.put(slot, dot(block, wkv))
-            add_to(gw_kv, dot(block, feed_yy.take(slot, ring), TN))
-            add_to(gb_kv, row_sum(block.astype(F32)))
-            return carry
-        lax.fori_loop(first, last, body, None)
+    def put_y(slot):
+        block = rows_of(g_kv, scat_y.rows(slot))
+        scat_y.put(slot, dot(block, wkv))
+        add_to(gw_kv, dot(block, feed_yy.take(slot, ring), TN))
+        add_to(gb_kv, row_sum(block.astype(F32)))
 
     loop_slots(ring, hooks, put_q)
     scat_q.step(half - 1)
@@ -752,21 +739,15 @@
 
     scat_q.finish()
     gather_a.start()
-    put_y(0, 3)
-    scat_y.step(0)
 
     def hooks(s):
         for g in gather_a.groups_before(s):
             gather_a.group(g)
-        if s == 1:
-            put_y(3, 5)
-            scat_y.step(1)
-        if s == 5:
-            put_y(5, ring)
-            scat_y.step(2)
+        if s >= 2 and s % 2 == 0:
+            scat_y.step(s // 2 - 1)
         gather_a.ready(s)
 
-    loop_slots(ring, hooks, out_back(gather_a, val, wo, gw_o))
+    loop_slots(ring, hooks, out_back(gather_a, val, wo, gw_o, put_y))
 
     def hooks(b):
         if b == batch // 4:
@@ -847,15 +828,15 @@
     )(*ins, *loads, *feeds)
 
 
-def mlp_body(tp_size, head_dim, *refs):
+def mlp_body(tp_size, *refs):
     at = Place(tp_size)
     take = cutter(refs)
-    x2, g, t_emb, table, biases, w1, w2, g_all = take(8)
-    b1, = biases_of(biases, ('1',), x2.shape[-1], head_dim)
+    x2, g, t_emb, table, b1_in, w1, w2, g_all = take(8)
+    b1 = row_of(b1_in)
     act_all, g_x2, g_cross, sums, gw_1, gw_2, gb_1 = take(7)
     h2, mod, fh, hid_all, g_h2, feed, *bufs = take(9)
     gather_h, scat_h = Gather(at, h2, fh, take(4)), Scatter(at, *bufs, take(4))
-    feed_g = RowFeed(g_all, feed, refs[-1], gather_h.rows)
+    feed_g, feed_again = [RowFeed(g_all, feed, refs[-1], stream.rows) for stream in (gather_h, scat_h)]
     batch = x2.shape[0]
 
     feed_g.copy(0).start()
@@ -886,17 +867,20 @@
         add_to(gb_1, row_sum(g_hidden))
         g_hidden = g_hidden.astype(BF16)
         put_rows(hid_all, rows, g_hidden)
-        add_to(gw_1, dot(g_hidden, h2_blk, TN))
-        add_to(gw_2, dot(act, g_blk, TN))
 
     loop_slots(at.ring, hooks, mlp)
+    feed_again.copy(0).start()
 
     def hooks(s):
         if s >= 2 and s % 2 == 0:
             scat_h.step(s // 2 - 1)
 
     def put_h(slot):
-        scat_h.put(slot, dot(rows_of(hid_all, scat_h.rows(slot)), w1, NT))
+        rows = scat_h.rows(slot)
+        g_hidden = rows_of(hid_all, rows)
+        scat_h.put(slot, dot(g_hidden, w1, NT))
+        add_to(gw_1, dot(rows_of(fh, rows), g_hidden, TN))
+        add_to(gw_2, dot(rows_of(act_all, rows), feed_again.take(slot, at.ring), TN))
 
     loop_slots(at.ring, hooks, put_h)
     scat_h.step(at.half - 1)
@@ -924,18 +908,18 @@
     scat_h.finish()
 
 
-def mlp_call(tp_size, cid, head_dim, *ins):
+def mlp_call(tp_size, cid, *ins):
     batch, n_loc, width = ins[0].shape
     ffn = ins[-2].shape[0]
     n_tok = n_loc * tp_size
     ring, half = tp_size // 2, tp_size // 4
     local, tokens, hidden = (batch, n_loc, width), (batch, n_tok, width), (batch, n_tok, ffn)
     chip = batch, 2 * n_loc, width
-    outs = [(hidden, BF16), (local, F32), (local, BF16), ((SUM_ROWS, width), F32), ((ffn, width), F32), ((ffn, width), F32), ((1, ffn), F32)]
+    outs = [(hidden, BF16), (local, F32), (local, BF16), ((SUM_ROWS, width), F32), ((width, ffn), F32), ((ffn, width), F32), ((1, ffn), F32)]
     scratch = [(local, BF16), ((3, batch, width), F32), (tokens, BF16), (hidden, BF16), (local, F32), ((2, *chip), BF16),
                ((ring, *chip), BF16), ((ring, *local), BF16), ((2, half, *local), BF16)]
     return pl.pallas_call(
-        functools.partial(mlp_body, tp_size, head_dim),
+        functools.partial(mlp_body, tp_size),
         out_shape=[jax.ShapeDtypeStruct(*o) for o in outs],
         in_specs=[VMEM] * (len(ins) - 1) + [ANY],
         out_specs=[VMEM] * len(outs),
@@ -945,28 +929,30 @@
     )(*ins)
 
 
-def finish_body(head_dim, n_head, *refs):
+def finish_body(head_dim, head_pad, n_head, n_bias, *refs):
     sources, results = refs[:len(refs) // 2], refs[len(refs) // 2:]
     for i, (source, result) in enumerate(zip(sources, results)):
-        if i >= n_head:
+        if i < n_head:
+            for p in range(result.shape[0] // head_dim):
+                result[p * head_dim:(p + 1) * head_dim, :] = source[p * head_pad:p * head_pad + head_dim, :].astype(result.dtype)
+        elif i < n_head + n_bias:
+            parts = [source[:, p:p + head_dim] for p in range(0, source.shape[1], head_pad)]
+            result[...] = jnp.concatenate(parts, axis=1).astype(result.dtype)
+        else:
             result[...] = source[...].astype(result.dtype)
-            continue
-        parts = result.shape[0] // head_dim
-        head_pad = source.shape[0] // parts
-        for p in range(parts):
-            result[p * head_dim:(p + 1) * head_dim, :] = source[p * head_pad:p * head_pad + head_dim, :].astype(result.dtype)
-
-
-def finish_call(head_dim, head_pad, padded, plain):
-    shapes = [(a.shape[0] // head_pad * head_dim, a.shape[1]) for a in padded] + [a.shape for a in plain]
+
+
+def finish_call(head_dim, head_pad, padded, biases, plain):
+    shapes = [(a.shape[0] // head_pad * head_dim, a.shape[1]) for a in padded]
+    shapes += [(1, b.shape[1] // head_pad * head_dim) for b in biases] + [a.shape for a in plain]
     return pl.pallas_call(
-        functools.partial(finish_body, head_dim, len(padded)),
+        functools.partial(finish_body, head_dim, head_pad, len(padded), len(biases)),
         out_shape=[jax.ShapeDtypeStruct(shape, BF16) for shape in shapes],
         in_specs=[VMEM] * len(shapes),
         out_specs=[VMEM] * len(shapes),
-        compiler_params=pltpu.CompilerParams(vmem_limit_bytes=67 * 1000 * 1000),
+        compiler_params=pltpu.CompilerParams(vmem_limit_bytes=60 * 1000 * 1000),
         name='results',
-    )(*padded, *plain)
+    )(*padded, *biases, *plain)
 
 
 def device_block(tp_size, x_loc, y_loc, t_loc, len_loc, mod_table, w_qkv, b_qkv, w_o, b_o, w_q, b_q, w_kv, b_kv, w_co, b_co, w_1, b_1, w_2, b_2, g_loc):
@@ -975,37 +961,22 @@
     wqkv, wq, wkv = [w.transpose(1, 2, 0)[0] for w in (w_qkv, w_q, w_kv)]
     wo, wco = w_o[0], w_co[0]
 
-    gap = jnp.zeros((1, head_pad - head_dim), BF16)
-    pieces = []
-    for bias in (b_qkv, b_kv, b_q):
-        for at in range(0, bias.shape[1], head_dim):
-            pieces += [bias[:, at:at + head_dim], gap]
-    biases = jnp.concatenate(pieces + [b[None] for b in (b_o, b_co, b_2, b_1)], axis=1).astype(F32)
-
     h1_all, y_all, x1_all, g_all, qkv, kv, q_cross, attn_val, cross_val, attn_prob, cross_prob, attn_total, x2_loc = forward_call(
-        tp_size, 0, head_dim, head_pad, x_loc, y_loc, g_loc, t_loc, mod_table, len_loc, biases, wqkv, wkv, wq, wo, wco)
+        tp_size, 0, head_dim, head_pad, x_loc, y_loc, g_loc, t_loc, mod_table, len_loc,
+        b_qkv, b_kv, b_q, b_o, b_co, wqkv, wkv, wq, wo, wco)
     gelu_out, g_x2, g_cross, sums, g_w_1, g_w_2, g_b_1 = mlp_call(
-        tp_size, 1, head_dim, x2_loc, g_loc, t_loc, mod_table, biases, w_1, w_2, g_all)
+        tp_size, 1, x2_loc, g_loc, t_loc, mod_table, b_1, w_1, w_2, g_all)
     x_out, g_x, g_y, sums, g_w_qkv, g_w_kv, g_w_q, g_w_o, g_w_co, g_b_qkv, g_b_kv, g_b_q = backward_call(
         tp_size, 2, head_dim, head_pad,
-        [g_cross, g_x2, x_loc, x2_loc, g_loc, attn_total, t_loc, mod_table, biases, w_2, wqkv, wkv, wq, wo, wco, sums],
+        [g_cross, g_x2, x_loc, x2_loc, g_loc, attn_total, t_loc, mod_table, b_2, w_2, wqkv, wkv, wq, wo, wco, sums],
         [qkv, kv, q_cross, attn_val, cross_val, attn_prob, cross_prob, gelu_out], [h1_all, x1_all, y_all])
 
-    g_w_qkv, g_w_kv, g_w_q, g_w_o, g_w_co, g_w_2, x_out, g_x, g_y = finish_call(
-        head_dim, head_pad, [g_w_qkv, g_w_kv, g_w_q, g_w_o, g_w_co], [g_w_2, x_out, g_x, g_y])
-
-    def head_weight(grad):
-        return grad[None].transpose(2, 0, 1)
-
-    def head_bias(grad):
-        return grad.reshape(-1, head_pad)[:, :head_dim].reshape(1, -1).astype(BF16)
-
+    g_w_qkv, g_w_kv, g_w_q, g_w_o, g_w_co, g_b_qkv, g_b_kv, g_b_q, g_w_1, g_b_1, g_w_2, x_out, g_x, g_y = finish_call(
+        head_dim, head_pad, [g_w_qkv, g_w_kv, g_w_q, g_w_o, g_w_co], [g_b_qkv, g_b_kv, g_b_q], [g_w_1, g_b_1, g_w_2, x_out, g_x, g_y])
+    g_w_qkv, g_w_kv, g_w_q = [grad[None].transpose(2, 0, 1) for grad in (g_w_qkv, g_w_kv, g_w_q)]
     vectors = sums.astype(BF16)
-    return (x_out, g_x, g_y, sums[:6],
-            head_weight(g_w_qkv), head_bias(g_b_qkv), g_w_o[None], vectors[B_O],
-            head_weight(g_w_q), head_bias(g_b_q), head_weight(g_w_kv), head_bias(g_b_kv),
-            g_w_co[None], vectors[B_CO],
-            g_w_1.T.astype(BF16), g_b_1[0].astype(BF16), g_w_2, vectors[B_2])
+    return (x_out, g_x, g_y, sums[:6], g_w_qkv, g_b_qkv, g_w_o[None], vectors[B_O], g_w_q, g_b_q, g_w_kv, g_b_kv,
+            g_w_co[None], vectors[B_CO], g_w_1, g_b_1[0], g_w_2, vectors[B_2])
 
 
 def solution(mesh):

time: 488 us -> 468 us (0.959); the launches traced: 478 us -> 467 us
  local copies, waits for them, and re-layouts: 9.16 us -> 1.28 us
where the time goes in v5:
time: 468 us; the launch traced here: 467 us
  Pallas kernels  464 us (99%)
    pallas_call x1, Pallas kernels, backward_call(): pl.pallas_call(functools.partial(backward_body, tp_size, head_dim), out_s...  196 us
    pallas_call x1, Pallas kernels, forward_call(): pl.pallas_call(functools.partial(forward_body, tp_size, head_dim), out_sh...  184 us
    pallas_call x1, Pallas kernels, mlp_call(): pl.pallas_call(functools.partial(mlp_body, tp_size), out_shape=[jax.Shape...  77.5 us

profile of v5, /device:TPU:21, one launch (start us, length us, event | category | flops | bytes accessed | tf_op | source)
XLA Modules:
  0.0 467.2 jit_solution(11279828407066352657)
XLA Ops:
  0.7 183.8 %attention_forward.1 = (bf16[8,256,1408]{2,1,0:T(8,128)(2,1)}, bf16[8,256,1408]{2,1,0:T(8,128)(2,1)}, bf16[8,256,1408]{2,1,0:T(8,128)(2,1)}, bf16[8,256,1408]{2,...) custom-call(bf16[8,16,1408]{2,1,0:T(8,128)(2,1)} %refs_2_.5, ...), custom_call_target="tpu_custom_call" | custom-call | tf_op jit(solution)/shard_map/attention_forward/pallas_call | solution.py:532
  184.5 77.5 %mlp_both_ways.1 = (bf16[8,256,384]{2,1,0:T(8,128)(2,1)}, f32[8,16,1408]{2,1,0:T(8,128)}, bf16[8,16,1408]{2,1,0:T(8,128)(2,1)}, f32[16,1408]{1,0:T(8,128)}, f32[...) custom-call(bf16[8,16,1408]{2,1,0:T(8,128)(2,1)} %get-tuple-element.64.refs_0_.refs_3_, ...), custom_call_target="tpu_custom_call" | custom-call | tf_op jit(solution)/shard_map/mlp_both_ways/pallas_call | solution.py:921
  262.0 196.0 %attention_backward.1 = (bf16[8,16,1408]{2,1,0:T(8,128)(2,1)}, bf16[8,16,1408]{2,1,0:T(8,128)(2,1)}, bf16[8,16,1408]{2,1,0:T(8,128)(2,1)}, f32[16,1408]{1,0:T(8,...) custom-call(bf16[8,16,1408]{2,1,0:T(8,128)(2,1)} %get-tuple-element., ...), custom_call_target="tpu_custom_call" | custom-call | tf_op jit(solution)/shard_map/attention_backward/pallas_call | solution.py:811
  458.0 0.0 copy-start
  458.0 6.6 %results.1 = (bf16[264,1408]{1,0:T(8,128)(2,1)}, bf16[176,1408]{1,0:T(8,128)(2,1)}, bf16[88,1408]{1,0:T(8,128)(2,1)}, bf16[88,1408]{1,0:T(8,128)(2,1)}, bf16[88,...) custom-call(f32[384,1408]{1,0:T(8,128)} %get-tuple-element.81.refs_0, ...), custom_call_target="tpu_custom_call" | custom-call | tf_op jit(solution)/shard_map/results/pallas_call | solution.py:948
  464.6 1.3 reduce.2
  465.9 0.0 copy-done
  465.9 0.6 slice.12
  466.5 0.7 slice_reduce_fusion
  (1 shorter events, 0.0 us)
Async XLA Ops:
  458.0 7.9 %copy-start = (f32[16,1408]{1,0:T(8,128)S(1)}, f32[16,1408]{1,0:T(8,128)}, u32[]{:S(2)}) copy-start(f32[16,1408]{1,0:T(8,128)} %get-tuple-element.98) | copy-start | bytes 270340

commit v6 on v5

--- a/solution.py
+++ b/solution.py
@@ -19,6 +19,7 @@
 TN = (((0,), (0,)), ((), ()))
 SHIFT1, SCALE1, GATE1, SHIFT2, SCALE2, GATE2, B_O, B_CO, B_2 = range(9)
 SUM_ROWS = 16
+LOADED = 19
 UP, DOWN = HALVES = WAYS = 0, 1
 SEND, TAKE = True, False
 KERNEL = functools.partial(pltpu.CompilerParams, has_side_effects=True, vmem_limit_bytes=67 * 1000 * 1000)
@@ -546,6 +547,17 @@
     )(*ins)
 
 
+class Emit:
+    def __init__(self, acc, stage, dest, sem):
+        self.acc, self.stage = acc, stage
+        self.copy = pltpu.make_async_copy(stage, dest, sem)
+
+    def start(self, head_dim, head_pad):
+        for p in range(self.stage.shape[0] // head_dim):
+            self.stage[p * head_dim:(p + 1) * head_dim, :] = self.acc[p * head_pad:p * head_pad + head_dim, :].astype(BF16)
+        self.copy.start()
+
+
 class RowFeed:
     def __init__(self, source, buf, sem, rows):
         self.source, self.buf, self.sem, self.rows = source, buf, sem, rows
@@ -563,7 +575,7 @@
         return block.reshape(block.shape[0] * block.shape[1], block.shape[2])
 
 
-def small_total(at, src, got, mine, out, sems):
+def small_total(at, src, got, mine, out, sems, between):
     send1, recv1, send2, recv2 = sems
     tiles = src.shape[1] // LANES
 
@@ -584,6 +596,7 @@
         @pl.when(at.me != tile)
         def _():
             first(tile, lax.rem(at.me - tile + at.tp_size, at.tp_size) - 1).start()
+    between()
     for tile in range(tiles):
         @pl.when(at.me == tile)
         def _():
@@ -607,24 +620,26 @@
 def backward_body(tp_size, head_dim, *refs):
     at = Place(tp_size)
     take = cutter(refs)
-    g_cross, g_x2, x, x2, g, atot, t_emb, table, b2_in, w2, wqkv_in, wkv_in, wq_in, wo_in, wco_in, sums_in = take(16)
+    g_cross, t_emb, table, b2_in, sums_in = take(5)
     b2 = row_of(b2_in)
-    loads, feeds = take(8), take(3)
-    x_out, g_x, g_y, sums_out = take(4)
-    accs = take(8)
-    gw_qkv, gw_kv, gw_q, gw_o, gw_co, gb_qkv, gb_kv, gb_q = accs
-    held = take(8)
-    qkv, kv, q_c, val, cval, prob, cprob, act_all = held
+    loads, feeds = take(LOADED), take(3)
+    x_out, g_x, g_y, sums_out, gb_qkv, gb_kv, gb_q = take(7)
+    dests, held = take(5), take(LOADED)
+    wqkv_in, wkv_in, wq_in, wo_in, wco_in, w2, act_all, cval, q_c, kv, cprob, g_x2, x, x2, g, atot, val, qkv, prob = held
+    accs, stages = take(5), take(5)
+    gw_qkv, gw_kv, gw_q, gw_o, gw_co = accs
     full, pbuf, sibr1, rcv1, pbufy, sibr2, rcv2, wqkv, wkv, wq, wo, wco = take(12)
     g_val, g_qkv, g_kv, g_q, g_x1, g_h1, g_attn, mod, sums, got, mine, feed_a, feed_y = take(13)
     gather_c, gather_a = [Gather(at, own, full, take(4)) for own in (g_cross, g_attn)]
     near, far = (pbuf, sibr1, rcv1), (pbufy, sibr2, rcv2)
     scat_m, scat_q, scat_y, scat_h = [Scatter(at, *bufs, take(4)) for bufs in (far, near, far, near)]
-    load_sem, *feed_sems = take(4)
+    load_sem, emit_sem, *feed_sems = take(5)
+    emits = [Emit(*e, emit_sem.at[i]) for i, e in enumerate(zip(accs, stages, dests))]
+    emit_qkv, emit_kv, emit_q, emit_o, emit_co = [functools.partial(e.start, head_dim, wq.shape[0]) for e in emits]
     feed_h, feed_x, feed_yy = [
         RowFeed(source, buf, sem, scat.rows)
         for source, buf, sem, scat in zip(feeds, (feed_a, feed_a, feed_y), feed_sems, (scat_h, scat_q, scat_y))]
-    batch, n_loc, width = x.shape
+    batch, _, width = x.shape
     ring, half = at.ring, at.half
     head_pad = wq.shape[0]
     scale = head_dim ** -0.5
@@ -639,12 +654,12 @@
     feed_x.copy(0).start()
     feed_yy.copy(0).start()
     fill_mod(mod, t_emb, table, (SHIFT1, SCALE1, GATE1, GATE2))
-    for dest, source in ((wqkv, wqkv_in), (wkv, wkv_in), (wq, wq_in), (wo, wo_in), (wco, wco_in)):
-        pad_rows(dest, source, head_dim)
     sums[...] = sums_in[...]
-    clear(accs)
+    clear((*accs, gb_qkv, gb_kv, gb_q))
     for i in range(len(held)):
         load_copy(i).wait()
+    for dest, source in zip((wqkv, wkv, wq, wo, wco), held):
+        pad_rows(dest, source, head_dim)
 
     def put_m(slot):
         scat_m.put(slot, dot(rows_of(act_all, scat_m.rows(slot)), w2))
@@ -667,6 +682,7 @@
 
     loop_slots(ring, hooks, out_back(gather_c, cval, wco, gw_co, put_m))
     gather_c.finish()
+    emit_co()
 
     def back_one(q_b, k_b, v_b, p_b, g_b):
         g_p = dot(g_b, v_b, NT)
@@ -711,6 +727,7 @@
 
     loop_slots(ring, hooks, put_q)
     scat_q.step(half - 1)
+    emit_q()
 
     def out_one(b, gate_sum):
         gate, g_out, total = at_sample(mod, b)[-1], g[b].astype(F32), g_h1[b]
@@ -759,6 +776,8 @@
             g_qkv[b, :, i * head_pad:(i + 1) * head_pad] = parts[i]
 
     loop_slots(batch, hooks, self_back)
+    emit_kv()
+    emit_o()
 
     def take_y(part, total):
         g_y[part] = total.astype(BF16)
@@ -777,51 +796,59 @@
 
     loop_slots(ring, hooks, put_h)
     scat_h.step(half - 1)
+    emit_qkv()
+
     def take_h(part, total):
         g_h1[part] = total
 
     scat_h.final(take_h)
 
-    def x_back(b, carry):
+    def sums_one(b, carry):
         shift_sum, scale_sum = carry
+        normed, _ = normalize(x[b])
+        return shift_sum + row_sum(g_h1[b]), scale_sum + row_sum(g_h1[b] * normed)
+
+    def x_one(b):
         normed, inv_std = normalize(x[b])
-        grad = g_h1[b]
-        back = normalize_back(normed, inv_std, grad * (1.0 + mod[1, pl.ds(b, 1), :]))
+        _, scale, *_ = at_sample(mod, b)
+        back = normalize_back(normed, inv_std, g_h1[b] * (1.0 + scale))
         g_x[b] = (g_x1[b] + back).astype(BF16)
-        return shift_sum + row_sum(grad), scale_sum + row_sum(grad * normed)
-
-    shift_sum, scale_sum = lax.fori_loop(0, batch, x_back, (zero, zero))
+
+    shift_sum, scale_sum = lax.fori_loop(0, batch, sums_one, (zero, zero))
     for row, value in ((SHIFT1, shift_sum), (SCALE1, scale_sum)):
         sums[row:row + 1, :] = value
-    small_total(at, sums, got, mine, sums_out, take(4))
+    small_total(at, sums, got, mine, sums_out, take(4), lambda: each(batch, x_one))
     for stream in (gather_a, scat_y, scat_h):
         stream.finish()
+    for emit in emits:
+        emit.copy.wait()
 
 
 def backward_call(tp_size, cid, head_dim, head_pad, ins, loads, feeds):
     batch, n_loc, width = ins[0].shape
     n_tok = n_loc * tp_size
     ring, half = tp_size // 2, tp_size // 4
-    n_sum = ins[-1].shape[0]
     tokens = lambda last: (batch, n_tok, last)
     local = (batch, n_loc, width)
     sib, rcv, pbuf = (ring, *local), (2, half, *local), (ring, batch, 2 * n_loc, width)
-    outs = [(local, BF16)] * 3 + [((n_sum, width), F32)]
-    outs += [((n * head_pad, width), F32) for n in (3, 2, 1, 1, 1)] + [((1, n * head_pad), F32) for n in (3, 2, 1)]
+    parts = 3, 2, 1, 1, 1
+    outs = [(local, BF16)] * 3 + [((SUM_ROWS, width), F32)] + [((1, n * head_pad), F32) for n in parts[:3]]
+    grads = [((n * head_dim, width), BF16) for n in parts]
     return pl.pallas_call(
         functools.partial(backward_body, tp_size, head_dim),
-        out_shape=[jax.ShapeDtypeStruct(*o) for o in outs],
+        out_shape=[jax.ShapeDtypeStruct(*o) for o in outs + grads],
         in_specs=[VMEM] * len(ins) + [ANY] * (len(loads) + len(feeds)),
-        out_specs=[VMEM] * len(outs),
+        out_specs=[VMEM] * len(outs) + [ANY] * len(grads),
         scratch_shapes=[pltpu.VMEM(a.shape, a.dtype) for a in loads]
+        + [pltpu.VMEM((n * head_pad, width), F32) for n in parts] + [pltpu.VMEM(*g) for g in grads]
         + [pltpu.VMEM(s, BF16) for s in (tokens(width), pbuf, sib, rcv, pbuf, sib, rcv)]
-        + [pltpu.VMEM((n * head_pad, width), BF16) for n in (3, 2, 1, 1, 1)]
+        + [pltpu.VMEM((n * head_pad, width), BF16) for n in parts]
         + [pltpu.VMEM(tokens(n * head_pad), BF16) for n in (1, 3, 2, 1)]
-        + [pltpu.VMEM(local, F32), pltpu.VMEM(local, F32), pltpu.VMEM(local, BF16), pltpu.VMEM((4, batch, width), F32), pltpu.VMEM((n_sum, width), F32),
-           pltpu.VMEM((tp_size - 1, n_sum, LANES), F32), pltpu.VMEM((n_sum, LANES), F32)]
+        + [pltpu.VMEM(local, F32), pltpu.VMEM(local, F32), pltpu.VMEM(local, BF16), pltpu.VMEM((4, batch, width), F32), pltpu.VMEM((SUM_ROWS, width), F32),
+           pltpu.VMEM((tp_size - 1, SUM_ROWS, LANES), F32), pltpu.VMEM((SUM_ROWS, LANES), F32)]
         + [pltpu.VMEM((2, batch, 2 * n_loc, width), BF16)] * 2
         + gather_sems(tp_size) * 2 + scatter_sems(tp_size) * 4
-        + [pltpu.SemaphoreType.DMA((len(loads),))] + [pltpu.SemaphoreType.DMA((2,))] * 3
+        + [pltpu.SemaphoreType.DMA((len(loads),)), pltpu.SemaphoreType.DMA((len(grads),))] + [pltpu.SemaphoreType.DMA((2,))] * 3
         + [pltpu.SemaphoreType.DMA((n,)) for n in (width // LANES, tp_size - 1, tp_size - 1, width // LANES)],
         compiler_params=KERNEL(collective_id=cid),
         name='attention_backward',
@@ -833,9 +860,13 @@
     take = cutter(refs)
     x2, g, t_emb, table, b1_in, w1, w2, g_all = take(8)
     b1 = row_of(b1_in)
-    act_all, g_x2, g_cross, sums, gw_1, gw_2, gb_1 = take(7)
-    h2, mod, fh, hid_all, g_h2, feed, *bufs = take(9)
+    g_x2, g_cross, sums, gb_1, act_out, *dests = take(7)
+    h2, mod, fh, hid_all, g_h2, feed, act_all, gw_1, gw_2, *stages = take(11)
+    bufs = take(3)
     gather_h, scat_h = Gather(at, h2, fh, take(4)), Scatter(at, *bufs, take(4))
+    act_sem, *emit_sems = take(3)
+    act_copy = pltpu.make_async_copy(act_all, act_out, act_sem)
+    emits = [Emit(*e) for e in zip((gw_1, gw_2), stages, dests, emit_sems)]
     feed_g, feed_again = [RowFeed(g_all, feed, refs[-1], stream.rows) for stream in (gather_h, scat_h)]
     batch = x2.shape[0]
 
@@ -869,6 +900,7 @@
         put_rows(hid_all, rows, g_hidden)
 
     loop_slots(at.ring, hooks, mlp)
+    act_copy.start()
     feed_again.copy(0).start()
 
     def hooks(s):
@@ -884,6 +916,9 @@
 
     loop_slots(at.ring, hooks, put_h)
     scat_h.step(at.half - 1)
+    for emit in emits:
+        rows = emit.acc.shape[0]
+        emit.start(rows, rows)
 
     def take_h(part, value):
         g_h2[part] = value
@@ -906,6 +941,8 @@
         sums[row:row + 1, :] = value
     gather_h.finish()
     scat_h.finish()
+    for copy in (act_copy, *[emit.copy for emit in emits]):
+        copy.wait()
 
 
 def mlp_call(tp_size, cid, *ins):
@@ -915,44 +952,58 @@
     ring, half = tp_size // 2, tp_size // 4
     local, tokens, hidden = (batch, n_loc, width), (batch, n_tok, width), (batch, n_tok, ffn)
     chip = batch, 2 * n_loc, width
-    outs = [(hidden, BF16), (local, F32), (local, BF16), ((SUM_ROWS, width), F32), ((width, ffn), F32), ((ffn, width), F32), ((1, ffn), F32)]
+    outs = [(local, F32), (local, BF16), ((SUM_ROWS, width), F32), ((1, ffn), F32)]
+    late = [(hidden, BF16), ((width, ffn), BF16), ((ffn, width), BF16)]
     scratch = [(local, BF16), ((3, batch, width), F32), (tokens, BF16), (hidden, BF16), (local, F32), ((2, *chip), BF16),
+               (hidden, BF16), ((width, ffn), F32), ((ffn, width), F32), *late[1:],
                ((ring, *chip), BF16), ((ring, *local), BF16), ((2, half, *local), BF16)]
     return pl.pallas_call(
         functools.partial(mlp_body, tp_size),
-        out_shape=[jax.ShapeDtypeStruct(*o) for o in outs],
+        out_shape=[jax.ShapeDtypeStruct(*o) for o in outs + late],
         in_specs=[VMEM] * (len(ins) - 1) + [ANY],
-        out_specs=[VMEM] * len(outs),
-        scratch_shapes=[pltpu.VMEM(*k) for k in scratch] + gather_sems(tp_size) + scatter_sems(tp_size) + [pltpu.SemaphoreType.DMA((2,))],
+        out_specs=[VMEM] * len(outs) + [ANY] * len(late),
+        scratch_shapes=[pltpu.VMEM(*k) for k in scratch] + gather_sems(tp_size) + scatter_sems(tp_size)
+        + [pltpu.SemaphoreType.DMA] * len(late) + [pltpu.SemaphoreType.DMA((2,))],
         compiler_params=KERNEL(collective_id=cid),
         name='mlp_both_ways',
     )(*ins)
 
 
-def finish_body(head_dim, head_pad, n_head, n_bias, *refs):
-    sources, results = refs[:len(refs) // 2], refs[len(refs) // 2:]
-    for i, (source, result) in enumerate(zip(sources, results)):
-        if i < n_head:
-            for p in range(result.shape[0] // head_dim):
-                result[p * head_dim:(p + 1) * head_dim, :] = source[p * head_pad:p * head_pad + head_dim, :].astype(result.dtype)
-        elif i < n_head + n_bias:
-            parts = [source[:, p:p + head_dim] for p in range(0, source.shape[1], head_pad)]
-            result[...] = jnp.concatenate(parts, axis=1).astype(result.dtype)
-        else:
-            result[...] = source[...].astype(result.dtype)
-
-
-def finish_call(head_dim, head_pad, padded, biases, plain):
-    shapes = [(a.shape[0] // head_pad * head_dim, a.shape[1]) for a in padded]
-    shapes += [(1, b.shape[1] // head_pad * head_dim) for b in biases] + [a.shape for a in plain]
+def finish_body(head_dim, head_pad, n_big, *refs):
+    take = cutter(refs)
+    sources, biases, (b_1, sums) = take(n_big), take(3), take(2)
+    results, bias_outs, vectors = take(n_big), take(3), take(4)
+    table, stages, (sem_in, sem_out) = take(1)[0], take(n_big), take(2)
+    copies_in = [pltpu.make_async_copy(*ends, sem_in.at[i]) for i, ends in enumerate(zip(sources, stages))]
+    copies_out = [pltpu.make_async_copy(*ends, sem_out.at[i]) for i, ends in enumerate(zip(stages, results))]
+    for copy in copies_in:
+        copy.start()
+    for source, result in zip(biases, bias_outs):
+        parts = [source[:, p:p + head_dim] for p in range(0, source.shape[1], head_pad)]
+        result[...] = jnp.concatenate(parts, axis=1).astype(BF16)
+    rows = [b_1[...]] + [sums[row:row + 1, :] for row in (B_O, B_CO, B_2)]
+    for row, result in zip(rows, vectors):
+        result[...] = row.astype(BF16).reshape(result.shape)
+    table[...] = sums[:B_O, :]
+    for arrived, leave in zip(copies_in, copies_out):
+        arrived.wait()
+        leave.start()
+    for copy in copies_out:
+        copy.wait()
+
+
+def finish_call(head_dim, head_pad, big, biases, b_1, sums):
+    width = sums.shape[1]
+    shapes = [a.shape for a in big] + [(1, b.shape[1] // head_pad * head_dim) for b in biases] + [(b_1.shape[1],)] + [(width,)] * 3
     return pl.pallas_call(
-        functools.partial(finish_body, head_dim, head_pad, len(padded), len(biases)),
-        out_shape=[jax.ShapeDtypeStruct(shape, BF16) for shape in shapes],
-        in_specs=[VMEM] * len(shapes),
-        out_specs=[VMEM] * len(shapes),
+        functools.partial(finish_body, head_dim, head_pad, len(big)),
+        out_shape=[jax.ShapeDtypeStruct(shape, BF16) for shape in shapes] + [jax.ShapeDtypeStruct((B_O, width), F32)],
+        in_specs=[ANY] * len(big) + [VMEM] * (len(biases) + 2),
+        out_specs=[ANY] * len(big) + [VMEM] * (len(biases) + 5),
+        scratch_shapes=[pltpu.VMEM(a.shape, BF16) for a in big] + [pltpu.SemaphoreType.DMA((len(big),))] * 2,
         compiler_params=pltpu.CompilerParams(vmem_limit_bytes=60 * 1000 * 1000),
         name='results',
-    )(*padded, *biases, *plain)
+    )(*big, *biases, b_1, sums)
 
 
 def device_block(tp_size, x_loc, y_loc, t_loc, len_loc, mod_table, w_qkv, b_qkv, w_o, b_o, w_q, b_q, w_kv, b_kv, w_co, b_co, w_1, b_1, w_2, b_2, g_loc):
@@ -964,19 +1015,20 @@
     h1_all, y_all, x1_all, g_all, qkv, kv, q_cross, attn_val, cross_val, attn_prob, cross_prob, attn_total, x2_loc = forward_call(
         tp_size, 0, head_dim, head_pad, x_loc, y_loc, g_loc, t_loc, mod_table, len_loc,
         b_qkv, b_kv, b_q, b_o, b_co, wqkv, wkv, wq, wo, wco)
-    gelu_out, g_x2, g_cross, sums, g_w_1, g_w_2, g_b_1 = mlp_call(
+    g_x2, g_cross, sums, g_b_1, gelu_out, g_w_1, g_w_2 = mlp_call(
         tp_size, 1, x2_loc, g_loc, t_loc, mod_table, b_1, w_1, w_2, g_all)
-    x_out, g_x, g_y, sums, g_w_qkv, g_w_kv, g_w_q, g_w_o, g_w_co, g_b_qkv, g_b_kv, g_b_q = backward_call(
-        tp_size, 2, head_dim, head_pad,
-        [g_cross, g_x2, x_loc, x2_loc, g_loc, attn_total, t_loc, mod_table, b_2, w_2, wqkv, wkv, wq, wo, wco, sums],
-        [qkv, kv, q_cross, attn_val, cross_val, attn_prob, cross_prob, gelu_out], [h1_all, x1_all, y_all])
-
-    g_w_qkv, g_w_kv, g_w_q, g_w_o, g_w_co, g_b_qkv, g_b_kv, g_b_q, g_w_1, g_b_1, g_w_2, x_out, g_x, g_y = finish_call(
-        head_dim, head_pad, [g_w_qkv, g_w_kv, g_w_q, g_w_o, g_w_co], [g_b_qkv, g_b_kv, g_b_q], [g_w_1, g_b_1, g_w_2, x_out, g_x, g_y])
+    x_out, g_x, g_y, sums, *rest = backward_call(
+        tp_size, 2, head_dim, head_pad, [g_cross, t_loc, mod_table, b_2, sums],
+        [wqkv, wkv, wq, wo, wco, w_2, gelu_out, cross_val, q_cross, kv, cross_prob, g_x2, x_loc, x2_loc, g_loc, attn_total,
+         attn_val, qkv, attn_prob], [h1_all, x1_all, y_all])
+    bias_grads, weight_grads = rest[:3], rest[3:]
+
+    results = finish_call(head_dim, head_pad, [x_out, g_x, g_y, g_w_1, g_w_2, *weight_grads], bias_grads, g_b_1, sums)
+    x_out, g_x, g_y, g_w_1, g_w_2, *results = results
+    g_w_qkv, g_w_kv, g_w_q, g_w_o, g_w_co, g_b_qkv, g_b_kv, g_b_q, g_b_1, g_b_o, g_b_co, g_b_2, g_table = results
     g_w_qkv, g_w_kv, g_w_q = [grad[None].transpose(2, 0, 1) for grad in (g_w_qkv, g_w_kv, g_w_q)]
-    vectors = sums.astype(BF16)
-    return (x_out, g_x, g_y, sums[:6], g_w_qkv, g_b_qkv, g_w_o[None], vectors[B_O], g_w_q, g_b_q, g_w_kv, g_b_kv,
-            g_w_co[None], vectors[B_CO], g_w_1, g_b_1[0], g_w_2, vectors[B_2])
+    return (x_out, g_x, g_y, g_table, g_w_qkv, g_b_qkv, g_w_o[None], g_b_o, g_w_q, g_b_q, g_w_kv, g_b_kv,
+            g_w_co[None], g_b_co, g_w_1, g_b_1, g_w_2, g_b_2)
 
 
 def solution(mesh):

time: 468 us -> 458 us (0.979)
  Pallas kernels: 464 us -> 457 us
where the time goes in v6:
time: 458 us
  Pallas kernels  457 us (100%)
    pallas_call x1, Pallas kernels, backward_call(): pl.pallas_call(functools.partial(backward_body, tp_size, head_dim), out_s...  191 us
    pallas_call x1, Pallas kernels, forward_call(): pl.pallas_call(functools.partial(forward_body, tp_size, head_dim), out_sh...  184 us
    pallas_call x1, Pallas kernels, mlp_call(): pl.pallas_call(functools.partial(mlp_body, tp_size), out_shape=[jax.Shape...  75.7 us

profile of v6, /device:TPU:21, one launch (start us, length us, event | category | flops | bytes accessed | tf_op | source)
XLA Modules:
  0.0 458.0 jit_solution(7256955478150024812)
XLA Ops:
  0.7 183.8 %attention_forward.1 = (bf16[8,256,1408]{2,1,0:T(8,128)(2,1)}, bf16[8,256,1408]{2,1,0:T(8,128)(2,1)}, bf16[8,256,1408]{2,1,0:T(8,128)(2,1)}, bf16[8,256,1408]{2,...) custom-call(bf16[8,16,1408]{2,1,0:T(8,128)(2,1)} %refs_17_.1, ...), custom_call_target="tpu_custom_call" | custom-call | tf_op jit(solution)/shard_map/attention_forward/pallas_call | solution.py:533
  184.5 75.7 %mlp_both_ways.1 = (f32[8,16,1408]{2,1,0:T(8,128)}, bf16[8,16,1408]{2,1,0:T(8,128)(2,1)}, f32[16,1408]{1,0:T(8,128)}, f32[1,384]{1,0:T(1,128)}, bf16[8,256,384]{...) custom-call(bf16[8,16,1408]{2,1,0:T(8,128)(2,1)} %get-tuple-element.68.refs_0_.refs_18_, ...), custom_call_target="tpu_custom_call" | custom-call | tf_op jit(solution)/shard_map/mlp_both_ways/pallas_call | solution.py:960
  260.2 191.4 %attention_backward.1 = (bf16[8,16,1408]{2,1,0:T(8,128)(2,1)}, bf16[8,16,1408]{2,1,0:T(8,128)(2,1)}, bf16[8,16,1408]{2,1,0:T(8,128)(2,1)}, f32[16,1408]{1,0:T(8,...) custom-call(bf16[8,16,1408]{2,1,0:T(8,128)(2,1)} %get-tuple-element., ...), custom_call_target="tpu_custom_call" | custom-call | tf_op jit(solution)/shard_map/attention_backward/pallas_call | solution.py:837
  451.6 6.2 %results.1 = (bf16[8,16,1408]{2,1,0:T(8,128)(2,1)}, bf16[8,16,1408]{2,1,0:T(8,128)(2,1)}, bf16[8,16,1408]{2,1,0:T(8,128)(2,1)}, bf16[1408,384]{1,0:T(8,128)(2,1)...) custom-call(bf16[8,16,1408]{2,1,0:T(8,128)(2,1)} %get-tuple-element., ...), custom_call_target="tpu_custom_call" | custom-call | tf_op jit(solution)/shard_map/results/pallas_call | solution.py:998

commit v7 on v6

--- a/solution.py
+++ b/solution.py
@@ -358,14 +358,19 @@
     at = Place(tp_size)
     take = cutter(refs)
     x, y, g, t_emb, table, lens, *bias_in = take(11)
-    wqkv_in, wkv_in, wq_in, wo_in, wco_in = take(5)
+    sources = take(5)
     h1_out, y_out, x1_out, g_out = take(4)
     outs, scratch = take(9), take(9)
     qkv, kv, q_c, val, cval, prob, cprob, atot, x2 = scratch
     h1, x1, gm, mod, fh, fy, fx, fg, pbuf, sibr1, rcv1, sibr2, rcv2, wqkv, wkv, wq, wo, wco = take(18)
+    raws = take(5)
     gather_h, gather_y, gather_x, gather_g = [Gather(at, own, full, take(4)) for own, full in ((h1, fh), (y, fy), (x1, fx), (gm, fg))]
     scat_o, scat_c = [Scatter(at, pbuf, sibr, rcv, take(4)) for sibr, rcv in ((sibr1, rcv1), (sibr2, rcv2))]
-    saves, out_sem = take(4), refs[-1]
+    *saves, raw_sem = take(5)
+    out_sem = refs[-1]
+    raw_copies = [pltpu.make_async_copy(*ends, raw_sem.at[i]) for i, ends in enumerate(zip(sources, raws))]
+    for copy in raw_copies:
+        copy.start()
     batch = x.shape[0]
     head_pad = wq.shape[0]
     bqkv, bkv, bq = [padded_bias(ref, head_dim, head_pad) for ref in bias_in[:3]]
@@ -387,7 +392,8 @@
 
     each(batch, norm_one)
     gather_h.start()
-    for dest, source in ((wqkv, wqkv_in), (wkv, wkv_in), (wq, wq_in), (wo, wo_in), (wco, wco_in)):
+    for copy, dest, source in zip(raw_copies, (wqkv, wkv, wq, wo, wco), raws):
+        copy.wait()
         pad_rows(dest, source, head_dim)
 
     def hooks(s):
@@ -421,8 +427,9 @@
         out_copy(i).start()
 
     def hooks(s):
-        if s >= 2 and s % 2 == 0:
-            scat_o.step(s // 2 - 1)
+        if s % 2:
+            scat_o.step(s // 2)
+        elif s:
             gather_y.group(s // 2 + 3)
         if s == at.ring - 1:
             gather_g.start()
@@ -431,7 +438,6 @@
         scat_o.put(slot, dot(rows_of(val, scat_o.rows(slot)), wo))
 
     loop_slots(at.ring, hooks, project_o)
-    scat_o.step(at.half - 1)
 
     def take_o(part, total):
         atot[part] = total + bo
@@ -489,8 +495,8 @@
             gather_g.save_copy(g_out, saves[3], slot).start()
 
     def hooks(s):
-        if s >= 2 and s % 2 == 0:
-            scat_c.step(s // 2 - 1)
+        if s % 2:
+            scat_c.step(s // 2)
         if s == 3:
             gather_g.group(5)
             save_g(range(3))
@@ -502,7 +508,6 @@
         scat_c.put(slot, dot(rows_of(cval, scat_c.rows(slot)), wco))
 
     loop_slots(at.ring, hooks, project_c)
-    scat_c.step(at.half - 1)
     save_g(range(5, at.ring))
 
     def take_c(part, total):
@@ -533,15 +538,15 @@
     return pl.pallas_call(
         functools.partial(forward_body, tp_size, head_dim),
         out_shape=[jax.ShapeDtypeStruct(tokens(width), BF16)] * 4 + [jax.ShapeDtypeStruct(*k) for k in kept],
-        in_specs=[VMEM] * 5 + [pl.BlockSpec(memory_space=pltpu.SMEM)] + [VMEM] * (len(ins) - 6),
+        in_specs=[VMEM] * 5 + [pl.BlockSpec(memory_space=pltpu.SMEM)] + [VMEM] * (len(ins) - 11) + [ANY] * 5,
         out_specs=[ANY] * (4 + len(kept)),
         scratch_shapes=[pltpu.VMEM(*k) for k in kept] + [
             *[pltpu.VMEM(local, BF16)] * 3, pltpu.VMEM((4, batch, width), F32), *[pltpu.VMEM(tokens(width), BF16)] * 4,
             pltpu.VMEM((ring, batch, 2 * n_loc, width), BF16),
             pltpu.VMEM(sib, BF16), pltpu.VMEM(rcv, BF16), pltpu.VMEM(sib, BF16), pltpu.VMEM(rcv, BF16)]
-        + [pltpu.VMEM((n * head_pad, width), BF16) for n in (3, 2, 1, 1, 1)]
+        + [pltpu.VMEM((n * head_pad, width), BF16) for n in (3, 2, 1, 1, 1)] + [pltpu.VMEM(w.shape, BF16) for w in ins[-5:]]
         + gather_sems(tp_size) * 4 + scatter_sems(tp_size) * 2
-        + [pltpu.SemaphoreType.DMA((ring,))] * 4 + [pltpu.SemaphoreType.DMA((len(kept),))],
+        + [pltpu.SemaphoreType.DMA((ring,))] * 4 + [pltpu.SemaphoreType.DMA((5,))] + [pltpu.SemaphoreType.DMA((len(kept),))],
         compiler_params=KERNEL(collective_id=cid),
         name='attention_forward',
     )(*ins)
@@ -704,8 +709,8 @@
     loop_slots(batch, hooks, cross_back)
 
     def hooks(s):
-        if s >= 2 and s % 2 == 0:
-            scat_q.step(s // 2 - 1)
+        if s % 2:
+            scat_q.step(s // 2)
         if s == 3:
             scat_m.final(take_m)
             scat_m.finish()
@@ -726,7 +731,6 @@
         add_to(gb_kv, row_sum(block.astype(F32)))
 
     loop_slots(ring, hooks, put_q)
-    scat_q.step(half - 1)
     emit_q()
 
     def out_one(b, gate_sum):
@@ -783,8 +787,8 @@
         g_y[part] = total.astype(BF16)
 
     def hooks(s):
-        if s >= 2 and s % 2 == 0:
-            scat_h.step(s // 2 - 1)
+        if s % 2:
+            scat_h.step(s // 2)
         if s == 5:
             scat_y.final(take_y)
 
@@ -795,7 +799,6 @@
         add_to(gb_qkv, row_sum(block.astype(F32)))
 
     loop_slots(ring, hooks, put_h)
-    scat_h.step(half - 1)
     emit_qkv()
 
     def take_h(part, total):
@@ -858,13 +861,16 @@
 def mlp_body(tp_size, *refs):
     at = Place(tp_size)
     take = cutter(refs)
-    x2, g, t_emb, table, b1_in, w1, w2, g_all = take(8)
+    x2, g, t_emb, table, b1_in, *sources, g_all = take(8)
     b1 = row_of(b1_in)
     g_x2, g_cross, sums, gb_1, act_out, *dests = take(7)
-    h2, mod, fh, hid_all, g_h2, feed, act_all, gw_1, gw_2, *stages = take(11)
+    h2, mod, fh, hid_all, g_h2, feed, w1, w2, act_all, gw_1, gw_2, *stages = take(13)
     bufs = take(3)
     gather_h, scat_h = Gather(at, h2, fh, take(4)), Scatter(at, *bufs, take(4))
     act_sem, *emit_sems = take(3)
+    weight_copies = [pltpu.make_async_copy(*ends) for ends in zip(sources, (w1, w2), take(2))]
+    for copy in weight_copies:
+        copy.start()
     act_copy = pltpu.make_async_copy(act_all, act_out, act_sem)
     emits = [Emit(*e) for e in zip((gw_1, gw_2), stages, dests, emit_sems)]
     feed_g, feed_again = [RowFeed(g_all, feed, refs[-1], stream.rows) for stream in (gather_h, scat_h)]
@@ -882,6 +888,8 @@
     each(batch, norm_one)
     gather_h.start()
     clear((gw_1, gw_2, gb_1, sums))
+    for copy in weight_copies:
+        copy.wait()
 
     def hooks(s):
         for group in gather_h.groups_before(s):
@@ -904,8 +912,8 @@
     feed_again.copy(0).start()
 
     def hooks(s):
-        if s >= 2 and s % 2 == 0:
-            scat_h.step(s // 2 - 1)
+        if s % 2:
+            scat_h.step(s // 2)
 
     def put_h(slot):
         rows = scat_h.rows(slot)
@@ -915,7 +923,6 @@
         add_to(gw_2, dot(rows_of(act_all, rows), feed_again.take(slot, at.ring), TN))
 
     loop_slots(at.ring, hooks, put_h)
-    scat_h.step(at.half - 1)
     for emit in emits:
         rows = emit.acc.shape[0]
         emit.start(rows, rows)
@@ -954,16 +961,16 @@
     chip = batch, 2 * n_loc, width
     outs = [(local, F32), (local, BF16), ((SUM_ROWS, width), F32), ((1, ffn), F32)]
     late = [(hidden, BF16), ((width, ffn), BF16), ((ffn, width), BF16)]
-    scratch = [(local, BF16), ((3, batch, width), F32), (tokens, BF16), (hidden, BF16), (local, F32), ((2, *chip), BF16),
+    scratch = [(local, BF16), ((3, batch, width), F32), (tokens, BF16), (hidden, BF16), (local, F32), ((2, *chip), BF16), *late[1:],
                (hidden, BF16), ((width, ffn), F32), ((ffn, width), F32), *late[1:],
                ((ring, *chip), BF16), ((ring, *local), BF16), ((2, half, *local), BF16)]
     return pl.pallas_call(
         functools.partial(mlp_body, tp_size),
         out_shape=[jax.ShapeDtypeStruct(*o) for o in outs + late],
-        in_specs=[VMEM] * (len(ins) - 1) + [ANY],
+        in_specs=[VMEM] * (len(ins) - 3) + [ANY] * 3,
         out_specs=[VMEM] * len(outs) + [ANY] * len(late),
         scratch_shapes=[pltpu.VMEM(*k) for k in scratch] + gather_sems(tp_size) + scatter_sems(tp_size)
-        + [pltpu.SemaphoreType.DMA] * len(late) + [pltpu.SemaphoreType.DMA((2,))],
+        + [pltpu.SemaphoreType.DMA] * 5 + [pltpu.SemaphoreType.DMA((2,))],
         compiler_params=KERNEL(collective_id=cid),
         name='mlp_both_ways',
     )(*ins)

time: 458 us -> 453 us (0.989)
  Pallas kernels: 457 us -> 452 us
where the time goes in v7:
time: 453 us
  Pallas kernels  452 us (100%)
    pallas_call x1, Pallas kernels, backward_call(): pl.pallas_call(functools.partial(backward_body, tp_size, head_dim), out_s...  193 us
    pallas_call x1, Pallas kernels, forward_call(): pl.pallas_call(functools.partial(forward_body, tp_size, head_dim), out_sh...  181 us
    pallas_call x1, Pallas kernels, mlp_call(): pl.pallas_call(functools.partial(mlp_body, tp_size), out_shape=[jax.Shape...  71.8 us

profile of v7, /device:TPU:21, one launch (start us, length us, event | category | flops | bytes accessed | tf_op | source)
XLA Modules:
  0.0 452.8 jit_solution(10726332126139283384)
XLA Ops:
  0.7 181.3 %attention_forward.1 = (bf16[8,256,1408]{2,1,0:T(8,128)(2,1)}, bf16[8,256,1408]{2,1,0:T(8,128)(2,1)}, bf16[8,256,1408]{2,1,0:T(8,128)(2,1)}, bf16[8,256,1408]{2,...) custom-call(bf16[8,16,1408]{2,1,0:T(8,128)(2,1)} %refs_17_.1, ...), custom_call_target="tpu_custom_call" | custom-call | tf_op jit(solution)/shard_map/attention_forward/pallas_call | solution.py:538
  181.9 71.8 %mlp_both_ways.1 = (f32[8,16,1408]{2,1,0:T(8,128)}, bf16[8,16,1408]{2,1,0:T(8,128)(2,1)}, f32[16,1408]{1,0:T(8,128)}, f32[1,384]{1,0:T(1,128)}, bf16[8,256,384]{...) custom-call(bf16[8,16,1408]{2,1,0:T(8,128)(2,1)} %get-tuple-element.68.refs_0_.refs_18_, ...), custom_call_target="tpu_custom_call" | custom-call | tf_op jit(solution)/shard_map/mlp_both_ways/pallas_call | solution.py:967
  253.8 192.6 %attention_backward.1 = (bf16[8,16,1408]{2,1,0:T(8,128)(2,1)}, bf16[8,16,1408]{2,1,0:T(8,128)(2,1)}, bf16[8,16,1408]{2,1,0:T(8,128)(2,1)}, f32[16,1408]{1,0:T(8,...) custom-call(bf16[8,16,1408]{2,1,0:T(8,128)(2,1)} %get-tuple-element., ...), custom_call_target="tpu_custom_call" | custom-call | tf_op jit(solution)/shard_map/attention_backward/pallas_call | solution.py:840
  446.4 6.2 %results.1 = (bf16[8,16,1408]{2,1,0:T(8,128)(2,1)}, bf16[8,16,1408]{2,1,0:T(8,128)(2,1)}, bf16[8,16,1408]{2,1,0:T(8,128)(2,1)}, bf16[1408,384]{1,0:T(8,128)(2,1)...) custom-call(bf16[8,16,1408]{2,1,0:T(8,128)(2,1)} %get-tuple-element., ...), custom_call_target="tpu_custom_call" | custom-call | tf_op jit(solution)/shard_map/results/pallas_call | solution.py:1005
